TPU v7x, 8 devices: a whole 2x2x1 slice. The times are simulated.
8 devices in a mesh: rep: 1 (over z), r: 2 (over y), s: 4 (over x, core).
Axes of the slice: x: 2, y: 2, z: 1, core: 2. Of those that a mesh axis runs over, the one named last changes fastest.
Arguments:
- x: bfloat16 [8, 4096, 512], P(('rep', 'r', 's'))
- dy: bfloat16 [8, 4096, 512], P(('rep', 'r', 's'))
- w_gate: bfloat16 [2, 512, 8192], P(None, 's')
- w_up: bfloat16 [2, 512, 8192], P(None, 's')
- w_down: bfloat16 [2, 8192, 512], P(None, 's')
- m_w_gate: float32 [2, 512, 8192], P(None, 's')
- m_w_up: float32 [2, 512, 8192], P(None, 's')
- m_w_down: float32 [2, 8192, 512], P(None, 's')
- v_w_gate: float32 [2, 512, 8192], P(None, 's')
- v_w_up: float32 [2, 512, 8192], P(None, 's')
- v_w_down: float32 [2, 8192, 512], P(None, 's')
Outputs:
- output 1: bfloat16 [2, 512, 8192], P('rep', 's')
- output 2: bfloat16 [2, 512, 8192], P('rep', 's')
- output 3: bfloat16 [2, 8192, 512], P('rep', 's')
- output 4: float32 [2, 512, 8192], P('rep', 's')
- output 5: float32 [2, 512, 8192], P('rep', 's')
- output 6: float32 [2, 8192, 512], P('rep', 's')
- output 7: float32 [2, 512, 8192], P('rep', 's')
- output 8: float32 [2, 512, 8192], P('rep', 's')
- output 9: float32 [2, 8192, 512], P('rep', 's')
All inputs are finite; a program needn't handle non-finite values.
Results may differ from a plain program's by a relative error of at most 0.0229.
Values are sent between devices in bfloat16 or wider.
A program may use at most 2 GiB of HBM per device.

v0:
```python
import jax
import jax.numpy as jnp
from jax import lax
from jax.sharding import PartitionSpec as P

NAMES = ("w_gate", "w_up", "w_down")


def matmul(a, w):
    return jnp.dot(a, w, preferred_element_type=jnp.float32).astype(jnp.bfloat16)


def normed(h):
    wide = h.astype(jnp.float32)
    scale = lax.rsqrt(jnp.mean(wide**2, -1, keepdims=True) + 1e-6)
    return (wide * scale).astype(jnp.bfloat16)


def layer(h, w):
    a = normed(h)
    gate = jnp.dot(a, w["w_gate"], preferred_element_type=jnp.float32)
    up = jnp.dot(a, w["w_up"], preferred_element_type=jnp.float32)
    return h + matmul((jax.nn.silu(gate) * up).astype(jnp.bfloat16), w["w_down"])


def adamw(w, m, v, g):
    m = 0.9 * m + 0.1 * g
    v = 0.95 * v + 0.05 * g * g
    step = m * lax.rsqrt(v + 1e-8) + 0.1 * w
    return (w - 0.02 * step).astype(jnp.bfloat16), m, v


def solution(mesh):
    def fetched(weights, number):
        return {name: lax.all_gather(w[number], "s", axis=0, tiled=True) for name, w in zip(NAMES, weights, strict=True)}

    def summed(term):
        return lax.psum(lax.psum_scatter(term, "s", scatter_dimension=0, tiled=True), "r")

    def step(x, dy, *arrays):
        weights, m, v = (arrays[i : i + 3] for i in (0, 3, 6))
        layers = weights[0].shape[0]
        h, kept = x[0], []
        for number in range(layers):
            kept.append(h)
            h = layer(h, fetched(weights, number))
        by_h, mine = dy[0], [None] * layers
        for number in reversed(range(layers)):
            _, back = jax.vjp(lambda w, h: layer(h, w), fetched(weights, number), kept[number])
            by_w, by_h = back(by_h)
            mine[number] = [summed(by_w[name]) for name in NAMES]
        gradients = [jnp.stack([mine[number][i] for number in range(layers)]).astype(jnp.float32) for i in range(3)]
        new = [adamw(w.astype(jnp.float32), m, v, g) for w, m, v, g in zip(weights, m, v, gradients, strict=True)]
        return tuple(one[which] for which in range(3) for one in new)

    states, cut = P(("rep", "r", "s"), None, None), P(None, "s", None)
    return jax.shard_map(
        step,
        mesh=mesh,
        in_specs=(states, states) + (cut,) * 9,
        out_specs=(P("rep", "s", None),) * 9,
        check_vma=False,
    )
```

profile of v0, /device:TPU:0, one launch (start us, length us, event | category | flops | bytes accessed | tf_op | source)
XLA Modules:
  0.0 1582.8 jit_solution(18124826545886547866)
XLA Ops:
  7.2 0.0 all-gather.13.cloned.1.call-start
  7.2 4.7 fusion.99
  11.9 0.0 all-gather.13.cloned.1.call-update
  11.9 0.0 all-gather.15.cloned.1.call-start
  12.0 4.7 fusion.98
  16.6 0.0 all-gather.15.cloned.1.call-update
  16.7 0.0 all-gather.17.cloned.1.call-start
  16.7 5.1 fusion.97
  21.8 0.0 all-gather.17.cloned.1.call-update
  21.8 0.0 all-gather.21.cloned.1.call-start
  21.8 0.5 all-gather.21.cloned.1.call-update
  22.4 0.0 all-gather.23.cloned.1.call-start
  22.4 0.5 all-gather.23.cloned.1.call-update
  23.0 0.0 all-gather.19.cloned.1.call-start
  23.0 0.5 all-gather.19.cloned.1.call-update
  23.5 0.0 reduce-scatter.15.cloned.1.call-start
  23.6 6.4 copy.20
  30.0 3.2 fusion.25
  33.1 6.3 copy.21
  39.5 30.9 %all-gather.13.cloned.1.call-done = bf16[1,512,8192]{2,1,0:T(8,128)(2,1)} async-done(((bf16[1,128,8192]{2,1,0:T(8,128)(2,1)}), bf16[1,512,8192]{2,1,0:T(8,128)(2,1)}) %all-gather.13.cloned.1.call-update) | async-done | bytes 8388624 | tf_op jit(solution)/shard_map/all_gather | solution.py:35
  70.4 54.7 %fusion.57 = f32[4096,8192]{1,0:T(8,128)} fusion(bf16[1,512,8192]{2,1,0:T(8,128)(2,1)} %all-gather.13.cloned.1.call-done, bf16[1,4096,512]{1,2,0:T(8,128)(2,1)} %copy.20, f32[4096]{0:T(1024)S(1)} %add_rsqrt_fusion), kind=kOutput, calls=%fused_computation.86 | convolution fusion | flops 34366029824 | bytes 146817024 | tf_op jit(solution)/shard_map/dot_general | solution.py:21
  125.0 3.0 all-gather.15.cloned.1.call-done
  128.0 117.3 %multiply_convert_fusion.1 = (bf16[4096,8192]{1,0:T(8,128)(2,1)}, f32[4096,8192]{1,0:T(8,128)}) fusion(f32[4096,8192]{1,0:T(8,128)} %fusion.57, bf16[1,512,8192]{2,1,0:T(8,128)(2,1)} %all-gather.15.cloned.1.call-done, bf16[1,4096,512]{1,2,0:T(8,128)(2,1)} %copy.20, f32[4096]{0:T(1024)S(1)} %add_rsqrt_fusion), kind=kOutput, calls=%fused_computation.17 | convolution fusion | flops 34567356416 | bytes 348143616 | tf_op jit(solution)/shard_map/dot_general | solution.py:22
  245.3 45.0 %fusion.41 = (f32[4096]{0:T(1024)S(1)}, bf16[4096,512]{0,1:T(8,128)(2,1)}) fusion(bf16[4096,8192]{1,0:T(8,128)(2,1)} %get-tuple-element.30, bf16[1,8192,512]{2,1,0:T(8,128)(2,1)} %all-gather.17.cloned.1.call-done, bf16[1,4096,512]{1,2,0:T(8,128)(2,1)} %copy.20), kind=kOutput, calls=%fused_computation.70 | convolution fusion | flops 34370220032 | bytes 83902464 | tf_op jit(solution)/shard_map/dot_general | solution.py:10
  290.3 47.2 %convolution_convert_fusion.1 = bf16[4096,8192]{1,0:T(8,128)(2,1)} fusion(bf16[1,8192,512]{2,1,0:T(8,128)(2,1)} %all-gather.21.cloned.1.call-done, bf16[1,4096,512]{2,1,0:T(8,128)(2,1)} %param.12), kind=kOutput, calls=%fused_computation.25 | convolution fusion | flops 34393292800 | bytes 79691776 | tf_op jit(solution)/shard_map/transpose(jvp())/dot_general | solution.py:10
  337.5 0.0 all-gather.23.cloned.1.call-done
  337.5 54.1 %fusion.44 = f32[4096,8192]{1,0:T(8,128)} fusion(bf16[1,512,8192]{2,1,0:T(8,128)(2,1)} %all-gather.23.cloned.1.call-done, bf16[4096,512]{0,1:T(8,128)(2,1)} %get-tuple-element.33, f32[4096]{0:T(1024)S(1)} %fusion.85), kind=kOutput, calls=%fused_computation.73 | convolution fusion | flops 34366029824 | bytes 146817024 | tf_op jit(solution)/shard_map/jvp()/dot_general | solution.py:22
  391.6 154.2 %fusion.2 = (bf16[4096,8192]{1,0:T(8,128)(2,1)}, f32[4096,8192]{1,0:T(8,128)}) fusion(f32[4096,8192]{1,0:T(8,128)} %fusion.44, bf16[4096,8192]{1,0:T(8,128)(2,1)} %convolution_convert_fusion.1, bf16[1,512,8192]{2,1,0:T(8,128)(2,1)} %all-gather.19.cloned.1.call-done, bf16[4096,512]{0,1:T(8,128)(2,1)} %get-tuple-element.33, f32[4096]{0:T(1024)S(1)} %fusion.85), kind=kOutput, calls=%fused_computation.8 | convolution fusion | flops 34768683008 | bytes 415252480 | tf_op jit(solution)/shard_map/jvp()/dot_general | solution.py:21
  545.9 70.0 %fusion.65 = bf16[4096,512]{0,1:T(8,128)(2,1)} fusion(bf16[1,512,8192]{2,1,0:T(8,128)(2,1)} %all-gather.23.cloned.1.call-done, bf16[4096,8192]{1,0:T(8,128)(2,1)} %convolution_convert_fusion.1, f32[4096,8192]{1,0:T(8,128)} %get-tuple-element.35), kind=kOutput, calls=%fused_computation.90 | convolution fusion | flops 34563162112 | bytes 213909504 | tf_op jit(solution)/shard_map/transpose(jvp())/dot_general | solution.py:22
  615.9 46.0 %fusion.43 = (f32[4096]{0:T(1024)S(1)}, bf16[4096,512]{0,1:T(8,128)(2,1)}) fusion(bf16[4096,512]{0,1:T(8,128)(2,1)} %get-tuple-element.33, bf16[4096,512]{0,1:T(8,128)(2,1)} %fusion.65, bf16[4096,8192]{1,0:T(8,128)(2,1)} %get-tuple-element.34, bf16[1,512,8192]{2,1,0:T(8,128)(2,1)} %all-gather.19.cloned.1.call-done), kind=kOutput, calls=%fused_computation.72 | convolution fusion | flops 34370220032 | bytes 88096768 | tf_op jit(solution)/shard_map/transpose(jvp())/dot_general | solution.py:21
  661.9 6.0 fusion.74
  668.0 2.0 copy-done.2
  670.0 43.4 %convolution_convert_fusion.3 = bf16[8192,512]{1,0:T(8,128)(2,1)} fusion(bf16[4096,8192]{1,0:T(8,128)(2,1)} %get-tuple-element.30, bf16[4096,512]{0,1:T(8,128)(2,1)S(1)} %fusion.74), kind=kOutput, calls=%fused_computation.38 | convolution fusion | flops 34363932672 | bytes 79691776 | tf_op jit(solution)/shard_map/transpose(jvp())/dot_general | solution.py:10
  713.4 0.0 reduce-scatter.15.cloned.1.call-update
  713.4 0.0 reduce-scatter.17.cloned.1.call-start
  713.5 92.1 %fusion.21 = bf16[8192,512]{1,0:T(8,128)(2,1)} fusion(f32[4096,8192]{1,0:T(8,128)} %fusion.44, bf16[1,4096,512]{2,1,0:T(8,128)(2,1)} %param.12, f32[4096,8192]{1,0:T(8,128)} %get-tuple-element.35), kind=kOutput, calls=%fused_computation.37 | convolution fusion | flops 34565259264 | bytes 281018368 | tf_op jit(solution)/shard_map/transpose(jvp())/dot_general | solution.py:10
  805.6 0.0 reduce-scatter.11.cloned.1.call-start
  805.7 47.4 %convolution_convert_fusion = bf16[4096,8192]{1,0:T(8,128)(2,1)} fusion(bf16[4096,512]{0,1:T(8,128)(2,1)} %copy-done.2, bf16[1,8192,512]{2,1,0:T(8,128)(2,1)} %all-gather.17.cloned.1.call-done), kind=kOutput, calls=%fused_computation.24 | convolution fusion | flops 34393292800 | bytes 79691776 | tf_op jit(solution)/shard_map/transpose(jvp())/dot_general | solution.py:10
  853.1 68.6 %fusion.20 = bf16[512,8192]{1,0:T(8,128)(2,1)} fusion(bf16[4096,8192]{1,0:T(8,128)(2,1)} %convolution_convert_fusion, f32[4096,8192]{1,0:T(8,128)} %fusion.57, bf16[1,4096,512]{1,2,0:T(8,128)(2,1)} %copy.20, f32[4096]{0:T(1024)S(1)} %copy-done.8), kind=kOutput, calls=%fused_computation.35 | convolution fusion | flops 34571550720 | bytes 213925888 | tf_op jit(solution)/shard_map/transpose(jvp())/dot_general | solution.py:22
  921.7 0.0 reduce-scatter.11.cloned.1.call-update
  921.7 0.0 reduce-scatter.13.cloned.1.call-start
  921.8 0.6 copy-done.5
  922.4 74.3 %fusion.16 = bf16[512,8192]{1,0:T(8,128)(2,1)} fusion(bf16[4096,8192]{1,0:T(8,128)(2,1)} %convolution_convert_fusion.1, bf16[4096,512]{0,1:T(8,128)(2,1)} %get-tuple-element.33, f32[4096]{0:T(1024)S(1)} %copy-done.5, f32[4096,8192]{1,0:T(8,128)} %get-tuple-element.35), kind=kOutput, calls=%fused_computation.33 | convolution fusion | flops 34571550720 | bytes 213925888 | tf_op jit(solution)/shard_map/transpose(jvp())/dot_general | solution.py:22
  996.7 0.0 reduce-scatter.13.cloned.1.call-update
  996.8 0.0 reduce-scatter.7.cloned.1.call-start
  996.8 0.6 copy-done.9
  997.5 114.1 %fusion.17 = bf16[512,8192]{1,0:T(8,128)(2,1)} fusion(f32[4096,8192]{1,0:T(8,128)} %fusion.57, f32[4096,8192]{1,0:T(8,128)} %get-tuple-element.31, bf16[4096,8192]{1,0:T(8,128)(2,1)} %convolution_convert_fusion, bf16[1,4096,512]{1,2,0:T(8,128)(2,1)} %copy.20, f32[4096]{0:T(1024)S(1)} %copy-done.9), kind=kOutput, calls=%fused_computation.34 | convolution fusion | flops 34739322880 | bytes 348143616 | tf_op jit(solution)/shard_map/transpose(jvp())/dot_general | solution.py:21
  1111.5 0.0 reduce-scatter.7.cloned.1.call-update
  1111.6 0.0 reduce-scatter.9.cloned.1.call-start
  1111.6 0.6 copy-done.6
  1112.2 47.5 %convolution_convert_fusion.2 = bf16[512,8192]{1,0:T(8,128)(2,1)} fusion(bf16[4096,8192]{1,0:T(8,128)(2,1)} %get-tuple-element.34, bf16[4096,512]{0,1:T(8,128)(2,1)} %get-tuple-element.33, f32[4096]{0:T(1024)S(1)} %copy-done.6), kind=kOutput, calls=%fused_computation.36 | convolution fusion | flops 34366029824 | bytes 79708160 | tf_op jit(solution)/shard_map/transpose(jvp())/dot_general | solution.py:21
  1159.8 0.0 reduce-scatter.9.cloned.1.call-update
  1159.8 0.0 all-reduce.3.cloned.1.call-start
  1159.8 0.0 reduce-scatter.15.cloned.1.call-done
  1159.9 0.0 reduce-scatter.17.cloned.1.call-done
  1159.9 0.0 reduce-scatter.11.cloned.1.call-done
  1159.9 0.0 reduce-scatter.13.cloned.1.call-done
  1160.0 17.8 %reduce-scatter.7.cloned.1.call-done = bf16[128,8192]{1,0:T(8,128)(2,1)} async-done(((bf16[512,8192]{1,0:T(8,128)(2,1)}), bf16[128,8192]{1,0:T(8,128)(2,1)}) %reduce-scatter.7.cloned.1.call-update) | async-done | bytes 2097168 | tf_op jit(solution)/shard_map/reduce_scatter | solution.py:38
  1177.7 68.9 %reduce-scatter.9.cloned.1.call-done = bf16[128,8192]{1,0:T(8,128)(2,1)} async-done(((bf16[512,8192]{1,0:T(8,128)(2,1)}), bf16[128,8192]{1,0:T(8,128)(2,1)}) %reduce-scatter.9.cloned.1.call-update) | async-done | bytes 2097168 | tf_op jit(solution)/shard_map/reduce_scatter | solution.py:38
  1246.6 0.0 all-reduce.3.cloned.1.call-update
  1246.6 285.5 %all-reduce.3.cloned.1.call-done = (bf16[1,128,8192]{2,1,0:T(8,128)(2,1)}, bf16[1,128,8192]{2,1,0:T(8,128)(2,1)}, bf16[1,128,8192]{2,1,0:T(8,128)(2,1)}, bf16[1,...) async-done(((bf16[1,128,8192]{2,1,0:T(8,128)(2,1)}, bf16[1,128,8192]{2,1,0:T(8,128)(2,1)}, bf16[1,128,8192]{2,1,0:T(8,128)(2,1)}, ...) | async-done | bytes 12582928 | tf_op jit(solution)/shard_map/psum | solution.py:38
  1532.1 16.7 %fusion.36 = (bf16[2,2048,512]{2,1,0:T(8,128)(2,1)}, f32[2,2048,512]{2,1,0:T(8,128)}, f32[2,2048,512]{2,1,0:T(8,128)}) fusion(bf16[2,2048,512]{2,1,0:T(8,128)(2,1)} %param.15, bf16[1,2048,512]{2,1,0:T(8,128)(2,1)} %get-tuple-element.13, bf16[1,2048,512]{2,1,0:T(8,128)(2,1)} %get-tuple-element.14, f32[2,2048,512]{2,1,0:T(8,128)} %param.21, ...), kind=kLoop, calls=%fused_computation.65 | loop fusion | flops 39845888 | bytes 46137344 | tf_op jit(solution)/shard_map/convert_element_type | solution.py:30
  1548.7 0.0 copy-done.1
  1548.8 27.1 %fusion.24 = (bf16[2,128,8192]{2,1,0:T(8,128)(2,1)}, f32[2,128,8192]{2,1,0:T(8,128)}, f32[2,128,8192]{2,1,0:T(8,128)}, bf16[2,128,8192]{2,1,0:T(8,128)(2,1)}, f3...) fusion(bf16[2,128,8192]{2,1,0:T(8,128)(2,1)S(1)} %copy-done, bf16[1,128,8192]{2,1,0:T(8,128)(2,1)} %get-tuple-element.9, ...), kind=kLoop, calls=%fused_computation.53 | loop fusion | flops 79691776 | bytes 92274688 | tf_op jit(solution)/shard_map/convert_element_type | solution.py:30
  (26 shorter events, 0.1 us)
Async XLA Ops:
  7.2 63.2 %all-gather.13.cloned.1.call-start = ((), (), s32[]{:S(2)}) async-start(), calls=%async_computation.12 | async-start | bytes 10485760 | tf_op jit(solution)/shard_map/all_gather | solution.py:35
  11.9 116.0 %all-gather.15.cloned.1.call-start = ((), (), s32[]{:S(2)}) async-start(), calls=%async_computation.13 | async-start | bytes 10485760 | tf_op jit(solution)/shard_map/all_gather | solution.py:35
  16.7 228.6 %all-gather.17.cloned.1.call-start = ((), (), s32[]{:S(2)}) async-start(), calls=%async_computation.14 | async-start | bytes 10485760 | tf_op jit(solution)/shard_map/all_gather | solution.py:35
  21.8 268.5 %all-gather.21.cloned.1.call-start = ((), (), s32[]{:S(2)}) async-start(), calls=%async_computation.16 | async-start | bytes 10485760 | tf_op jit(solution)/shard_map/all_gather | solution.py:35
  22.4 315.2 %all-gather.23.cloned.1.call-start = ((), (), s32[]{:S(2)}) async-start(), calls=%async_computation.17 | async-start | bytes 10485760 | tf_op jit(solution)/shard_map/all_gather | solution.py:35
  23.0 368.7 %all-gather.19.cloned.1.call-start = ((), (), s32[]{:S(2)}) async-start(), calls=%async_computation.15 | async-start | bytes 10485760 | tf_op jit(solution)/shard_map/all_gather | solution.py:35
  23.5 1136.3 %reduce-scatter.15.cloned.1.call-start = ((), (), s32[]{:S(2)}) async-start(), calls=%async_computation.10 | async-start | bytes 10485760 | tf_op jit(solution)/shard_map/reduce_scatter | solution.py:38
  33.1 94.8 %copy-start.7 = (f32[4096]{0:T(1024)}, f32[4096]{0:T(1024)S(1)}, u32[]{:S(2)}) copy-start(f32[4096]{0:T(1024)S(1)} %add_rsqrt_fusion) | copy-start | bytes 49156
  290.3 47.2 %copy-start.10 = (f32[4096]{0:T(1024)}, f32[4096]{0:T(1024)S(1)}, u32[]{:S(2)}) copy-start(f32[4096]{0:T(1024)S(1)} %get-tuple-element.32) | copy-start | bytes 49156
  337.5 54.2 %copy-start.3 = (f32[4096]{0:T(1024)}, f32[4096]{0:T(1024)S(1)}, u32[]{:S(2)}) copy-start(f32[4096]{0:T(1024)S(1)} %fusion.85) | copy-start | bytes 49156
  615.9 46.0 %copy-start.11 = (f32[4096]{0:T(1024)S(1)}, f32[4096]{0:T(1024)}, u32[]{:S(2)}) copy-start(f32[4096]{0:T(1024)} %copy-done.10) | copy-start | bytes 49156
  615.9 46.0 %copy-start.4 = (f32[4096]{0:T(1024)S(1)}, f32[4096]{0:T(1024)}, u32[]{:S(2)}) copy-start(f32[4096]{0:T(1024)} %copy-done.3) | copy-start | bytes 49156
  668.0 2.0 copy-start.2
  713.4 446.5 %reduce-scatter.17.cloned.1.call-start = ((), (), s32[]{:S(2)}) async-start(), calls=%async_computation.11 | async-start | bytes 10485760 | tf_op jit(solution)/shard_map/reduce_scatter | solution.py:38
  805.6 47.5 %copy-start.8 = (f32[4096]{0:T(1024)S(1)}, f32[4096]{0:T(1024)}, u32[]{:S(2)}) copy-start(f32[4096]{0:T(1024)} %copy-done.7) | copy-start | bytes 49156
  805.6 354.3 %reduce-scatter.11.cloned.1.call-start = ((), (), s32[]{:S(2)}) async-start(), calls=%async_computation.8 | async-start | bytes 10485760 | tf_op jit(solution)/shard_map/reduce_scatter | solution.py:38
  921.7 0.7 copy-start.5
  921.7 238.2 %reduce-scatter.13.cloned.1.call-start = ((), (), s32[]{:S(2)}) async-start(), calls=%async_computation.9 | async-start | bytes 10485760 | tf_op jit(solution)/shard_map/reduce_scatter | solution.py:38
  996.7 0.7 copy-start.9
  996.8 180.9 %reduce-scatter.7.cloned.1.call-start = ((), (), s32[]{:S(2)}) async-start(), calls=%async_computation.6 | async-start | bytes 10485760 | tf_op jit(solution)/shard_map/reduce_scatter | solution.py:38
  1111.5 0.7 copy-start.6
  1111.6 135.0 %reduce-scatter.9.cloned.1.call-start = ((), (), s32[]{:S(2)}) async-start(), calls=%async_computation.7 | async-start | bytes 10485760 | tf_op jit(solution)/shard_map/reduce_scatter | solution.py:38
  1159.8 372.3 %all-reduce.3.cloned.1.call-start = ((), (), s32[]{:S(2)}) async-start(), calls=%async_computation.18 | async-start | bytes 25165824 | tf_op jit(solution)/shard_map/psum | solution.py:38
  1532.1 16.7 %copy-start = (bf16[2,128,8192]{2,1,0:T(8,128)(2,1)S(1)}, bf16[2,128,8192]{2,1,0:T(8,128)(2,1)}, u32[]{:S(2)}) copy-start(bf16[2,128,8192]{2,1,0:T(8,128)(2,1)} %param.13) | copy-start | bytes 12582916
  1532.1 16.7 %copy-start.1 = (bf16[2,128,8192]{2,1,0:T(8,128)(2,1)S(1)}, bf16[2,128,8192]{2,1,0:T(8,128)(2,1)}, u32[]{:S(2)}) copy-start(bf16[2,128,8192]{2,1,0:T(8,128)(2,1)} %param.14) | copy-start | bytes 12582916
Sparse Core Ops, SparseCore 0:
  12.0 58.2 all-gather.12
  72.4 55.4 all-gather.14
  130.1 55.4 all-gather.16
  187.5 55.4 all-gather.20
  245.0 55.4 all-gather.22
  302.5 55.4 all-gather.18
  713.6 65.9 reduce-scatter.14
  805.7 65.9 reduce-scatter.16
  921.8 65.8 reduce-scatter.10
  996.9 66.0 reduce-scatter.12
  1111.7 65.9 reduce-scatter.6
  1180.7 65.8 reduce-scatter.8
  1249.4 282.5 all-reduce.2
where the time goes:
time: 1590 us; the launch traced here: 1580 us
  matrix products  1080 us (68%)
  waiting for transfers between devices  408 us (26%)
  other arithmetic  53 us (3%)
  local copies, waits for them, and re-layouts  31.1 us (2%)
    dot_general x5, matrix products, layer(): gate = jnp.dot(a, w['w_gate'], preferred_element_type=jnp.float32)  417 us
    dot_general x5, matrix products, layer(): up = jnp.dot(a, w['w_up'], preferred_element_type=jnp.float32)  384 us
    psum x1, waiting for transfers between devices, summed(): lax.psum(lax.psum_scatter(term, 's', scatter_dimension=0, tiled=True), 'r')  285 us
    dot_general x5, matrix products, matmul(): jnp.dot(a, w, preferred_element_type=jnp.float32).astype(jnp.bfloat16)  275 us
    reduce_scatter x6, waiting for transfers between devices, summed(): lax.psum_scatter(term, 's', scatter_dimension=0, tiled=True)  86.7 us
    convert_element_type x2, other arithmetic, adamw(): return ((w - 0.02 * step).astype(jnp.bfloat16), m, v)  43.8 us
    all_gather x6, waiting for transfers between devices, fetched(): lax.all_gather(w[number], 's', axis=0, tiled=True)  33.9 us
  transfers between devices with their start and end apart: 13, of which 5 were waited for; matrix products, arithmetic and copies ran while one was open for 50% of the time, Pallas kernels for 0%

commit v1 on v0

v1 whole, which is shorter than its diff:
```python
import functools
import jax, jax.numpy as jnp
from jax import lax
from jax.experimental import pallas as pl
from jax.experimental.pallas import tpu as pltpu
from jax.sharding import PartitionSpec as P

F32, BF16 = jnp.float32, jnp.bfloat16
TOK, D, W = 4096, 512, 512
T = 512
ANY = pl.BlockSpec(memory_space=pl.ANY)


def dot(a, b):
    return jnp.dot(a, b, preferred_element_type=F32)


def fwd_kernel(n, first, last, *refs):
    if first:
        a_h, p, out_h, a_v, y_v, sa, so = refs
    elif last:
        a_h, y_h, _, p, out_h, a_v, y_v, _, _, sa, sy, _, so = refs
    else:
        a_h, y_h, p, out_h, a_v, y_v, sa, sy, so = refs
    k = pl.program_id(0)

    def tile(ref, t):
        return ref.at[pl.ds(pl.multiple_of(t * T, T), T), :]

    def load(src, dst, sem, t):
        return pltpu.make_async_copy(tile(src, t), tile(dst, t), sem.at[t])

    @pl.when(k == 0)
    def _():
        for t in range(TOK // T):
            load(a_h, a_v, sa, t).start()
            if not first:
                load(y_h, y_v, sy, t).start()

    wg = p[:, 0, 0].reshape(D, W)
    wu = p[:, 0, 1].reshape(D, W)
    wd = p[:, 0, 2].reshape(W, D)

    @pl.loop(0, TOK // T)
    def _(t):
        @pl.when(k == 0)
        def _():
            load(a_h, a_v, sa, t).wait()
            if not first:
                load(y_h, y_v, sy, t).wait()
            else:
                tile(y_v, t)[...] = jnp.zeros((T, D), F32)

        a = tile(a_v, t)[...]
        gate = dot(a, wg)
        up = dot(a, wu)
        act = (gate * jax.nn.sigmoid(gate) * up).astype(BF16)
        tile(y_v, t)[...] += dot(act, wd)

        @pl.when(k == n - 1)
        def _():
            pltpu.make_async_copy(tile(y_v, t), tile(out_h, t), so.at[t]).start()

    @pl.when(k == n - 1)
    def _():
        for t in range(TOK // T):
            pltpu.make_async_copy(tile(y_v, t), tile(out_h, t), so.at[t]).wait()


def fwd(a, p, y=None):
    n = p.shape[1]
    first = y is None
    nt = TOK // T
    return pl.pallas_call(
        functools.partial(fwd_kernel, n, first, False),
        grid=(n,),
        out_shape=jax.ShapeDtypeStruct((TOK, D), F32),
        in_specs=[ANY] * (1 if first else 2) + [pl.BlockSpec((4, 1, 3, 128, 512), lambda k: (0, k, 0, 0, 0))],
        out_specs=ANY,
        scratch_shapes=[pltpu.VMEM((TOK, D), BF16), pltpu.VMEM((TOK, D), F32)] + [pltpu.SemaphoreType.DMA((nt,))] * (2 if first else 3),
        compiler_params=pltpu.CompilerParams(vmem_limit_bytes=60 << 20, dimension_semantics=("arbitrary",)),
        cost_estimate=pl.CostEstimate(flops=6 * TOK * D * W * n, bytes_accessed=n * 3 * (1 << 19) + (20 << 20), transcendentals=TOK * W * n),
        name="fwd",
    )(*((a,) if first else (a, y)), p)


def bwd_kernel(n, need, first, skip, *refs):
    refs = list(refs)[skip:]
    a_h, dy_h = refs[:2]; refs = refs[2:]
    if need and not first:
        da_h = refs.pop(0)
    p = refs.pop(0)
    g = refs.pop(0)
    if need:
        out_h = refs.pop(0)
    a_v, dy_v, aT, dyT, act_v, dg_v, du_v, wgT, wuT, wdT = refs[:10]; refs = refs[10:]
    if need:
        da_v = refs.pop(0)
    sa, sd = refs[:2]; refs = refs[2:]
    if need:
        sp, so = refs
    k = pl.program_id(0)
    nt = TOK // T

    def tile(ref, t):
        return ref.at[pl.ds(pl.multiple_of(t * T, T), T), :]

    def col(ref, t):
        return ref.at[:, pl.ds(pl.multiple_of(t * T, T), T)]

    def load(src, dst, sem, t):
        return pltpu.make_async_copy(tile(src, t), tile(dst, t), sem.at[t])

    @pl.when(k == 0)
    def _():
        for t in range(nt):
            load(a_h, a_v, sa, t).start()
            load(dy_h, dy_v, sd, t).start()
            if need and not first:
                load(da_h, da_v, sp, t).start()

    wg = p[:, 0, 0].reshape(D, W)
    wu = p[:, 0, 1].reshape(D, W)
    wd = p[:, 0, 2].reshape(W, D)
    wdT[...] = wd.T
    if need:
        wgT[...] = wg.T
        wuT[...] = wu.T

    @pl.loop(0, nt)
    def _(t):
        @pl.when(k == 0)
        def _():
            load(a_h, a_v, sa, t).wait()
            load(dy_h, dy_v, sd, t).wait()
            col(aT, t)[...] = tile(a_v, t)[...].T
            col(dyT, t)[...] = tile(dy_v, t)[...].T
            if need:
                if first:
                    tile(da_v, t)[...] = jnp.zeros((T, D), F32)
                else:
                    load(da_h, da_v, sp, t).wait()

        a = tile(a_v, t)[...]
        dy = tile(dy_v, t)[...]
        gate = dot(a, p[:, 0, 0].reshape(D, W))
        up = dot(a, p[:, 0, 1].reshape(D, W))
        dact = dot(dy, wdT[...]).astype(BF16).astype(F32)
        sig = jax.nn.sigmoid(gate)
        silu = gate * sig
        tile(act_v, t)[...] = (silu * up).astype(BF16)
        du = (dact * silu).astype(BF16)
        dg = (dact * up * (sig + silu * (1 - sig))).astype(BF16)
        tile(du_v, t)[...] = du
        tile(dg_v, t)[...] = dg
        if need:
            tile(da_v, t)[...] += dot(dg, wgT[...]) + dot(du, wuT[...])

            @pl.when(k == n - 1)
            def _():
                pltpu.make_async_copy(tile(da_v, t), tile(out_h, t), so.at[t]).start()

    g[:, 0, 0] = dot(aT[...], dg_v[...]).astype(BF16).reshape(4, 128, W)
    g[:, 0, 1] = dot(aT[...], du_v[...]).astype(BF16).reshape(4, 128, W)
    g[:, 0, 2] = dot(dyT[...], act_v[...]).astype(BF16).T.reshape(4, 128, D)

    if need:
        @pl.when(k == n - 1)
        def _():
            for t in range(nt):
                pltpu.make_async_copy(tile(da_v, t), tile(out_h, t), so.at[t]).wait()


def bwd(a, dy, p, da=None, need=True, deps=()):
    n = p.shape[1]
    first = da is None
    nt = TOK // T
    blk = pl.BlockSpec((4, 1, 3, 128, 512), lambda k: (0, k, 0, 0, 0))
    sem = pltpu.SemaphoreType.DMA((nt,))
    out = [jax.ShapeDtypeStruct((4, n, 3, 128, 512), BF16)] + ([jax.ShapeDtypeStruct((TOK, D), F32)] if need else [])
    args = tuple(deps) + (a, dy) + ((da,) if need and not first else ()) + (p,)
    big = lambda dt: pltpu.VMEM((TOK, D), dt)
    return pl.pallas_call(
        functools.partial(bwd_kernel, n, need, first, len(deps)),
        grid=(n,),
        out_shape=out,
        in_specs=[ANY] * (len(args) - 1) + [blk],
        out_specs=[blk] + ([ANY] if need else []),
        scratch_shapes=[big(BF16)] * 2 + [pltpu.VMEM((D, TOK), BF16)] * 2 + [big(BF16)] * 3 + [pltpu.VMEM((D, W), BF16)] * 3
        + ([big(F32)] if need else []) + [sem] * (4 if need else 2),
        compiler_params=pltpu.CompilerParams(vmem_limit_bytes=62 << 20, dimension_semantics=("arbitrary",)),
        cost_estimate=pl.CostEstimate(flops=2 * (8 if need else 6) * TOK * D * W * n, bytes_accessed=n * 6 * (1 << 19) + (20 << 20), transcendentals=TOK * W * n),
        name="bwd",
    )(*args)


CHUNKS = 4


def normed(h):
    wide = h.astype(F32)
    scale = lax.rsqrt(jnp.mean(wide**2, -1, keepdims=True) + 1e-6)
    return (wide * scale).astype(BF16)


def pack_kernel(*refs):
    gates, ups, down, out = refs[:4], refs[4:8], refs[8], refs[9]
    for k in range(4):
        for which, parts in ((0, gates), (1, ups)):
            for s in range(4):
                out[k, which, :, 128 * s : 128 * (s + 1)] = parts[s][0, :, 128 * k : 128 * (k + 1)]
        out[k, 2] = down[0, 128 * k : 128 * (k + 1), :]


def pack(l, j, w_gate, w_up, w_down):
    wide = [pl.BlockSpec((1, 128, 512), functools.partial(lambda s, i: (l, 0, 4 * s + j), s)) for s in range(4)]
    return pl.pallas_call(
        pack_kernel,
        grid=(1,),
        out_shape=jax.ShapeDtypeStruct((4, 3, 128, 512), BF16),
        in_specs=wide + wide + [pl.BlockSpec((1, 512, 512), lambda i: (l, j, 0))],
        out_specs=pl.BlockSpec((4, 3, 128, 512), lambda i: (0, 0, 0, 0)),
        cost_estimate=pl.CostEstimate(flops=1 << 21, bytes_accessed=3 << 20, transcendentals=0),
        name="pack",
    )(*[w_gate] * 4, *[w_up] * 4, w_down)


def adamw(w, m, v, g):
    m = 0.9 * m + 0.1 * g
    v = 0.95 * v + 0.05 * g * g
    step = m * lax.rsqrt(v + 1e-8) + 0.1 * w
    return (w - 0.02 * step).astype(BF16), m, v


def adam_kernel(*refs):
    gs, gr, w, m, v = (refs[3 * i : 3 * i + 3] for i in range(5))
    outs = refs[-10:-1]
    refs[-1][...] = jnp.zeros((8, 128), F32)
    for which in range(3):
        g = (gs[which][...].astype(F32) + gr[which][...].astype(F32)).astype(BF16).astype(F32)
        for k in range(4 if which < 2 else 1):
            c = slice(128 * k, 128 * (k + 1)) if which < 2 else slice(0, 512)
            new = adamw(w[which][0, :, c].astype(F32), m[which][0, :, c], v[which][0, :, c], g[k, 0])
            for i in range(3):
                outs[3 * i + which][0, :, c] = new[i]


def adam(l, j, gs, gr, weights, m, v, before):
    cols = [pl.BlockSpec((4, 1, 128, 128), functools.partial(lambda which, i: (0, which, 0, i), which)) for which in range(2)]
    cols.append(pl.BlockSpec((1, 1, 128, 512), lambda i: (i, 2, 0, 0)))
    own = [pl.BlockSpec((1, 128, 512), lambda i: (l, 0, 4 * i + j))] * 2 + [pl.BlockSpec((1, 128, 512), lambda i: (l, 4 * j + i, 0))]
    shapes = [jax.ShapeDtypeStruct(w.shape, dt) for dt in (BF16, F32, F32) for w in weights]
    shapes.append(jax.ShapeDtypeStruct((8, 128), F32))
    before = list(before or [])
    return pl.pallas_call(
        adam_kernel,
        grid=(4,),
        out_shape=shapes,
        in_specs=cols * 2 + own * 3 + [ANY] * len(before),
        out_specs=own * 3 + [pl.BlockSpec((8, 128), lambda i: (0, 0))],
        input_output_aliases={15 + i: i for i in range(len(before))},
        cost_estimate=pl.CostEstimate(flops=10 * 3 * 4 * 128 * 512, bytes_accessed=18 << 20, transcendentals=3 * 4 * 128 * 512),
        name="adam",
    )(*[gs] * 3, *[gr] * 3, *weights, *m, *v, *before)


def solution(mesh):
    pairs = [(0, 1), (1, 0)]

    def step(x, dy, *arrays):
        weights, m, v = (arrays[i : i + 3] for i in (0, 3, 6))
        x, dy = x[0], dy[0]
        full = [[lax.all_gather(pack(l, j, *weights), "s", axis=0) for j in range(CHUNKS)] for l in range(2)]
        a0 = normed(x)
        y = None
        for j in range(CHUNKS):
            y = fwd(a0, full[0][j], y)
        h1 = x + y.astype(BF16)
        a1, back = jax.vjp(normed, h1)
        order = [(1, j) for j in range(CHUNKS)] + [(0, j) for j in range(CHUNKS)]
        ours, theirs, out, marks, da = [], [], None, [], None

        def settle(i):
            nonlocal out
            *out, mark = adam(*order[i], ours[i], theirs[i], weights, m, v, out)
            marks.append(mark)

        for i, (l, j) in enumerate(order):
            deps = []
            if i >= 3:
                settle(i - 3)
                deps = [ours[i - 2], marks[i - 3]]
            if (l, j) == (0, 0):
                dh = dy + back(da.astype(BF16))[0]
            if i >= 2:
                theirs.append(lax.ppermute(ours[i - 2], "r", pairs))
            if l == 1:
                term, da = bwd(a1, dy, full[1][j], da, deps=deps)
            else:
                term = bwd(a0, dh, full[0][j], need=False, deps=deps)[0]
            ours.append(lax.psum_scatter(term, "s", scatter_dimension=0, tiled=True)[0])
        theirs += [lax.ppermute(one, "r", pairs) for one in ours[-2:]]
        for i in range(len(order) - 3, len(order)):
            settle(i)
        return tuple(out)

    states, cut = P(("rep", "r", "s"), None, None), P(None, "s", None)
    return jax.shard_map(
        step,
        mesh=mesh,
        in_specs=(states, states) + (cut,) * 9,
        out_specs=(P("rep", "s", None),) * 9,
        check_vma=False,
    )
```

time: 1590 us -> 1270 us (0.80)
  matrix products: 1080 us -> 0 us
  Pallas kernels: 0 us -> 899 us
  waiting for transfers between devices: 408 us -> 299 us
  other arithmetic: 53 us -> 24.8 us
    dot_general x15 -> x0, matrix products: 1080 us -> none  [the longest x5 417 us: layer(): gate = jnp.dot(a, w['w_gate'], preferred_element_type=jnp.float32)]
    pallas_call x0 -> x28, Pallas kernels: none -> 899 us  [the longest x8 663 us: bwd(): pl.pallas_call(functools.partial(bwd_kernel, n, need, first, len(deps)),...]
    psum x1 -> x0, waiting for transfers between devices: 285 us -> none  [summed(): lax.psum(lax.psum_scatter(term, 's', scatter_dimension=0, tiled=True), 'r')]
    ppermute x0 -> x8, waiting for transfers between devices: none -> 198 us  [the longest x6 168 us: step(): theirs.append(lax.ppermute(ours[i - 2], 'r', pairs))]
    reduce_scatter x6 -> x0, waiting for transfers between devices: 86.7 us -> none  [summed(): lax.psum_scatter(term, 's', scatter_dimension=0, tiled=True)]
    unnamed x13 -> x24, waiting for transfers between devices: 1.74 us -> 50.8 us
    convert_element_type x2, other arithmetic: 43.8 us -> 5.05 us  [normed(): return (wide * scale).astype(BF16)]
    all_gather x6 -> x8, waiting for transfers between devices: 33.9 us -> 50 us  [step(): lax.all_gather(pack(l, j, *weights), 's', axis=0)]
  transfers between devices with their start and end apart: 13 -> 24, of which waited for: 5 -> 12; matrix products, arithmetic and copies ran while one was open for 50% -> 2% of each run, Pallas kernels for 0% -> 70%
where the time goes in v1:
time: 1270 us
  Pallas kernels  899 us (71%)
  waiting for transfers between devices  299 us (24%)
  other arithmetic  24.8 us (2%)
  local copies, waits for them, and re-layouts  18.7 us (1%)
  between operations  14.8 us (1%)
    pallas_call x8, Pallas kernels, bwd(): pl.pallas_call(functools.partial(bwd_kernel, n, need, first, len(deps)),...  663 us
    ppermute x6, waiting for transfers between devices, step(): theirs.append(lax.ppermute(ours[i - 2], 'r', pairs))  168 us
    pallas_call x4, Pallas kernels, fwd(): pl.pallas_call(functools.partial(fwd_kernel, n, first, False), grid=(n,),...  146 us
    pallas_call x8, Pallas kernels, adam(): pl.pallas_call(adam_kernel, grid=(4,), out_shape=shapes, in_specs=cols *...  66.3 us
    unnamed x24, waiting for transfers between devices  50.8 us
    all_gather x8, waiting for transfers between devices, step(): lax.all_gather(pack(l, j, *weights), 's', axis=0)  50 us
    ppermute x2, waiting for transfers between devices, step(): theirs += [lax.ppermute(one, 'r', pairs) for one in ours[-2:]]  30 us
  transfers between devices with their start and end apart: 24, of which 12 were waited for; matrix products, arithmetic and copies ran while one was open for 2% of the time, Pallas kernels for 70%

profile of v1, /device:TPU:0, one launch (start us, length us, event | category | flops | bytes accessed | tf_op | source)
XLA Modules:
  0.0 1267.1 jit_solution(3684603382629688191)
XLA Ops:
  7.2 2.8 pack.8
  10.1 2.8 pack.9
  13.0 2.8 pack.10
  16.0 3.0 pack.11
  19.1 3.3 pack.12
  22.4 2.8 pack.13
  25.4 2.8 pack.14
  28.3 3.2 fusion
  31.8 2.5 fusion.1.refs_0_.refs_2_
  34.3 22.3 %all-gather.17.cloned.1.call-done = bf16[16,3,128,512]{3,2,1,0:T(8,128)(2,1)} async-done(((bf16[4,3,128,512]{3,2,1,0:T(8,128)(2,1)}), bf16[16,3,128,512]{3,2,1,0:T(8,128)(2,1)}) %all-gather.17.cloned.1.call-update) | async-done | bytes 6291472 | tf_op jit(solution)/shard_map/all_gather | solution.py:273
  56.6 36.5 %fwd.4.refs_1_ = f32[4096,512]{1,0:T(8,128)} custom-call(bf16[4096,512]{1,0:T(8,128)(2,1)} %fusion.1.refs_0_.refs_2_, bf16[4,4,3,128,512]{4,3,2,1,0:T(8,128)(2,1)} %bitcast.71), custom_call_target="tpu_custom_call" | custom-call | flops 25769803776 | bytes 27262976 | tf_op jit(solution)/shard_map/fwd/pallas_call | solution.py:74
  93.2 9.2 all-gather.19.cloned.1.call-done
  102.3 36.4 %fwd.5.refs_1_ = f32[4096,512]{1,0:T(8,128)} custom-call(bf16[4096,512]{1,0:T(8,128)(2,1)} %fusion.1.refs_0_.refs_2_, f32[4096,512]{1,0:T(8,128)} %fwd.4.refs_1_, bf16[4,4,3,128,512]{4,3,2,1,0:T(8,128)(2,1)} %bitcast.69), custom_call_target="tpu_custom_call" | custom-call | flops 25769803776 | bytes 27262976 | tf_op jit(solution)/shard_map/fwd/pallas_call | solution.py:74
  138.7 9.3 all-gather.21.cloned.1.call-done
  148.0 36.4 %fwd.6.refs_1_ = f32[4096,512]{1,0:T(8,128)} custom-call(bf16[4096,512]{1,0:T(8,128)(2,1)} %fusion.1.refs_0_.refs_2_, f32[4096,512]{1,0:T(8,128)} %fwd.5.refs_1_, bf16[4,4,3,128,512]{4,3,2,1,0:T(8,128)(2,1)} %bitcast.67), custom_call_target="tpu_custom_call" | custom-call | flops 25769803776 | bytes 27262976 | tf_op jit(solution)/shard_map/fwd/pallas_call | solution.py:74
  184.5 9.2 all-gather.23.cloned.1.call-done
  193.6 36.4 %fwd.7 = f32[4096,512]{1,0:T(8,128)} custom-call(bf16[4096,512]{1,0:T(8,128)(2,1)} %fusion.1.refs_0_.refs_2_, f32[4096,512]{1,0:T(8,128)} %fwd.6.refs_1_, bf16[4,4,3,128,512]{4,3,2,1,0:T(8,128)(2,1)} %bitcast.65), custom_call_target="tpu_custom_call" | custom-call | flops 25769803776 | bytes 27262976 | tf_op jit(solution)/shard_map/fwd/pallas_call | solution.py:74
  230.0 5.9 fusion.4
  236.5 1.4 copy-done
  237.9 2.5 fusion.5.refs_0_.refs_2_
  240.4 93.2 %bwd.8 = (bf16[4,4,3,128,512]{4,3,2,1,0:T(8,128)(2,1)}, f32[4096,512]{1,0:T(8,128)}) custom-call(bf16[4096,512]{1,0:T(8,128)(2,1)} %fusion.5.refs_0_.refs_2_, bf16[4096,512]{1,0:T(8,128)(2,1)} %bitcast.61, bf16[4,4,3,128,512]{4,3,2,1,0:T(8,128)(2,1)} %bitcast.76), custom_call_target="tpu_custom_call" | custom-call | flops 68719476736 | bytes 33554432 | tf_op jit(solution)/shard_map/bwd/pallas_call | solution.py:183
  333.8 2.9 pack.15
  336.7 93.7 %bwd.9 = (bf16[4,4,3,128,512]{4,3,2,1,0:T(8,128)(2,1)}, f32[4096,512]{1,0:T(8,128)}) custom-call(bf16[4096,512]{1,0:T(8,128)(2,1)} %fusion.5.refs_0_.refs_2_, bf16[4096,512]{1,0:T(8,128)(2,1)} %bitcast.62, f32[4096,512]{1,0:T(8,128)} %get-tuple-element.94.refs_2_, bf16[4,4,3,128,512]{4,3,2,1,0:T(8,128)(2,1)} %bitcast.74), custom_call_target="tpu_custom_call" | custom-call | flops 68719476736 | bytes 33554432 | tf_op jit(solution)/shard_map/bwd/pallas_call | solution.py:183
  430.6 93.6 %bwd.10 = (bf16[4,4,3,128,512]{4,3,2,1,0:T(8,128)(2,1)}, f32[4096,512]{1,0:T(8,128)}) custom-call(bf16[4096,512]{1,0:T(8,128)(2,1)} %fusion.5.refs_0_.refs_2_, bf16[4096,512]{1,0:T(8,128)(2,1)} %bitcast.63, f32[4096,512]{1,0:T(8,128)} %get-tuple-element.98.refs_2_, bf16[4,4,3,128,512]{4,3,2,1,0:T(8,128)(2,1)} %bitcast.73), custom_call_target="tpu_custom_call" | custom-call | flops 68719476736 | bytes 33554432 | tf_op jit(solution)/shard_map/bwd/pallas_call | solution.py:183
  525.4 35.5 %collective-permute-done.refs_3_.refs_4_.refs_5_ = bf16[4,3,128,512]{3,2,1,0:T(8,128)(2,1)S(1)} collective-permute-done((bf16[4,3,128,512]{3,2,1,0:T(8,128)(2,1)}, bf16[4,3,128,512]{3,2,1,0:T(8,128)(2,1)S(1)}, u32[]{:S(2)}, u32[]{:S(2)}) %collective-permute-start) | collective-permute-done | bytes 1572896 | tf_op jit(solution)/shard_map/ppermute | solution.py:296
  560.9 1.2 copy-done.14
  562.1 8.3 adam.8
  570.5 93.0 %bwd.11 = (bf16[4,4,3,128,512]{4,3,2,1,0:T(8,128)(2,1)}, f32[4096,512]{1,0:T(8,128)}) custom-call(bf16[4,3,128,512]{3,2,1,0:T(8,128)(2,1)} %bitcast.48, f32[8,128]{1,0:T(8,128)} %get-tuple-element.97.refs_1_, bf16[4096,512]{1,0:T(8,128)(2,1)} %fusion.5.refs_0_.refs_2_, bf16[4096,512]{1,0:T(8,128)(2,1)} %bitcast.64, f32[4096,512]{1,0:T(8,128)} %get-tuple-element.99.refs_4_, ...), custom_call_target="tpu_custom_call" | custom-call | flops 68719476736 | bytes 33554432 | tf_op jit(solution)/shard_map/bwd/pallas_call | solution.py:183
  663.6 1.3 copy-done.8
  664.9 1.3 collective-permute-start.2
  666.2 34.4 %collective-permute-done.2.refs_3_.refs_4_.refs_5_ = bf16[4,3,128,512]{3,2,1,0:T(8,128)(2,1)S(1)} collective-permute-done((bf16[4,3,128,512]{3,2,1,0:T(8,128)(2,1)S(1)}, bf16[4,3,128,512]{3,2,1,0:T(8,128)(2,1)S(1)}, u32[]{:S(2)}, u32[]{:S(2)}) %collective-permute-start.2) | collective-permute-done | bytes 1572896 | tf_op jit(solution)/shard_map/ppermute | solution.py:296
  701.7 8.4 adam.9
  710.1 5.7 fusion.6
  716.0 2.6 copy-done.3
  718.6 4.9 fusion.7.refs_3_
  723.5 72.4 %bwd.13 = bf16[4,4,3,128,512]{4,3,2,1,0:T(8,128)(2,1)} custom-call(bf16[4,3,128,512]{3,2,1,0:T(8,128)(2,1)} %bitcast.29, f32[8,128]{1,0:T(8,128)} %get-tuple-element.122.refs_1_, bf16[4096,512]{1,0:T(8,128)(2,1)} %fusion.1.refs_0_.refs_2_, bf16[4096,512]{1,0:T(8,128)(2,1)} %fusion.7.refs_3_, bf16[4,4,3,128,512]{4,3,2,1,0:T(8,128)(2,1)} %bitcast.72), custom_call_target="tpu_custom_call" | custom-call | flops 51539607552 | bytes 33554432 | tf_op jit(solution)/shard_map/bwd/pallas_call | solution.py:183
  796.0 1.3 copy-done.5
  797.3 1.4 collective-permute-start.1
  798.7 33.5 %collective-permute-done.1.refs_3_.refs_4_.refs_5_ = bf16[4,3,128,512]{3,2,1,0:T(8,128)(2,1)S(1)} collective-permute-done((bf16[4,3,128,512]{3,2,1,0:T(8,128)(2,1)S(1)}, bf16[4,3,128,512]{3,2,1,0:T(8,128)(2,1)S(1)}, u32[]{:S(2)}, u32[]{:S(2)}) %collective-permute-start.1) | collective-permute-done | bytes 1572896 | tf_op jit(solution)/shard_map/ppermute | solution.py:296
  832.2 1.2 copy-done.11
  833.4 8.4 adam.10
  841.8 72.4 %bwd.12 = bf16[4,4,3,128,512]{4,3,2,1,0:T(8,128)(2,1)} custom-call(bf16[4,3,128,512]{3,2,1,0:T(8,128)(2,1)} %bitcast.34, f32[8,128]{1,0:T(8,128)} %get-tuple-element.120.refs_1_, bf16[4096,512]{1,0:T(8,128)(2,1)} %fusion.1.refs_0_.refs_2_, bf16[4096,512]{1,0:T(8,128)(2,1)} %fusion.7.refs_3_, bf16[4,4,3,128,512]{4,3,2,1,0:T(8,128)(2,1)} %bitcast.70), custom_call_target="tpu_custom_call" | custom-call | flops 51539607552 | bytes 33554432 | tf_op jit(solution)/shard_map/bwd/pallas_call | solution.py:183
  914.3 1.3 copy-done.6
  915.6 1.6 collective-permute-start.4
  917.2 32.8 %collective-permute-done.4.refs_3_.refs_4_.refs_5_ = bf16[4,3,128,512]{3,2,1,0:T(8,128)(2,1)S(1)} collective-permute-done((bf16[4,3,128,512]{3,2,1,0:T(8,128)(2,1)S(1)}, bf16[4,3,128,512]{3,2,1,0:T(8,128)(2,1)S(1)}, u32[]{:S(2)}, u32[]{:S(2)}) %collective-permute-start.4) | collective-permute-done | bytes 1572896 | tf_op jit(solution)/shard_map/ppermute | solution.py:296
  950.0 1.2 copy-done.12
  951.2 8.2 adam.11
  959.4 72.5 %bwd.15 = bf16[4,4,3,128,512]{4,3,2,1,0:T(8,128)(2,1)} custom-call(bf16[4,3,128,512]{3,2,1,0:T(8,128)(2,1)} %bitcast.39, f32[8,128]{1,0:T(8,128)} %get-tuple-element.142.refs_1_, bf16[4096,512]{1,0:T(8,128)(2,1)} %fusion.1.refs_0_.refs_2_, bf16[4096,512]{1,0:T(8,128)(2,1)} %fusion.7.refs_3_, bf16[4,4,3,128,512]{4,3,2,1,0:T(8,128)(2,1)} %bitcast.68), custom_call_target="tpu_custom_call" | custom-call | flops 51539607552 | bytes 33554432 | tf_op jit(solution)/shard_map/bwd/pallas_call | solution.py:183
  1031.9 1.3 copy-done.7
  1033.3 1.6 collective-permute-start.3
  1034.9 32.0 %collective-permute-done.3.refs_3_.refs_4_.refs_5_ = bf16[4,3,128,512]{3,2,1,0:T(8,128)(2,1)S(1)} collective-permute-done((bf16[4,3,128,512]{3,2,1,0:T(8,128)(2,1)S(1)}, bf16[4,3,128,512]{3,2,1,0:T(8,128)(2,1)S(1)}, u32[]{:S(2)}, u32[]{:S(2)}) %collective-permute-start.3) | collective-permute-done | bytes 1572896 | tf_op jit(solution)/shard_map/ppermute | solution.py:296
  1066.9 1.2 copy-done.13
  1068.1 8.5 adam.12
  1076.6 72.5 %bwd.14 = bf16[4,4,3,128,512]{4,3,2,1,0:T(8,128)(2,1)} custom-call(bf16[4,3,128,512]{3,2,1,0:T(8,128)(2,1)} %bitcast.24, f32[8,128]{1,0:T(8,128)} %get-tuple-element.141.refs_1_, bf16[4096,512]{1,0:T(8,128)(2,1)} %fusion.1.refs_0_.refs_2_, bf16[4096,512]{1,0:T(8,128)(2,1)} %fusion.7.refs_3_, bf16[4,4,3,128,512]{4,3,2,1,0:T(8,128)(2,1)} %bitcast.66), custom_call_target="tpu_custom_call" | custom-call | flops 51539607552 | bytes 33554432 | tf_op jit(solution)/shard_map/bwd/pallas_call | solution.py:183
  1149.1 1.4 copy-done.4
  1150.5 1.7 collective-permute-start.7
  1152.5 50.4 %reduce-scatter.37.cloned.1.call-done = bf16[1,4,3,128,512]{4,3,2,1,0:T(8,128)(2,1)} async-done(((bf16[4,4,3,128,512]{4,3,2,1,0:T(8,128)(2,1)}), bf16[1,4,3,128,512]{4,3,2,1,0:T(8,128)(2,1)}) %reduce-scatter.37.cloned.1.call-update) | async-done | bytes 1572880
  1203.0 1.5 collective-permute-start.5
  1204.4 8.2 adam.13
  1212.6 9.0 collective-permute-done.6.refs_3_.refs_4_.refs_5_
  1221.6 8.2 adam.14
  1229.7 21.0 %collective-permute-done.5.refs_3_.refs_4_.refs_5_ = bf16[4,3,128,512]{3,2,1,0:T(8,128)(2,1)S(1)} collective-permute-done((bf16[4,3,128,512]{3,2,1,0:T(8,128)(2,1)}, bf16[4,3,128,512]{3,2,1,0:T(8,128)(2,1)S(1)}, u32[]{:S(2)}, u32[]{:S(2)}) %collective-permute-start.5) | collective-permute-done | bytes 1572896 | tf_op jit(solution)/shard_map/ppermute | solution.py:302
  1250.7 1.2 copy-done.9
  1251.9 8.2 adam.15
  (75 shorter events, 4.7 us)
Async XLA Ops:
  7.2 49.4 %all-gather.17.cloned.1.call-start = ((), (), s32[]{:S(2)}) async-start(), calls=%async_computation.8 | async-start | bytes 7864320 | tf_op jit(solution)/shard_map/all_gather | solution.py:273
  10.1 92.2 %all-gather.19.cloned.1.call-start = ((), (), s32[]{:S(2)}) async-start(), calls=%async_computation.9 | async-start | bytes 7864320 | tf_op jit(solution)/shard_map/all_gather | solution.py:273
  13.0 135.0 %all-gather.21.cloned.1.call-start = ((), (), s32[]{:S(2)}) async-start(), calls=%async_computation.10 | async-start | bytes 7864320 | tf_op jit(solution)/shard_map/all_gather | solution.py:273
  15.9 177.7 %all-gather.23.cloned.1.call-start = ((), (), s32[]{:S(2)}) async-start(), calls=%async_computation.11 | async-start | bytes 7864320 | tf_op jit(solution)/shard_map/all_gather | solution.py:273
  19.0 221.4 %all-gather.25.cloned.1.call-start = ((), (), s32[]{:S(2)}) async-start(), calls=%async_computation.12 | async-start | bytes 7864320 | tf_op jit(solution)/shard_map/all_gather | solution.py:273
  22.4 314.3 %all-gather.27.cloned.1.call-start = ((), (), s32[]{:S(2)}) async-start(), calls=%async_computation.13 | async-start | bytes 7864320 | tf_op jit(solution)/shard_map/all_gather | solution.py:273
  25.3 405.2 %all-gather.29.cloned.1.call-start = ((), (), s32[]{:S(2)}) async-start(), calls=%async_computation.14 | async-start | bytes 7864320 | tf_op jit(solution)/shard_map/all_gather | solution.py:273
  28.2 496.0 %reduce-scatter.27.cloned.1.call-start = ((), (), s32[]{:S(2)}) async-start(), calls=%async_computation.17 | async-start | bytes 7864320
  28.3 3.5 copy-start.2
  235.9 0.6 copy-start.17
  235.9 2.0 copy-start
  236.5 1.4 copy-start.15
  333.7 236.7 %all-gather.31.cloned.1.call-start = ((), (), s32[]{:S(2)}) async-start(), calls=%async_computation.15 | async-start | bytes 7864320 | tf_op jit(solution)/shard_map/all_gather | solution.py:273
  336.6 233.8 %reduce-scatter.25.cloned.1.call-start = ((), (), s32[]{:S(2)}) async-start(), calls=%async_computation.16 | async-start | bytes 7864320
  430.5 293.0 %reduce-scatter.31.cloned.1.call-start = ((), (), s32[]{:S(2)}) async-start(), calls=%async_computation.19 | async-start | bytes 7864320
  524.2 317.7 %reduce-scatter.29.cloned.1.call-start = ((), (), s32[]{:S(2)}) async-start(), calls=%async_computation.18 | async-start | bytes 7864320
  524.2 36.7 %collective-permute-start = (bf16[4,3,128,512]{3,2,1,0:T(8,128)(2,1)}, bf16[4,3,128,512]{3,2,1,0:T(8,128)(2,1)S(1)}, u32[]{:S(2)}, u32[]{:S(2)}) collective-permute-start(bf16[4,3,128,512]{3,2,1,0:T(8,128)(2,1)} %bitcast.57), channel_id=1, source_target_pairs={{0,4},{4,0},{1,5},{5,1},{2,6},{6,2},{3,7},{7,3}} | collective-permute-start | bytes 4718600 | tf_op jit(solution)/shard_map/ppermute | solution.py:296
  560.9 1.2 copy-start.14
  663.5 1.4 copy-start.8
  663.5 295.8 %reduce-scatter.35.cloned.1.call-start = ((), (), s32[]{:S(2)}) async-start(), calls=%async_computation.21 | async-start | bytes 7864320
  664.9 35.7 %collective-permute-start.2 = (bf16[4,3,128,512]{3,2,1,0:T(8,128)(2,1)S(1)}, bf16[4,3,128,512]{3,2,1,0:T(8,128)(2,1)S(1)}, u32[]{:S(2)}, u32[]{:S(2)}) collective-permute-start(bf16[4,3,128,512]{3,2,1,0:T(8,128)(2,1)S(1)} %bitcast.52), channel_id=1, source_target_pairs={{0,4},{4,0},{1,5},{5,1},{2,6},{6,2},{3,7},{7,3}} | collective-permute-start | bytes 4718600 | tf_op jit(solution)/shard_map/ppermute | solution.py:296
  700.6 1.1 copy-start.10
  701.7 14.1 %copy-start.18 = (f32[4096]{0:T(1024)S(1)}, f32[4096]{0:T(1024)}, u32[]{:S(2)}) copy-start(f32[4096]{0:T(1024)} %copy-done.17) | copy-start | bytes 49156
  710.1 5.8 copy-start.1
  710.1 8.4 copy-start.3
  710.1 8.4 copy-start.16
  795.9 1.4 copy-start.5
  795.9 280.7 %reduce-scatter.33.cloned.1.call-start = ((), (), s32[]{:S(2)}) async-start(), calls=%async_computation.20 | async-start | bytes 7864320
  797.3 34.9 %collective-permute-start.1 = (bf16[4,3,128,512]{3,2,1,0:T(8,128)(2,1)S(1)}, bf16[4,3,128,512]{3,2,1,0:T(8,128)(2,1)S(1)}, u32[]{:S(2)}, u32[]{:S(2)}) collective-permute-start(bf16[4,3,128,512]{3,2,1,0:T(8,128)(2,1)S(1)} %bitcast.33), channel_id=1, source_target_pairs={{0,4},{4,0},{1,5},{5,1},{2,6},{6,2},{3,7},{7,3}} | collective-permute-start | bytes 4718600 | tf_op jit(solution)/shard_map/ppermute | solution.py:296
  832.2 1.2 copy-start.11
  914.2 1.4 copy-start.6
  914.2 237.9 %reduce-scatter.39.cloned.1.call-start = ((), (), s32[]{:S(2)}) async-start(), calls=%async_computation.23 | async-start | bytes 7864320
  915.6 34.3 %collective-permute-start.4 = (bf16[4,3,128,512]{3,2,1,0:T(8,128)(2,1)S(1)}, bf16[4,3,128,512]{3,2,1,0:T(8,128)(2,1)S(1)}, u32[]{:S(2)}, u32[]{:S(2)}) collective-permute-start(bf16[4,3,128,512]{3,2,1,0:T(8,128)(2,1)S(1)} %bitcast.38), channel_id=1, source_target_pairs={{0,4},{4,0},{1,5},{5,1},{2,6},{6,2},{3,7},{7,3}} | collective-permute-start | bytes 4718600 | tf_op jit(solution)/shard_map/ppermute | solution.py:296
  950.0 1.2 copy-start.12
  1031.8 1.4 copy-start.7
  1031.9 171.1 %reduce-scatter.37.cloned.1.call-start = ((), (), s32[]{:S(2)}) async-start(), calls=%async_computation.22 | async-start | bytes 7864320
  1033.3 33.6 %collective-permute-start.3 = (bf16[4,3,128,512]{3,2,1,0:T(8,128)(2,1)S(1)}, bf16[4,3,128,512]{3,2,1,0:T(8,128)(2,1)S(1)}, u32[]{:S(2)}, u32[]{:S(2)}) collective-permute-start(bf16[4,3,128,512]{3,2,1,0:T(8,128)(2,1)S(1)} %bitcast.43), channel_id=1, source_target_pairs={{0,4},{4,0},{1,5},{5,1},{2,6},{6,2},{3,7},{7,3}} | collective-permute-start | bytes 4718600 | tf_op jit(solution)/shard_map/ppermute | solution.py:296
  1066.9 1.2 copy-start.13
  1149.1 1.4 copy-start.4
  1150.5 53.9 %collective-permute-start.7 = (bf16[4,3,128,512]{3,2,1,0:T(8,128)(2,1)S(1)}, bf16[4,3,128,512]{3,2,1,0:T(8,128)(2,1)}, u32[]{:S(2)}, u32[]{:S(2)}) collective-permute-start(bf16[4,3,128,512]{3,2,1,0:T(8,128)(2,1)S(1)} %bitcast.28), channel_id=1, source_target_pairs={{0,4},{4,0},{1,5},{5,1},{2,6},{6,2},{3,7},{7,3}} | collective-permute-start | bytes 4718600 | tf_op jit(solution)/shard_map/ppermute | solution.py:296
  1152.2 69.4 %collective-permute-start.6 = (bf16[4,3,128,512]{3,2,1,0:T(8,128)(2,1)}, bf16[4,3,128,512]{3,2,1,0:T(8,128)(2,1)}, u32[]{:S(2)}, u32[]{:S(2)}) collective-permute-start(bf16[4,3,128,512]{3,2,1,0:T(8,128)(2,1)} %bitcast.44), channel_id=1, source_target_pairs={{0,4},{4,0},{1,5},{5,1},{2,6},{6,2},{3,7},{7,3}} | collective-permute-start | bytes 4718600 | tf_op jit(solution)/shard_map/ppermute | solution.py:302
  1203.0 47.8 %collective-permute-start.5 = (bf16[4,3,128,512]{3,2,1,0:T(8,128)(2,1)}, bf16[4,3,128,512]{3,2,1,0:T(8,128)(2,1)S(1)}, u32[]{:S(2)}, u32[]{:S(2)}) collective-permute-start(bf16[4,3,128,512]{3,2,1,0:T(8,128)(2,1)} %bitcast.53), channel_id=1, source_target_pairs={{0,4},{4,0},{1,5},{5,1},{2,6},{6,2},{3,7},{7,3}} | collective-permute-start | bytes 4718600 | tf_op jit(solution)/shard_map/ppermute | solution.py:302
  1250.7 1.2 copy-start.9
Sparse Core Ops, SparseCore 0:
  10.2 46.3 all-gather.16
  58.7 43.5 all-gather.18
  104.4 43.5 all-gather.20
  150.0 43.5 all-gather.22
  195.6 43.5 all-gather.24
  241.1 43.5 all-gather.26
  286.8 43.6 all-gather.28
  333.8 53.3 reduce-scatter.26
  388.7 43.5 all-gather.30
  434.7 53.2 reduce-scatter.24
  524.3 53.3 reduce-scatter.30
  663.6 53.4 reduce-scatter.28
  796.0 53.5 reduce-scatter.34
  914.4 53.7 reduce-scatter.32
  1032.0 53.6 reduce-scatter.38
  1149.2 53.6 reduce-scatter.36

commit v2 on v0

v2 whole, which is shorter than its diff:
```python
import functools
import jax, jax.numpy as jnp
from jax import lax
from jax.experimental import pallas as pl
from jax.experimental.pallas import tpu as pltpu
from jax.sharding import PartitionSpec as P

F32, BF16 = jnp.float32, jnp.bfloat16
TOK, D, W = 4096, 512, 512
T = 512
NT = TOK // T
ROWS = 32
ANY = pl.BlockSpec(memory_space=pl.ANY)
STRIP = pl.BlockSpec((4, 1, 3, 128, 512), lambda k: (0, k, 0, 0, 0))


def dot(a, b):
    return jnp.dot(a, b, preferred_element_type=F32)


def tile(ref, t):
    return ref.at[pl.ds(pl.multiple_of(t * T, T), T), :]


def copies(src, dst, sem, t):
    return pltpu.make_async_copy(tile(src, t), tile(dst, t), sem.at[t])


def pipelined(head, tail, before, after):
    before(0, 1)
    head(0, 0)

    @pl.loop(0, NT // 2 - 1)
    def _(i):
        before(2 * i + 1, 2)
        head(2 * i + 1, 1)
        tail(2 * i, 0)
        head(2 * i + 2, 0)
        tail(2 * i + 1, 1)
        after(2 * i, 2)

    before(NT - 1, 1)
    head(NT - 1, 1)
    tail(NT - 2, 0)
    tail(NT - 1, 1)


def fwd_kernel(n, first, *refs):
    refs = list(refs)
    a_h = refs.pop(0)
    y_h = None if first else refs.pop(0)
    p, out_h, a_v, y_v, g0, u0, g1, u1, act_s, sa, sy, so = refs
    k = pl.program_id(0)
    gate_s, up_s = (g0, g1), (u0, u1)

    @pl.when(k == 0)
    def _():
        for t in range(NT):
            copies(a_h, a_v, sa, t).start()
            if not first:
                copies(y_h, y_v, sy, t).start()

    def before(t, count):
        @pl.when(k == 0)
        def _():
            for i in range(count):
                copies(a_h, a_v, sa, t + i).wait()
                if not first:
                    copies(y_h, y_v, sy, t + i).wait()

    def head(t, slot):
        a = tile(a_v, t)[...]
        gate_s[slot][...] = dot(a, p[:, 0, 0].reshape(D, W))
        up_s[slot][...] = dot(a, p[:, 0, 1].reshape(D, W))

    def tail(t, slot):
        for r in range(0, T, ROWS):
            gate = gate_s[slot][r : r + ROWS]
            act_s[r : r + ROWS] = (gate * jax.nn.sigmoid(gate) * up_s[slot][r : r + ROWS]).astype(BF16)
        old = tile(y_v, t)[...]
        if first:
            old = jnp.where(k == 0, 0.0, old)
        tile(y_v, t)[...] = old + dot(act_s[...], p[:, 0, 2].reshape(W, D))

    def after(t, count):
        @pl.when(k == n - 1)
        def _():
            for i in range(count):
                copies(y_v, out_h, so, t + i).start()

    pipelined(head, tail, before, after)
    after(NT - 2, 2)

    @pl.when(k == n - 1)
    def _():
        for t in range(NT):
            copies(y_v, out_h, so, t).wait()


def fwd(a, p, y=None):
    n = p.shape[1]
    first = y is None
    sem = pltpu.SemaphoreType.DMA((NT,))
    return pl.pallas_call(
        functools.partial(fwd_kernel, n, first),
        grid=(n,),
        out_shape=jax.ShapeDtypeStruct((TOK, D), F32),
        in_specs=[ANY] * (1 if first else 2) + [STRIP],
        out_specs=ANY,
        scratch_shapes=[pltpu.VMEM((TOK, D), BF16), pltpu.VMEM((TOK, D), F32)] + [pltpu.VMEM((T, W), F32)] * 4 + [pltpu.VMEM((T, W), BF16)] + [sem] * 3,
        compiler_params=pltpu.CompilerParams(vmem_limit_bytes=60 << 20, dimension_semantics=("arbitrary",)),
        cost_estimate=pl.CostEstimate(flops=6 * TOK * D * W * n, bytes_accessed=n * 3 * (1 << 19) + (20 << 20), transcendentals=TOK * W * n),
        name="fwd",
    )(*((a,) if first else (a, y)), p)


def adamw(w, m, v, g):
    m = 0.9 * m + 0.1 * g
    v = 0.95 * v + 0.05 * g * g
    step = m * lax.rsqrt(v + 1e-8) + 0.1 * w
    return (w - 0.02 * step).astype(BF16), m, v


def adam_step(ins, outs):
    gs, gr, w, m, v = (ins[3 * i : 3 * i + 3] for i in range(5))
    for which in range(3):
        g = (gs[which][...].astype(F32) + gr[which][...].astype(F32)).astype(BF16).astype(F32)
        for k in range(4 if which < 2 else 1):
            c = slice(128 * k, 128 * (k + 1)) if which < 2 else slice(0, 512)
            new = adamw(w[which][0, :, c].astype(F32), m[which][0, :, c], v[which][0, :, c], g[k, 0])
            for i in range(3):
                outs[3 * i + which][0, :, c] = new[i]


def adam_specs(l, j):
    cols = [pl.BlockSpec((4, 1, 128, 128), functools.partial(lambda which, i: (0, which, 0, i), which)) for which in range(2)]
    cols.append(pl.BlockSpec((1, 1, 128, 512), lambda i: (i, 2, 0, 0)))
    own = [pl.BlockSpec((1, 128, 512), lambda i: (l, 0, 4 * i + j))] * 2 + [pl.BlockSpec((1, 128, 512), lambda i: (l, 4 * j + i, 0))]
    return cols * 2 + own * 3, own * 3


def bwd_kernel(n, need, first, state, skip, *refs):
    refs = list(refs)
    take = lambda count: [refs.pop(0) for _ in range(count)]
    take(skip)
    ad_in = take(15) if state else []
    a_h, dy_h, aT_h, dyT_h = take(4)
    da_h = take(1)[0] if need and not first else None
    p = refs.pop(0)
    g = refs.pop(0)
    out_h = refs.pop(0) if need else None
    ad_out = take(9) if state else []
    a_v, dy_v, aT, dyT, act_v, dgu_v, wT, wdT = take(8)
    gate_s, up_s, dact_s = take(2), take(2), take(2)
    da_v = refs.pop(0) if need else None
    sa, sd, st = take(3)
    sp, so = take(2) if need else (None, None)
    k = pl.program_id(0)

    def turned(which):
        return pltpu.make_async_copy((aT_h, dyT_h)[which], (aT, dyT)[which], st.at[which])

    @pl.when(k == 0)
    def _():
        for t in range(NT):
            copies(a_h, a_v, sa, t).start()
            copies(dy_h, dy_v, sd, t).start()
            if need and not first:
                copies(da_h, da_v, sp, t).start()
        for which in range(2):
            turned(which).start()

    def before(t, count):
        @pl.when(k == 0)
        def _():
            for i in range(count):
                copies(a_h, a_v, sa, t + i).wait()
                copies(dy_h, dy_v, sd, t + i).wait()
                if need and not first:
                    copies(da_h, da_v, sp, t + i).wait()

    def head(t, slot):
        a = tile(a_v, t)[...]
        gate_s[slot][...] = dot(a, p[:, 0, 0].reshape(D, W))
        up_s[slot][...] = dot(a, p[:, 0, 1].reshape(D, W))
        dact_s[slot][...] = dot(tile(dy_v, t)[...], wdT[...]).astype(BF16)

    def tail(t, slot):
        for r in range(0, T, ROWS):
            rows = slice(r, r + ROWS)
            here = pl.ds(pl.multiple_of(t * T + r, ROWS), ROWS)
            gate, up, dact = gate_s[slot][rows], up_s[slot][rows], dact_s[slot][rows].astype(F32)
            sig = jax.nn.sigmoid(gate)
            silu = gate * sig
            act_v[here] = (silu * up).astype(BF16)
            dgu_v[here, W:] = (dact * silu).astype(BF16)
            dgu_v[here, :W] = (dact * up * (sig + silu * (1 - sig))).astype(BF16)
        if need:
            old = tile(da_v, t)[...]
            if first:
                old = jnp.where(k == 0, 0.0, old)
            tile(da_v, t)[...] = old + dot(tile(dgu_v, t)[...], wT[...])

    def after(t, count):
        if need:
            @pl.when(k == n - 1)
            def _():
                for i in range(count):
                    copies(da_v, out_h, so, t + i).start()

    wdT[...] = p[:, 0, 2].reshape(W, D).T
    if need:
        wT[:W] = p[:, 0, 0].reshape(D, W).T
        wT[W:] = p[:, 0, 1].reshape(D, W).T
    pipelined(head, tail, before, after)
    after(NT - 2, 2)

    @pl.when(k == 0)
    def _():
        for which in range(2):
            turned(which).wait()

    for which in range(2):
        g[:, 0, which] = dot(aT[...], dgu_v[:, W * which : W * (which + 1)]).astype(BF16).reshape(4, 128, W)
    g[:, 0, 2] = dot(dyT[...], act_v[...]).astype(BF16).T.reshape(4, 128, D)
    if state:
        adam_step(ad_in, ad_out)

    if need:
        @pl.when(k == n - 1)
        def _():
            for t in range(NT):
                copies(da_v, out_h, so, t).wait()


def bwd(a, dy, aT, dyT, p, da=None, need=True, deps=(), state=None):
    n = p.shape[1]
    first = da is None
    sem = pltpu.SemaphoreType.DMA((NT,))
    args = list(deps)
    specs = [ANY] * len(args)
    out_shapes = [jax.ShapeDtypeStruct((4, n, 3, 128, 512), BF16)]
    out_specs = [STRIP]
    if need:
        out_shapes.append(jax.ShapeDtypeStruct((TOK, D), F32))
        out_specs.append(ANY)
    aliases = {}
    if state:
        l, j, gs, gr, weights, m, v, before = state
        before = list(before or [])
        aliases = {len(args) + i: len(out_shapes) + i for i in range(len(before))}
        args += before
        specs += [ANY] * len(before)
    skip = len(args)
    if state:
        ins, outs = adam_specs(l, j)
        args += [gs] * 3 + [gr] * 3 + [*weights, *m, *v]
        specs += ins
        out_shapes += [jax.ShapeDtypeStruct(w.shape, dt) for dt in (BF16, F32, F32) for w in weights]
        out_specs += outs
    rest = [a, dy, aT, dyT] + ([da] if need and not first else [])
    args += rest + [p]
    specs += [ANY] * len(rest) + [STRIP]
    big = lambda dt: pltpu.VMEM((TOK, D), dt)
    return pl.pallas_call(
        functools.partial(bwd_kernel, n, need, first, bool(state), skip),
        grid=(n,),
        out_shape=out_shapes,
        in_specs=specs,
        out_specs=out_specs,
        scratch_shapes=[big(BF16)] * 2 + [pltpu.VMEM((D, TOK), BF16)] * 2 + [big(BF16), pltpu.VMEM((TOK, 2 * W), BF16), pltpu.VMEM((2 * W, D), BF16), pltpu.VMEM((D, W), BF16)]
        + [pltpu.VMEM((T, W), F32)] * 4 + [pltpu.VMEM((T, W), BF16)] * 2
        + ([big(F32)] if need else []) + [sem] * 2 + [pltpu.SemaphoreType.DMA((2,))] + ([sem] * 2 if need else []),
        input_output_aliases=aliases,
        compiler_params=pltpu.CompilerParams(vmem_limit_bytes=63 << 20, dimension_semantics=("arbitrary",)),
        cost_estimate=pl.CostEstimate(flops=2 * (8 if need else 6) * TOK * D * W * n, bytes_accessed=n * 6 * (1 << 19) + (20 << 20), transcendentals=TOK * W * n),
        name="bwd",
    )(*args)


def normed(h):
    wide = h.astype(F32)
    scale = lax.rsqrt(jnp.mean(wide**2, -1, keepdims=True) + 1e-6)
    return (wide * scale).astype(BF16)


def rowwise(body, ins, outs):
    spec = lambda one: pl.BlockSpec((T, D), lambda t: (t, 0)) if one.shape[0] == TOK else pl.BlockSpec((D, T), lambda t: (0, t))
    return pl.pallas_call(
        body,
        grid=(NT,),
        out_shape=outs,
        in_specs=[spec(one) for one in ins],
        out_specs=[spec(one) for one in outs],
        cost_estimate=pl.CostEstimate(flops=20 * TOK * D, bytes_accessed=24 << 20, transcendentals=TOK),
    )(*ins)


ROW, COL = jax.ShapeDtypeStruct((TOK, D), BF16), jax.ShapeDtypeStruct((D, TOK), BF16)


def start_kernel(x, dy, a, aT, dyT):
    a[...] = normed(x[...])
    aT[...] = a[...].T
    dyT[...] = dy[...].T


def middle_kernel(x, y, h, a, aT):
    h[...] = (x[...].astype(F32) + y[...].astype(BF16).astype(F32)).astype(BF16)
    a[...] = normed(h[...])
    aT[...] = a[...].T


def back_kernel(h, dy, da, dh, dhT):
    wide = h[...].astype(F32)
    scale = lax.rsqrt(jnp.mean(wide**2, -1, keepdims=True) + 1e-6)
    by_a = da[...].astype(BF16).astype(F32)
    by_h = by_a * scale - wide * (scale * scale * scale * jnp.mean(by_a * wide, -1, keepdims=True))
    dh[...] = (dy[...].astype(F32) + by_h.astype(BF16).astype(F32)).astype(BF16)
    dhT[...] = dh[...].T


CHUNKS = 4


def pack_kernel(*refs):
    gates, ups, down, out = refs[:4], refs[4:8], refs[8], refs[9]
    for k in range(4):
        for which, parts in ((0, gates), (1, ups)):
            for s in range(4):
                out[k, which, :, 128 * s : 128 * (s + 1)] = parts[s][0, :, 128 * k : 128 * (k + 1)]
        out[k, 2] = down[0, 128 * k : 128 * (k + 1), :]


def pack(l, j, w_gate, w_up, w_down):
    wide = [pl.BlockSpec((1, 128, 512), functools.partial(lambda s, i: (l, 0, 4 * s + j), s)) for s in range(4)]
    return pl.pallas_call(
        pack_kernel,
        grid=(1,),
        out_shape=jax.ShapeDtypeStruct((4, 3, 128, 512), BF16),
        in_specs=wide + wide + [pl.BlockSpec((1, 512, 512), lambda i: (l, j, 0))],
        out_specs=pl.BlockSpec((4, 3, 128, 512), lambda i: (0, 0, 0, 0)),
        cost_estimate=pl.CostEstimate(flops=1 << 21, bytes_accessed=3 << 20, transcendentals=0),
        name="pack",
    )(*[w_gate] * 4, *[w_up] * 4, w_down)


def adam_kernel(skip, *refs):
    adam_step(refs[skip : skip + 15], refs[skip + 15 : skip + 24])


def adam(l, j, gs, gr, weights, m, v, before):
    ins, outs = adam_specs(l, j)
    shapes = [jax.ShapeDtypeStruct(w.shape, dt) for dt in (BF16, F32, F32) for w in weights]
    before = list(before or [])
    return pl.pallas_call(
        functools.partial(adam_kernel, len(before)),
        grid=(4,),
        out_shape=shapes,
        in_specs=[ANY] * len(before) + ins,
        out_specs=outs,
        input_output_aliases={i: i for i in range(len(before))},
        cost_estimate=pl.CostEstimate(flops=10 * 3 * 4 * 128 * 512, bytes_accessed=18 << 20, transcendentals=3 * 4 * 128 * 512),
        name="adam",
    )(*before, *[gs] * 3, *[gr] * 3, *weights, *m, *v)


def solution(mesh):
    pairs = [(0, 1), (1, 0)]

    def step(x, dy, *arrays):
        weights, m, v = (arrays[i : i + 3] for i in (0, 3, 6))
        x, dy = x[0], dy[0]
        full = [[lax.all_gather(pack(l, j, *weights), "s", axis=0) for j in range(CHUNKS)] for l in range(2)]
        a0, a0T, dyT = rowwise(start_kernel, [x, dy], [ROW, COL, COL])
        y = None
        for j in range(CHUNKS):
            y = fwd(a0, full[0][j], y)
        h1, a1, a1T = rowwise(middle_kernel, [x, y], [ROW, ROW, COL])
        order = [(1, j) for j in range(CHUNKS)] + [(0, j) for j in range(CHUNKS)]
        ours, theirs, out, da = [], [], None, None
        for i, (l, j) in enumerate(order):
            deps, state = [], None
            if i >= 3:
                deps = [ours[i - 2]]
            if i >= 4:
                state = (*order[i - 4], ours[i - 4], theirs[i - 4], weights, m, v, out)
            if (l, j) == (0, 0):
                dh, dhT = rowwise(back_kernel, [h1, dy, da], [ROW, COL])
            if i >= 2:
                theirs.append(lax.ppermute(ours[i - 2], "r", pairs))
            if l == 1:
                term, da, *new = bwd(a1, dy, a1T, dyT, full[1][j], da, deps=deps, state=state)
            else:
                term, *new = bwd(a0, dh, a0T, dhT, full[0][j], need=False, deps=deps, state=state)
            if state:
                out = new
            ours.append(lax.psum_scatter(term, "s", scatter_dimension=0, tiled=True)[0])
        last = len(order) - 1
        theirs.append(lax.ppermute(ours[last - 1], "r", pairs))
        for i in range(last - 3, last):
            out = adam(*order[i], ours[i], theirs[i], weights, m, v, out)
        theirs.append(lax.ppermute(ours[last], "r", pairs))
        out = adam(*order[last], ours[last], theirs[last], weights, m, v, out)
        return tuple(out)

    states, cut = P(("rep", "r", "s"), None, None), P(None, "s", None)
    return jax.shard_map(
        step,
        mesh=mesh,
        in_specs=(states, states) + (cut,) * 9,
        out_specs=(P("rep", "s", None),) * 9,
        check_vma=False,
    )
```

time: 1590 us -> 1200 us (0.75)
  matrix products: 1080 us -> 0 us
  Pallas kernels: 0 us -> 893 us
  waiting for transfers between devices: 408 us -> 272 us
  other arithmetic: 53 us -> 0 us
  local copies, waits for them, and re-layouts: 31.1 us -> 5.35 us
    dot_general x15 -> x0, matrix products: 1080 us -> none  [the longest x5 417 us: layer(): gate = jnp.dot(a, w['w_gate'], preferred_element_type=jnp.float32)]
    pallas_call x0 -> x27, Pallas kernels: none -> 893 us  [the longest x8 659 us: bwd(): pl.pallas_call(functools.partial(bwd_kernel, n, need, first, bool(state),...]
    psum x1 -> x0, waiting for transfers between devices: 285 us -> none  [summed(): lax.psum(lax.psum_scatter(term, 's', scatter_dimension=0, tiled=True), 'r')]
    ppermute x0 -> x8, waiting for transfers between devices: none -> 177 us  [the longest x6 130 us: step(): theirs.append(lax.ppermute(ours[i - 2], 'r', pairs))]
    reduce_scatter x6 -> x0, waiting for transfers between devices: 86.7 us -> none  [summed(): lax.psum_scatter(term, 's', scatter_dimension=0, tiled=True)]
    unnamed x13 -> x24, waiting for transfers between devices: 1.74 us -> 49.4 us
    convert_element_type x2 -> x0, other arithmetic: 43.8 us -> none  [adamw(): return ((w - 0.02 * step).astype(jnp.bfloat16), m, v)]
    all_gather x6 -> x8, waiting for transfers between devices: 33.9 us -> 45.7 us  [step(): lax.all_gather(pack(l, j, *weights), 's', axis=0)]
  transfers between devices with their start and end apart: 13 -> 24, of which waited for: 5 -> 12; matrix products, arithmetic and copies ran while one was open for 50% -> 0% of each run, Pallas kernels for 0% -> 74%
where the time goes in v2:
time: 1200 us
  Pallas kernels  893 us (74%)
  waiting for transfers between devices  272 us (23%)
  between operations  14.4 us (1%)
  starting transfers between devices  12.6 us (1%)
    pallas_call x8, Pallas kernels, bwd(): pl.pallas_call(functools.partial(bwd_kernel, n, need, first, bool(state),...  659 us
    pallas_call x4, Pallas kernels, fwd(): pl.pallas_call(functools.partial(fwd_kernel, n, first), grid=(n,), out_sh...  141 us
    ppermute x6, waiting for transfers between devices, step(): theirs.append(lax.ppermute(ours[i - 2], 'r', pairs))  130 us
    unnamed x24, waiting for transfers between devices  49.4 us
    all_gather x8, waiting for transfers between devices, step(): lax.all_gather(pack(l, j, *weights), 's', axis=0)  45.7 us
    pallas_call x3, Pallas kernels, rowwise(): pl.pallas_call(body, grid=(NT,), out_shape=outs, in_specs=[spec(one) for...  36.8 us
    pallas_call x4, Pallas kernels, adam(): pl.pallas_call(functools.partial(adam_kernel, len(before)), grid=(4,), ou...  32.5 us
    ppermute x1, waiting for transfers between devices, step(): theirs.append(lax.ppermute(ours[last - 1], 'r', pairs))  25.6 us
  transfers between devices with their start and end apart: 24, of which 12 were waited for; matrix products, arithmetic and copies ran while one was open for 0% of the time, Pallas kernels for 74%

profile of v2, /device:TPU:0, one launch (start us, length us, event | category | flops | bytes accessed | tf_op | source)
XLA Modules:
  0.0 1196.9 jit_solution(15360492360446178453)
XLA Ops:
  7.2 2.8 pack.8
  10.1 0.0 all-gather.19.cloned.1.call-start
  10.1 2.8 pack.9
  13.0 0.0 all-gather.21.cloned.1.call-start
  13.0 2.8 pack.10
  15.9 0.0 all-gather.23.cloned.1.call-start
  16.0 3.0 pack.11
  19.0 0.0 all-gather.25.cloned.1.call-start
  19.1 3.3 pack.12
  22.4 0.0 all-gather.27.cloned.1.call-start
  22.4 2.9 pack.13
  25.3 0.0 all-gather.29.cloned.1.call-start
  25.4 2.9 pack.14
  28.3 0.0 all-gather.31.cloned.1.call-start
  28.4 2.9 pack.15
  31.3 0.5 reduce-scatter.25.cloned.1.call-start
  31.8 10.6 shard_map.178
  42.4 14.2 %all-gather.17.cloned.1.call-done = bf16[16,3,128,512]{3,2,1,0:T(8,128)(2,1)} async-done(((bf16[4,3,128,512]{3,2,1,0:T(8,128)(2,1)}), bf16[16,3,128,512]{3,2,1,0:T(8,128)(2,1)}) %all-gather.17.cloned.1.call-update) | async-done | bytes 6291472 | tf_op jit(solution)/shard_map/all_gather | solution.py:374
  56.6 34.7 %fwd.4.refs_1_ = f32[4096,512]{1,0:T(8,128)} custom-call(bf16[4096,512]{1,0:T(8,128)(2,1)} %get-tuple-element.92.refs_0_.refs_16_.refs_25_, bf16[4,4,3,128,512]{4,3,2,1,0:T(8,128)(2,1)} %bitcast.51), custom_call_target="tpu_custom_call" | custom-call | flops 25769803776 | bytes 27262976 | tf_op jit(solution)/shard_map/fwd/pallas_call | solution.py:104
  91.3 11.0 all-gather.19.cloned.1.call-done
  102.3 35.4 %fwd.5.refs_1_ = f32[4096,512]{1,0:T(8,128)} custom-call(bf16[4096,512]{1,0:T(8,128)(2,1)} %get-tuple-element.92.refs_0_.refs_16_.refs_25_, f32[4096,512]{1,0:T(8,128)} %fwd.4.refs_1_, bf16[4,4,3,128,512]{4,3,2,1,0:T(8,128)(2,1)} %bitcast.49), custom_call_target="tpu_custom_call" | custom-call | flops 25769803776 | bytes 27262976 | tf_op jit(solution)/shard_map/fwd/pallas_call | solution.py:104
  137.7 10.3 all-gather.21.cloned.1.call-done
  148.0 35.4 %fwd.6.refs_1_ = f32[4096,512]{1,0:T(8,128)} custom-call(bf16[4096,512]{1,0:T(8,128)(2,1)} %get-tuple-element.92.refs_0_.refs_16_.refs_25_, f32[4096,512]{1,0:T(8,128)} %fwd.5.refs_1_, bf16[4,4,3,128,512]{4,3,2,1,0:T(8,128)(2,1)} %bitcast.47), custom_call_target="tpu_custom_call" | custom-call | flops 25769803776 | bytes 27262976 | tf_op jit(solution)/shard_map/fwd/pallas_call | solution.py:104
  183.4 10.2 all-gather.23.cloned.1.call-done
  193.6 35.5 %fwd.7.y = f32[4096,512]{1,0:T(8,128)} custom-call(bf16[4096,512]{1,0:T(8,128)(2,1)} %get-tuple-element.92.refs_0_.refs_16_.refs_25_, f32[4096,512]{1,0:T(8,128)} %fwd.6.refs_1_, bf16[4,4,3,128,512]{4,3,2,1,0:T(8,128)(2,1)} %bitcast.45), custom_call_target="tpu_custom_call" | custom-call | flops 25769803776 | bytes 27262976 | tf_op jit(solution)/shard_map/fwd/pallas_call | solution.py:104
  229.2 11.6 shard_map.179
  240.8 88.9 %bwd.8 = (bf16[4,4,3,128,512]{4,3,2,1,0:T(8,128)(2,1)}, f32[4096,512]{1,0:T(8,128)}) custom-call(bf16[4096,512]{1,0:T(8,128)(2,1)} %get-tuple-element.93.refs_0_.refs_1_, bf16[4096,512]{1,0:T(8,128)(2,1)} %bitcast.22, bf16[512,4096]{1,0:T(8,128)(2,1)} %get-tuple-element.94.refs_2_.refs_3_, bf16[512,4096]{1,0:T(8,128)(2,1)} %get-tuple-element.95.refs_3_.refs_4_, ...), custom_call_target="tpu_custom_call" | custom-call | flops 68719476736 | bytes 33554432 | tf_op jit(solution)/shard_map/bwd/pallas_call | solution.py:265
  329.7 89.9 %bwd.9 = (bf16[4,4,3,128,512]{4,3,2,1,0:T(8,128)(2,1)}, f32[4096,512]{1,0:T(8,128)}) custom-call(bf16[4096,512]{1,0:T(8,128)(2,1)} %get-tuple-element.93.refs_0_.refs_1_, bf16[4096,512]{1,0:T(8,128)(2,1)} %bitcast.23, bf16[512,4096]{1,0:T(8,128)(2,1)} %get-tuple-element.94.refs_2_.refs_3_, bf16[512,4096]{1,0:T(8,128)(2,1)} %get-tuple-element.95.refs_3_.refs_4_, ...), custom_call_target="tpu_custom_call" | custom-call | flops 68719476736 | bytes 33554432 | tf_op jit(solution)/shard_map/bwd/pallas_call | solution.py:265
  419.6 0.5 reduce-scatter.31.cloned.1.call-update
  420.3 90.6 %bwd.10 = (bf16[4,4,3,128,512]{4,3,2,1,0:T(8,128)(2,1)}, f32[4096,512]{1,0:T(8,128)}) custom-call(bf16[4096,512]{1,0:T(8,128)(2,1)} %get-tuple-element.93.refs_0_.refs_1_, bf16[4096,512]{1,0:T(8,128)(2,1)} %bitcast.24, bf16[512,4096]{1,0:T(8,128)(2,1)} %get-tuple-element.94.refs_2_.refs_3_, bf16[512,4096]{1,0:T(8,128)(2,1)} %get-tuple-element.95.refs_3_.refs_4_, ...), custom_call_target="tpu_custom_call" | custom-call | flops 68719476736 | bytes 33554432 | tf_op jit(solution)/shard_map/bwd/pallas_call | solution.py:265
  510.9 0.0 reduce-scatter.27.cloned.1.call-start
  511.0 89.7 %bwd.11 = (bf16[4,4,3,128,512]{4,3,2,1,0:T(8,128)(2,1)}, f32[4096,512]{1,0:T(8,128)}) custom-call(bf16[4,3,128,512]{3,2,1,0:T(8,128)(2,1)} %bitcast.67, bf16[4096,512]{1,0:T(8,128)(2,1)} %get-tuple-element.93.refs_0_.refs_1_, bf16[4096,512]{1,0:T(8,128)(2,1)} %bitcast.25, bf16[512,4096]{1,0:T(8,128)(2,1)} %get-tuple-element.94.refs_2_.refs_3_, ...), custom_call_target="tpu_custom_call" | custom-call | flops 68719476736 | bytes 33554432 | tf_op jit(solution)/shard_map/bwd/pallas_call | solution.py:265
  600.7 0.0 reduce-scatter.35.cloned.1.call-start
  600.8 1.4 collective-permute-start
  602.2 14.6 %shard_map.180 = (bf16[4096,512]{1,0:T(8,128)(2,1)}, bf16[512,4096]{1,0:T(8,128)(2,1)}) custom-call(bf16[4096,512]{1,0:T(8,128)(2,1)} %get-tuple-element.103.h, bf16[4096,512]{1,0:T(8,128)(2,1)} %bitcast.26, f32[4096,512]{1,0:T(8,128)} %get-tuple-element.104.da), custom_call_target="tpu_custom_call" | custom-call | flops 41943040 | bytes 25165824 | tf_op jit(solution)/shard_map/pallas_call | solution.py:289
  616.8 20.7 %collective-permute-done.refs_4_.refs_5_.refs_6_ = bf16[4,3,128,512]{3,2,1,0:T(8,128)(2,1)} collective-permute-done((bf16[4,3,128,512]{3,2,1,0:T(8,128)(2,1)}, bf16[4,3,128,512]{3,2,1,0:T(8,128)(2,1)}, u32[]{:S(2)}, u32[]{:S(2)}) %collective-permute-start) | collective-permute-done | bytes 1572896 | tf_op jit(solution)/shard_map/ppermute | solution.py:391
  637.5 74.7 %bwd.12 = (bf16[4,4,3,128,512]{4,3,2,1,0:T(8,128)(2,1)}, bf16[2,128,8192]{2,1,0:T(8,128)(2,1)}, bf16[2,128,8192]{2,1,0:T(8,128)(2,1)}, bf16[2,2048,512]{2,1,0:T(...) custom-call(bf16[4,3,128,512]{3,2,1,0:T(8,128)(2,1)} %bitcast.62, ...), custom_call_target="tpu_custom_call" | custom-call | flops 51539607552 | bytes 33554432 | tf_op jit(solution)/shard_map/bwd/pallas_call | solution.py:265
  712.2 0.0 reduce-scatter.33.cloned.1.call-start
  712.3 1.3 copy-done.4
  713.6 1.5 collective-permute-start.1
  715.1 34.1 %collective-permute-done.1.refs_13_.refs_14_.refs_15_ = bf16[4,3,128,512]{3,2,1,0:T(8,128)(2,1)} collective-permute-done((bf16[4,3,128,512]{3,2,1,0:T(8,128)(2,1)S(1)}, bf16[4,3,128,512]{3,2,1,0:T(8,128)(2,1)}, u32[]{:S(2)}, u32[]{:S(2)}) %collective-permute-start.1) | collective-permute-done | bytes 1572896 | tf_op jit(solution)/shard_map/ppermute | solution.py:391
  749.2 75.1 %bwd.13 = (bf16[4,4,3,128,512]{4,3,2,1,0:T(8,128)(2,1)}, bf16[2,128,8192]{2,1,0:T(8,128)(2,1)}, bf16[2,128,8192]{2,1,0:T(8,128)(2,1)}, bf16[2,2048,512]{2,1,0:T(...) custom-call(bf16[4,3,128,512]{3,2,1,0:T(8,128)(2,1)} %bitcast.57, ...), custom_call_target="tpu_custom_call", output_to_operand_aliasing={{1}: (1, {}), {2}: (2, {}), {3}: (3, {}), {4}: (4, {}), {5}... | custom-call | flops 51539607552 | bytes 33554432 | tf_op jit(solution)/shard_map/bwd/pallas_call | solution.py:265
  824.5 1.3 copy-done.3
  825.8 1.6 collective-permute-start.2
  827.4 33.2 %collective-permute-done.2.refs_13_.refs_14_.refs_15_ = bf16[4,3,128,512]{3,2,1,0:T(8,128)(2,1)} collective-permute-done((bf16[4,3,128,512]{3,2,1,0:T(8,128)(2,1)S(1)}, bf16[4,3,128,512]{3,2,1,0:T(8,128)(2,1)}, u32[]{:S(2)}, u32[]{:S(2)}) %collective-permute-start.2) | collective-permute-done | bytes 1572896 | tf_op jit(solution)/shard_map/ppermute | solution.py:391
  860.7 75.0 %bwd.14 = (bf16[4,4,3,128,512]{4,3,2,1,0:T(8,128)(2,1)}, bf16[2,128,8192]{2,1,0:T(8,128)(2,1)}, bf16[2,128,8192]{2,1,0:T(8,128)(2,1)}, bf16[2,2048,512]{2,1,0:T(...) custom-call(bf16[4,3,128,512]{3,2,1,0:T(8,128)(2,1)} %bitcast.27, ...), custom_call_target="tpu_custom_call", output_to_operand_aliasing={{1}: (1, {}), {2}: (2, {}), {3}: (3, {}), {4}: (4, {}), {5}... | custom-call | flops 51539607552 | bytes 33554432 | tf_op jit(solution)/shard_map/bwd/pallas_call | solution.py:265
  935.7 0.0 reduce-scatter.39.cloned.1.call-start
  935.8 1.3 copy-done.2
  937.1 1.7 collective-permute-start.3
  938.7 32.4 %collective-permute-done.3.refs_13_.refs_14_.refs_15_ = bf16[4,3,128,512]{3,2,1,0:T(8,128)(2,1)} collective-permute-done((bf16[4,3,128,512]{3,2,1,0:T(8,128)(2,1)S(1)}, bf16[4,3,128,512]{3,2,1,0:T(8,128)(2,1)}, u32[]{:S(2)}, u32[]{:S(2)}) %collective-permute-start.3) | collective-permute-done | bytes 1572896 | tf_op jit(solution)/shard_map/ppermute | solution.py:391
  971.2 75.1 %bwd.15 = (bf16[4,4,3,128,512]{4,3,2,1,0:T(8,128)(2,1)}, bf16[2,128,8192]{2,1,0:T(8,128)(2,1)}, bf16[2,128,8192]{2,1,0:T(8,128)(2,1)}, bf16[2,2048,512]{2,1,0:T(...) custom-call(bf16[4,3,128,512]{3,2,1,0:T(8,128)(2,1)} %bitcast.32, ...), custom_call_target="tpu_custom_call", output_to_operand_aliasing={{1}: (1, {}), {2}: (2, {}), {3}: (3, {}), {4}: (4, {}), {5}... | custom-call | flops 51539607552 | bytes 33554432 | tf_op jit(solution)/shard_map/bwd/pallas_call | solution.py:265
  1046.3 1.4 copy-done
  1047.7 1.7 collective-permute-start.4
  1049.4 0.5 collective-permute-start.5
  1049.9 1.6 collective-permute-start.6
  1051.4 48.6 %reduce-scatter.39.cloned.1.call-done = bf16[1,4,3,128,512]{4,3,2,1,0:T(8,128)(2,1)} async-done(((bf16[4,4,3,128,512]{4,3,2,1,0:T(8,128)(2,1)}), bf16[1,4,3,128,512]{4,3,2,1,0:T(8,128)(2,1)}) %reduce-scatter.39.cloned.1.call-update) | async-done | bytes 1572880
  1100.0 1.5 collective-permute-start.7
  1101.5 8.1 adam.4
  1109.6 9.1 collective-permute-done.5.refs_12_.refs_13_.refs_14_
  1118.7 8.1 adam.5
  1126.9 25.6 %collective-permute-done.6.refs_12_.refs_13_.refs_14_ = bf16[4,3,128,512]{3,2,1,0:T(8,128)(2,1)} collective-permute-done((bf16[4,3,128,512]{3,2,1,0:T(8,128)(2,1)}, bf16[4,3,128,512]{3,2,1,0:T(8,128)(2,1)}, u32[]{:S(2)}, u32[]{:S(2)}) %collective-permute-start.6) | collective-permute-done | bytes 1572896 | tf_op jit(solution)/shard_map/ppermute | solution.py:400
  1152.5 8.1 adam.6
  1160.6 21.4 %collective-permute-done.7.refs_12_.refs_13_.refs_14_ = bf16[4,3,128,512]{3,2,1,0:T(8,128)(2,1)} collective-permute-done((bf16[4,3,128,512]{3,2,1,0:T(8,128)(2,1)}, bf16[4,3,128,512]{3,2,1,0:T(8,128)(2,1)}, u32[]{:S(2)}, u32[]{:S(2)}) %collective-permute-start.7) | collective-permute-done | bytes 1572896 | tf_op jit(solution)/shard_map/ppermute | solution.py:403
  1182.0 8.1 adam.7
  (37 shorter events, 0.5 us)
Async XLA Ops:
  7.2 49.4 %all-gather.17.cloned.1.call-start = ((), (), s32[]{:S(2)}) async-start(), calls=%async_computation.8 | async-start | bytes 7864320 | tf_op jit(solution)/shard_map/all_gather | solution.py:374
  10.1 92.2 %all-gather.19.cloned.1.call-start = ((), (), s32[]{:S(2)}) async-start(), calls=%async_computation.9 | async-start | bytes 7864320 | tf_op jit(solution)/shard_map/all_gather | solution.py:374
  13.0 135.0 %all-gather.21.cloned.1.call-start = ((), (), s32[]{:S(2)}) async-start(), calls=%async_computation.10 | async-start | bytes 7864320 | tf_op jit(solution)/shard_map/all_gather | solution.py:374
  15.9 177.7 %all-gather.23.cloned.1.call-start = ((), (), s32[]{:S(2)}) async-start(), calls=%async_computation.11 | async-start | bytes 7864320 | tf_op jit(solution)/shard_map/all_gather | solution.py:374
  19.0 221.7 %all-gather.25.cloned.1.call-start = ((), (), s32[]{:S(2)}) async-start(), calls=%async_computation.12 | async-start | bytes 7864320 | tf_op jit(solution)/shard_map/all_gather | solution.py:374
  22.4 307.3 %all-gather.27.cloned.1.call-start = ((), (), s32[]{:S(2)}) async-start(), calls=%async_computation.13 | async-start | bytes 7864320 | tf_op jit(solution)/shard_map/all_gather | solution.py:374
  25.3 394.9 %all-gather.29.cloned.1.call-start = ((), (), s32[]{:S(2)}) async-start(), calls=%async_computation.14 | async-start | bytes 7864320 | tf_op jit(solution)/shard_map/all_gather | solution.py:374
  28.3 482.6 %all-gather.31.cloned.1.call-start = ((), (), s32[]{:S(2)}) async-start(), calls=%async_computation.15 | async-start | bytes 7864320 | tf_op jit(solution)/shard_map/all_gather | solution.py:374
  31.3 479.7 %reduce-scatter.25.cloned.1.call-start = ((), (), s32[]{:S(2)}) async-start(), calls=%async_computation.16 | async-start | bytes 7864320
  419.6 181.2 %reduce-scatter.31.cloned.1.call-start = ((), (), s32[]{:S(2)}) async-start(), calls=%async_computation.19 | async-start | bytes 7864320
  420.2 196.6 %reduce-scatter.29.cloned.1.call-start = ((), (), s32[]{:S(2)}) async-start(), calls=%async_computation.18 | async-start | bytes 7864320
  510.9 238.4 %reduce-scatter.27.cloned.1.call-start = ((), (), s32[]{:S(2)}) async-start(), calls=%async_computation.17 | async-start | bytes 7864320
  600.7 259.9 %reduce-scatter.35.cloned.1.call-start = ((), (), s32[]{:S(2)}) async-start(), calls=%async_computation.21 | async-start | bytes 7864320
  600.8 36.7 %collective-permute-start = (bf16[4,3,128,512]{3,2,1,0:T(8,128)(2,1)}, bf16[4,3,128,512]{3,2,1,0:T(8,128)(2,1)}, u32[]{:S(2)}, u32[]{:S(2)}) collective-permute-start(bf16[4,3,128,512]{3,2,1,0:T(8,128)(2,1)} %bitcast.72), channel_id=1, source_target_pairs={{0,4},{4,0},{1,5},{5,1},{2,6},{6,2},{3,7},{7,3}} | collective-permute-start | bytes 4718600 | tf_op jit(solution)/shard_map/ppermute | solution.py:391
  712.2 1.4 copy-start.4
  712.2 259.0 %reduce-scatter.33.cloned.1.call-start = ((), (), s32[]{:S(2)}) async-start(), calls=%async_computation.20 | async-start | bytes 7864320
  713.6 35.6 %collective-permute-start.1 = (bf16[4,3,128,512]{3,2,1,0:T(8,128)(2,1)S(1)}, bf16[4,3,128,512]{3,2,1,0:T(8,128)(2,1)}, u32[]{:S(2)}, u32[]{:S(2)}) collective-permute-start(bf16[4,3,128,512]{3,2,1,0:T(8,128)(2,1)S(1)} %bitcast.71), channel_id=1, source_target_pairs={{0,4},{4,0},{1,5},{5,1},{2,6},{6,2},{3,7},{7,3}} | collective-permute-start | bytes 4718600 | tf_op jit(solution)/shard_map/ppermute | solution.py:391
  824.4 1.4 copy-start.3
  824.4 225.5 %reduce-scatter.37.cloned.1.call-start = ((), (), s32[]{:S(2)}) async-start(), calls=%async_computation.22 | async-start | bytes 7864320
  825.8 34.9 %collective-permute-start.2 = (bf16[4,3,128,512]{3,2,1,0:T(8,128)(2,1)S(1)}, bf16[4,3,128,512]{3,2,1,0:T(8,128)(2,1)}, u32[]{:S(2)}, u32[]{:S(2)}) collective-permute-start(bf16[4,3,128,512]{3,2,1,0:T(8,128)(2,1)S(1)} %bitcast.66), channel_id=1, source_target_pairs={{0,4},{4,0},{1,5},{5,1},{2,6},{6,2},{3,7},{7,3}} | collective-permute-start | bytes 4718600 | tf_op jit(solution)/shard_map/ppermute | solution.py:391
  935.7 1.4 copy-start.2
  935.7 164.3 %reduce-scatter.39.cloned.1.call-start = ((), (), s32[]{:S(2)}) async-start(), calls=%async_computation.23 | async-start | bytes 7864320
  937.1 34.1 %collective-permute-start.3 = (bf16[4,3,128,512]{3,2,1,0:T(8,128)(2,1)S(1)}, bf16[4,3,128,512]{3,2,1,0:T(8,128)(2,1)}, u32[]{:S(2)}, u32[]{:S(2)}) collective-permute-start(bf16[4,3,128,512]{3,2,1,0:T(8,128)(2,1)S(1)} %bitcast.61), channel_id=1, source_target_pairs={{0,4},{4,0},{1,5},{5,1},{2,6},{6,2},{3,7},{7,3}} | collective-permute-start | bytes 4718600 | tf_op jit(solution)/shard_map/ppermute | solution.py:391
  1046.3 1.4 copy-start
  1046.3 3.1 copy-start.1
  1047.7 53.8 %collective-permute-start.4 = (bf16[4,3,128,512]{3,2,1,0:T(8,128)(2,1)S(1)}, bf16[4,3,128,512]{3,2,1,0:T(8,128)(2,1)}, u32[]{:S(2)}, u32[]{:S(2)}) collective-permute-start(bf16[4,3,128,512]{3,2,1,0:T(8,128)(2,1)S(1)} %bitcast.31), channel_id=1, source_target_pairs={{0,4},{4,0},{1,5},{5,1},{2,6},{6,2},{3,7},{7,3}} | collective-permute-start | bytes 4718600 | tf_op jit(solution)/shard_map/ppermute | solution.py:391
  1049.4 69.3 %collective-permute-start.5 = (bf16[4,3,128,512]{3,2,1,0:T(8,128)(2,1)S(1)}, bf16[4,3,128,512]{3,2,1,0:T(8,128)(2,1)}, u32[]{:S(2)}, u32[]{:S(2)}) collective-permute-start(bf16[4,3,128,512]{3,2,1,0:T(8,128)(2,1)S(1)} %bitcast.36), channel_id=1, source_target_pairs={{0,4},{4,0},{1,5},{5,1},{2,6},{6,2},{3,7},{7,3}} | collective-permute-start | bytes 4718600 | tf_op jit(solution)/shard_map/ppermute | solution.py:391
  1049.9 102.6 %collective-permute-start.6 = (bf16[4,3,128,512]{3,2,1,0:T(8,128)(2,1)}, bf16[4,3,128,512]{3,2,1,0:T(8,128)(2,1)}, u32[]{:S(2)}, u32[]{:S(2)}) collective-permute-start(bf16[4,3,128,512]{3,2,1,0:T(8,128)(2,1)} %bitcast.37), channel_id=1, source_target_pairs={{0,4},{4,0},{1,5},{5,1},{2,6},{6,2},{3,7},{7,3}} | collective-permute-start | bytes 4718600 | tf_op jit(solution)/shard_map/ppermute | solution.py:400
  1100.0 82.0 %collective-permute-start.7 = (bf16[4,3,128,512]{3,2,1,0:T(8,128)(2,1)}, bf16[4,3,128,512]{3,2,1,0:T(8,128)(2,1)}, u32[]{:S(2)}, u32[]{:S(2)}) collective-permute-start(bf16[4,3,128,512]{3,2,1,0:T(8,128)(2,1)} %bitcast.41), channel_id=1, source_target_pairs={{0,4},{4,0},{1,5},{5,1},{2,6},{6,2},{3,7},{7,3}} | collective-permute-start | bytes 4718600 | tf_op jit(solution)/shard_map/ppermute | solution.py:403
Sparse Core Ops, SparseCore 0:
  10.2 46.3 all-gather.16
  58.7 43.5 all-gather.18
  104.4 43.5 all-gather.20
  150.0 43.5 all-gather.22
  195.6 43.5 all-gather.24
  240.5 43.5 all-gather.26
  285.7 43.5 all-gather.28
  330.8 43.5 all-gather.30
  419.7 53.1 reduce-scatter.24
  475.8 53.2 reduce-scatter.30
  532.2 53.2 reduce-scatter.28
  600.8 53.5 reduce-scatter.26
  712.3 53.6 reduce-scatter.34
  824.5 53.6 reduce-scatter.32
  935.8 53.5 reduce-scatter.36
  1046.4 53.5 reduce-scatter.38

commit v3 on v2

--- a/solution.py
+++ b/solution.py
@@ -43,75 +43,6 @@
     head(NT - 1, 1)
     tail(NT - 2, 0)
     tail(NT - 1, 1)
-
-
-def fwd_kernel(n, first, *refs):
-    refs = list(refs)
-    a_h = refs.pop(0)
-    y_h = None if first else refs.pop(0)
-    p, out_h, a_v, y_v, g0, u0, g1, u1, act_s, sa, sy, so = refs
-    k = pl.program_id(0)
-    gate_s, up_s = (g0, g1), (u0, u1)
-
-    @pl.when(k == 0)
-    def _():
-        for t in range(NT):
-            copies(a_h, a_v, sa, t).start()
-            if not first:
-                copies(y_h, y_v, sy, t).start()
-
-    def before(t, count):
-        @pl.when(k == 0)
-        def _():
-            for i in range(count):
-                copies(a_h, a_v, sa, t + i).wait()
-                if not first:
-                    copies(y_h, y_v, sy, t + i).wait()
-
-    def head(t, slot):
-        a = tile(a_v, t)[...]
-        gate_s[slot][...] = dot(a, p[:, 0, 0].reshape(D, W))
-        up_s[slot][...] = dot(a, p[:, 0, 1].reshape(D, W))
-
-    def tail(t, slot):
-        for r in range(0, T, ROWS):
-            gate = gate_s[slot][r : r + ROWS]
-            act_s[r : r + ROWS] = (gate * jax.nn.sigmoid(gate) * up_s[slot][r : r + ROWS]).astype(BF16)
-        old = tile(y_v, t)[...]
-        if first:
-            old = jnp.where(k == 0, 0.0, old)
-        tile(y_v, t)[...] = old + dot(act_s[...], p[:, 0, 2].reshape(W, D))
-
-    def after(t, count):
-        @pl.when(k == n - 1)
-        def _():
-            for i in range(count):
-                copies(y_v, out_h, so, t + i).start()
-
-    pipelined(head, tail, before, after)
-    after(NT - 2, 2)
-
-    @pl.when(k == n - 1)
-    def _():
-        for t in range(NT):
-            copies(y_v, out_h, so, t).wait()
-
-
-def fwd(a, p, y=None):
-    n = p.shape[1]
-    first = y is None
-    sem = pltpu.SemaphoreType.DMA((NT,))
-    return pl.pallas_call(
-        functools.partial(fwd_kernel, n, first),
-        grid=(n,),
-        out_shape=jax.ShapeDtypeStruct((TOK, D), F32),
-        in_specs=[ANY] * (1 if first else 2) + [STRIP],
-        out_specs=ANY,
-        scratch_shapes=[pltpu.VMEM((TOK, D), BF16), pltpu.VMEM((TOK, D), F32)] + [pltpu.VMEM((T, W), F32)] * 4 + [pltpu.VMEM((T, W), BF16)] + [sem] * 3,
-        compiler_params=pltpu.CompilerParams(vmem_limit_bytes=60 << 20, dimension_semantics=("arbitrary",)),
-        cost_estimate=pl.CostEstimate(flops=6 * TOK * D * W * n, bytes_accessed=n * 3 * (1 << 19) + (20 << 20), transcendentals=TOK * W * n),
-        name="fwd",
-    )(*((a,) if first else (a, y)), p)
 
 
 def adamw(w, m, v, g):
@@ -233,8 +164,8 @@
                 copies(da_v, out_h, so, t).wait()
 
 
-def bwd(a, dy, aT, dyT, p, da=None, need=True, deps=(), state=None):
-    n = p.shape[1]
+def bwd(a, dy, aT, dyT, p, at, da=None, need=True, deps=(), state=None):
+    n = 4
     first = da is None
     sem = pltpu.SemaphoreType.DMA((NT,))
     args = list(deps)
@@ -260,7 +191,7 @@
         out_specs += outs
     rest = [a, dy, aT, dyT] + ([da] if need and not first else [])
     args += rest + [p]
-    specs += [ANY] * len(rest) + [STRIP]
+    specs += [ANY] * len(rest) + [pl.BlockSpec((4, 1, 3, 128, 512), lambda k: (0, at + k, 0, 0, 0))]
     big = lambda dt: pltpu.VMEM((TOK, D), dt)
     return pl.pallas_call(
         functools.partial(bwd_kernel, n, need, first, bool(state), skip),
@@ -299,50 +230,191 @@
 ROW, COL = jax.ShapeDtypeStruct((TOK, D), BF16), jax.ShapeDtypeStruct((D, TOK), BF16)
 
 
-def start_kernel(x, dy, a, aT, dyT):
-    a[...] = normed(x[...])
-    aT[...] = a[...].T
-    dyT[...] = dy[...].T
-
-
-def middle_kernel(x, y, h, a, aT):
+def middle_kernel(x, y, dy, h, a, aT, dyT):
     h[...] = (x[...].astype(F32) + y[...].astype(BF16).astype(F32)).astype(BF16)
     a[...] = normed(h[...])
     aT[...] = a[...].T
-
-
-def back_kernel(h, dy, da, dh, dhT):
+    dyT[...] = dy[...].T
+
+
+def back_kernel(h, dy, da, a, dh, dhT, aT):
     wide = h[...].astype(F32)
     scale = lax.rsqrt(jnp.mean(wide**2, -1, keepdims=True) + 1e-6)
     by_a = da[...].astype(BF16).astype(F32)
     by_h = by_a * scale - wide * (scale * scale * scale * jnp.mean(by_a * wide, -1, keepdims=True))
     dh[...] = (dy[...].astype(F32) + by_h.astype(BF16).astype(F32)).astype(BF16)
     dhT[...] = dh[...].T
-
-
-CHUNKS = 4
-
-
-def pack_kernel(*refs):
-    gates, ups, down, out = refs[:4], refs[4:8], refs[8], refs[9]
-    for k in range(4):
-        for which, parts in ((0, gates), (1, ups)):
-            for s in range(4):
-                out[k, which, :, 128 * s : 128 * (s + 1)] = parts[s][0, :, 128 * k : 128 * (k + 1)]
-        out[k, 2] = down[0, 128 * k : 128 * (k + 1), :]
-
-
-def pack(l, j, w_gate, w_up, w_down):
-    wide = [pl.BlockSpec((1, 128, 512), functools.partial(lambda s, i: (l, 0, 4 * s + j), s)) for s in range(4)]
+    aT[...] = a[...].T
+
+
+STRIPS = 16
+
+
+def pack_kernel(base, *refs):
+    gates, ups, down = refs[:4], refs[4:8], refs[8]
+    outs = refs[9:]
+    for i, (lo, hi) in enumerate(base):
+        @pl.when((pl.program_id(0) >= lo) & (pl.program_id(0) < hi))
+        def _(out=outs[i]):
+            for k in range(4):
+                for which, parts in ((0, gates), (1, ups)):
+                    for s in range(4):
+                        out[k, which, :, 128 * s : 128 * (s + 1)] = parts[s][0, :, 128 * k : 128 * (k + 1)]
+                out[k, 2] = down[0, 128 * k : 128 * (k + 1), :]
+
+
+def pack(l, base, w_gate, w_up, w_down):
+    wide = [pl.BlockSpec((1, 128, 512), functools.partial(lambda s, j: (l, 0, 4 * s + j), s)) for s in range(4)]
     return pl.pallas_call(
-        pack_kernel,
-        grid=(1,),
-        out_shape=jax.ShapeDtypeStruct((4, 3, 128, 512), BF16),
-        in_specs=wide + wide + [pl.BlockSpec((1, 512, 512), lambda i: (l, j, 0))],
-        out_specs=pl.BlockSpec((4, 3, 128, 512), lambda i: (0, 0, 0, 0)),
-        cost_estimate=pl.CostEstimate(flops=1 << 21, bytes_accessed=3 << 20, transcendentals=0),
+        functools.partial(pack_kernel, base),
+        grid=(4,),
+        out_shape=[jax.ShapeDtypeStruct((4 * (hi - lo), 3, 128, 512), BF16) for lo, hi in base],
+        in_specs=wide + wide + [pl.BlockSpec((1, 512, 512), lambda j: (l, j, 0))],
+        out_specs=[pl.BlockSpec((4, 3, 128, 512), functools.partial(lambda lo, hi, j: (jnp.clip(j - lo, 0, hi - lo - 1), 0, 0, 0), lo, hi)) for lo, hi in base],
+        cost_estimate=pl.CostEstimate(flops=1 << 21, bytes_accessed=12 << 20, transcendentals=0),
         name="pack",
     )(*[w_gate] * 4, *[w_up] * 4, w_down)
+
+
+def gather_kernel(x_h, pk, full_h, a_h, y_h, full, a_v, y_v, g0, u0, g1, u1, act_s, *sems):
+    load, own, x_send, x_recv, y_send, y_recv, own_send, own_recv, on_send, on_recv, put, a_out, y_out = sems
+    gate_s, up_s = (g0, g1), (u0, u1)
+    s, r = lax.axis_index("s"), lax.axis_index("r")
+    by_x, by_core = lax.rem(s + 2, 4), s + 1 - 2 * lax.rem(s, 2)
+    far = lax.rem(by_core + 2, 4)
+
+    def remote(src, block, k, send, recv, where):
+        return pltpu.make_async_remote_copy(
+            src_ref=src, dst_ref=full.at[block, k], send_sem=send.at[k], recv_sem=recv.at[k],
+            device_id=where, device_id_type=pl.DeviceIdType.MESH,
+        )
+
+    def strip(b):
+        odd, first, last = lax.rem(b, 2), (15 - b) // 15, b // 15
+        return odd * (b + 1 + r) + (1 - odd) * (b - 1 - r) + (first - last) * (1 + 2 * r), odd * (1 - last) + first
+
+    def from_x(block, k):
+        return remote(pk.at[k], block, k, x_send, x_recv, {"s": by_x})
+
+    def from_y(block, k):
+        return remote(full.at[block, k], block, k, y_send, y_recv, {"r": 1 - r})
+
+    def from_core(block, k):
+        return remote(pk.at[k], block, k, own_send, own_recv, {"s": by_core})
+
+    def handed_on(block, k):
+        return remote(full.at[block, k], block, k, on_send, on_recv, {"s": by_core})
+
+    def mine(k):
+        return pltpu.make_async_copy(pk.at[k], full.at[s, k], own.at[k])
+
+    def kept(k):
+        return pltpu.make_async_copy(full.at[:, k], full_h.at[:, k], put.at[k])
+
+    for t in range(NT):
+        copies(x_h, a_v, load, t).start()
+    barrier = pltpu.get_barrier_semaphore()
+    for where in ({"s": by_x}, {"s": by_core}, {"r": 1 - r}):
+        pl.semaphore_signal(barrier, inc=1, device_id=where, device_id_type=pl.DeviceIdType.MESH)
+    pl.semaphore_wait(barrier, 3)
+
+    @pl.loop(0, STRIPS // 2)
+    def _(i):
+        from_x(s, 2 * i + r).start()
+
+    @pl.loop(0, STRIPS)
+    def _(b):
+        k, _ = strip(b)
+        from_core(s, k).start()
+        mine(k).start()
+
+    @pl.loop(0, NT)
+    def _(t):
+        copies(x_h, a_v, load, t).wait()
+        tile(a_v, t)[...] = normed(tile(a_v, t)[...])
+        copies(a_v, a_h, a_out, t).start()
+
+    def arrive(b):
+        k, along_x = strip(b)
+
+        @pl.when(along_x == 1)
+        def _():
+            from_x(by_x, k).wait_recv()
+            from_y(by_x, k).start()
+            handed_on(by_x, k).start()
+
+        @pl.when(along_x == 0)
+        def _():
+            from_y(by_x, k).wait_recv()
+            handed_on(by_x, k).start()
+
+    arrive(0)
+
+    @pl.loop(0, STRIPS)
+    def _(b):
+        k, _ = strip(b)
+        mine(k).wait()
+        from_core(by_core, k).wait_recv()
+        handed_on(far, k).wait_recv()
+        kept(k).start()
+
+        def head(t, slot):
+            a = tile(a_v, t)[...]
+            gate_s[slot][...] = dot(a, full[:, k, 0].reshape(D, W))
+            up_s[slot][...] = dot(a, full[:, k, 1].reshape(D, W))
+
+        def tail(t, slot):
+            for q in range(0, T, ROWS):
+                gate = gate_s[slot][q : q + ROWS]
+                act_s[q : q + ROWS] = (gate * jax.nn.sigmoid(gate) * up_s[slot][q : q + ROWS]).astype(BF16)
+            old = jnp.where(b == 0, 0.0, tile(y_v, t)[...])
+            tile(y_v, t)[...] = old + dot(act_s[...], full[:, k, 2].reshape(W, D))
+
+        def before(t, count):
+            if not isinstance(t, int) or t != NT - 1:
+                return
+
+            @pl.when(b < STRIPS - 1)
+            def _():
+                arrive(b + 1)
+
+        pipelined(head, tail, before, lambda t, count: None)
+
+    for t in range(NT):
+        copies(y_v, y_h, y_out, t).start()
+
+    @pl.loop(0, STRIPS // 2)
+    def _(i):
+        from_x(s, 2 * i + r).wait_send()
+        from_y(by_x, 2 * i + r).wait_send()
+
+    @pl.loop(0, STRIPS)
+    def _(k):
+        from_core(s, k).wait_send()
+        handed_on(by_x, k).wait_send()
+        kept(k).wait()
+
+    for t in range(NT):
+        copies(a_v, a_h, a_out, t).wait()
+        copies(y_v, y_h, y_out, t).wait()
+
+
+def gather_fwd(x, pk):
+    sem = lambda n: pltpu.SemaphoreType.DMA((n,))
+    return pl.pallas_call(
+        gather_kernel,
+        out_shape=[jax.ShapeDtypeStruct((4, STRIPS, 3, 128, 512), BF16), ROW, jax.ShapeDtypeStruct((TOK, D), F32)],
+        in_specs=[ANY] * 2,
+        out_specs=[ANY] * 3,
+        scratch_shapes=[pltpu.VMEM((4, STRIPS, 3, 128, 512), BF16), pltpu.VMEM((TOK, D), BF16), pltpu.VMEM((TOK, D), F32)]
+        + [pltpu.VMEM((T, W), F32)] * 4 + [pltpu.VMEM((T, W), BF16)] + [sem(NT)] + [sem(STRIPS)] * 10 + [sem(NT)] * 2,
+        compiler_params=pltpu.CompilerParams(vmem_limit_bytes=60 << 20, collective_id=0, has_side_effects=True),
+        cost_estimate=pl.CostEstimate(flops=6 * TOK * D * W * STRIPS, bytes_accessed=80 << 20, transcendentals=TOK * W * STRIPS),
+        name="gather_fwd",
+    )(x, pk)
+
+
+CHUNKS = 4
 
 
 def adam_kernel(skip, *refs):
@@ -371,12 +443,12 @@
     def step(x, dy, *arrays):
         weights, m, v = (arrays[i : i + 3] for i in (0, 3, 6))
         x, dy = x[0], dy[0]
-        full = [[lax.all_gather(pack(l, j, *weights), "s", axis=0) for j in range(CHUNKS)] for l in range(2)]
-        a0, a0T, dyT = rowwise(start_kernel, [x, dy], [ROW, COL, COL])
-        y = None
-        for j in range(CHUNKS):
-            y = fwd(a0, full[0][j], y)
-        h1, a1, a1T = rowwise(middle_kernel, [x, y], [ROW, ROW, COL])
+        early, *rest = pack(1, ((0, 1), (1, 2), (2, 4)), *weights)
+        parts = [lax.all_gather(early, "s", axis=0)]
+        full0, a0, y = gather_fwd(x, pack(0, ((0, 4),), *weights)[0])
+        parts += [lax.all_gather(one, "s", axis=0) for one in rest]
+        full1 = [(parts[0], 0), (parts[1], 0), (parts[2], 0), (parts[2], 4)]
+        h1, a1, a1T, dyT = rowwise(middle_kernel, [x, y, dy], [ROW, ROW, COL, COL])
         order = [(1, j) for j in range(CHUNKS)] + [(0, j) for j in range(CHUNKS)]
         ours, theirs, out, da = [], [], None, None
         for i, (l, j) in enumerate(order):
@@ -386,13 +458,13 @@
             if i >= 4:
                 state = (*order[i - 4], ours[i - 4], theirs[i - 4], weights, m, v, out)
             if (l, j) == (0, 0):
-                dh, dhT = rowwise(back_kernel, [h1, dy, da], [ROW, COL])
+                dh, dhT, a0T = rowwise(back_kernel, [h1, dy, da, a0], [ROW, COL, COL])
             if i >= 2:
                 theirs.append(lax.ppermute(ours[i - 2], "r", pairs))
             if l == 1:
-                term, da, *new = bwd(a1, dy, a1T, dyT, full[1][j], da, deps=deps, state=state)
+                term, da, *new = bwd(a1, dy, a1T, dyT, *full1[j], da, deps=deps, state=state)
             else:
-                term, *new = bwd(a0, dh, a0T, dhT, full[0][j], need=False, deps=deps, state=state)
+                term, *new = bwd(a0, dh, a0T, dhT, full0, 4 * j, need=False, deps=deps, state=state)
             if state:
                 out = new
             ours.append(lax.psum_scatter(term, "s", scatter_dimension=0, tiled=True)[0])

time: 1200 us -> 1160 us (0.967)
  waiting for transfers between devices: 272 us -> 228 us
    all_gather x8 -> x3, waiting for transfers between devices: 45.7 us -> 0.04 us  [the longest x2 0.04 us: step(): parts += [lax.all_gather(one, 's', axis=0) for one in rest]]
    pallas_call x12 -> x3, Pallas kernels: 165 us -> 178 us  [the longest x1 166 us: gather_fwd(): pl.pallas_call(gather_kernel, out_shape=[jax.ShapeDtypeStruct((4, STRIPS,...]
    pallas_call x3 -> x2, Pallas kernels: 36.8 us -> 30.5 us  [rowwise(): pl.pallas_call(body, grid=(NT,), out_shape=outs, in_specs=[spec(one) for...]
    unnamed x24 -> x19, waiting for transfers between devices: 49.4 us -> 51.7 us
  transfers between devices with their start and end apart: 24 -> 19, of which waited for: 12 -> 8; matrix products, arithmetic and copies ran while one was open for 0% -> 0% of each run, Pallas kernels for 74% -> 77%
where the time goes in v3:
time: 1160 us
  Pallas kernels  900 us (78%)
  waiting for transfers between devices  228 us (20%)
  between operations  14.5 us (1%)
    pallas_call x8, Pallas kernels, bwd(): pl.pallas_call(functools.partial(bwd_kernel, n, need, first, bool(state),...  659 us
    pallas_call x1, Pallas kernels, gather_fwd(): pl.pallas_call(gather_kernel, out_shape=[jax.ShapeDtypeStruct((4, STRIPS,...  166 us
    ppermute x6, waiting for transfers between devices, step(): theirs.append(lax.ppermute(ours[i - 2], 'r', pairs))  130 us
    unnamed x19, waiting for transfers between devices  51.7 us
    pallas_call x4, Pallas kernels, adam(): pl.pallas_call(functools.partial(adam_kernel, len(before)), grid=(4,), ou...  32.5 us
    pallas_call x2, Pallas kernels, rowwise(): pl.pallas_call(body, grid=(NT,), out_shape=outs, in_specs=[spec(one) for...  30.5 us
    ppermute x1, waiting for transfers between devices, step(): theirs.append(lax.ppermute(ours[last - 1], 'r', pairs))  25.6 us
  transfers between devices with their start and end apart: 19, of which 8 were waited for; matrix products, arithmetic and copies ran while one was open for 0% of the time, Pallas kernels for 77%

profile of v3, /device:TPU:0, one launch (start us, length us, event | category | flops | bytes accessed | tf_op | source)
XLA Modules:
  0.0 1156.6 jit_solution(10837090200002992709)
XLA Ops:
  7.2 0.0 all-gather.7.cloned.1.call-start
  7.2 6.1 pack.3
  13.4 0.0 all-gather.7.cloned.1.call-update
  13.4 0.0 all-gather.9.cloned.1.call-start
  13.4 0.7 all-gather.9.cloned.1.call-update
  14.1 0.0 all-gather.11.cloned.1.call-start
  14.2 0.7 all-gather.11.cloned.1.call-update
  14.9 0.0 reduce-scatter.25.cloned.1.call-start
  14.9 6.3 pack.2.pk
  21.2 165.7 %gather_fwd.1 = (bf16[4,16,3,128,512]{4,3,2,1,0:T(8,128)(2,1)}, bf16[4096,512]{1,0:T(8,128)(2,1)}, f32[4096,512]{1,0:T(8,128)}) custom-call(bf16[4096,512]{1,0:T(8,128)(2,1)} %bitcast.38, bf16[16,3,128,512]{3,2,1,0:T(8,128)(2,1)} %pack.2.pk), custom_call_target="tpu_custom_call" | custom-call | flops 103079215104 | bytes 83886080 | tf_op jit(solution)/shard_map/gather_fwd/pallas_call | solution.py:404
  187.0 13.6 %shard_map.178 = (bf16[4096,512]{1,0:T(8,128)(2,1)}, bf16[4096,512]{1,0:T(8,128)(2,1)}, bf16[512,4096]{1,0:T(8,128)(2,1)}, bf16[512,4096]{1,0:T(8,128)(2,1)}) custom-call(bf16[4096,512]{1,0:T(8,128)(2,1)} %bitcast.39, f32[4096,512]{1,0:T(8,128)} %get-tuple-element.97.y, bf16[4096,512]{1,0:T(8,128)(2,1)} %bitcast.14), custom_call_target="tpu_custom_call" | custom-call | flops 41943040 | bytes 25165824 | tf_op jit(solution)/shard_map/pallas_call | solution.py:220
  200.6 89.1 %bwd.8 = (bf16[4,4,3,128,512]{4,3,2,1,0:T(8,128)(2,1)}, f32[4096,512]{1,0:T(8,128)}) custom-call(bf16[4096,512]{1,0:T(8,128)(2,1)} %get-tuple-element.98.refs_0_.refs_1_, bf16[4096,512]{1,0:T(8,128)(2,1)} %bitcast.15, bf16[512,4096]{1,0:T(8,128)(2,1)} %get-tuple-element.99.refs_2_.refs_3_, bf16[512,4096]{1,0:T(8,128)(2,1)} %get-tuple-element.100.refs_3_.refs_4_, ...), custom_call_target="tpu_custom_call" | custom-call | flops 68719476736 | bytes 33554432 | tf_op jit(solution)/shard_map/bwd/pallas_call | solution.py:196
  289.7 0.0 all-gather.9.cloned.1.call-done
  289.7 89.9 %bwd.9 = (bf16[4,4,3,128,512]{4,3,2,1,0:T(8,128)(2,1)}, f32[4096,512]{1,0:T(8,128)}) custom-call(bf16[4096,512]{1,0:T(8,128)(2,1)} %get-tuple-element.98.refs_0_.refs_1_, bf16[4096,512]{1,0:T(8,128)(2,1)} %bitcast.16, bf16[512,4096]{1,0:T(8,128)(2,1)} %get-tuple-element.99.refs_2_.refs_3_, bf16[512,4096]{1,0:T(8,128)(2,1)} %get-tuple-element.100.refs_3_.refs_4_, ...), custom_call_target="tpu_custom_call" | custom-call | flops 68719476736 | bytes 33554432 | tf_op jit(solution)/shard_map/bwd/pallas_call | solution.py:196
  379.6 0.0 reduce-scatter.25.cloned.1.call-update
  379.6 0.0 reduce-scatter.31.cloned.1.call-start
  379.7 0.5 reduce-scatter.31.cloned.1.call-update
  380.2 0.0 reduce-scatter.29.cloned.1.call-start
  380.3 0.0 all-gather.11.cloned.1.call-done
  380.3 90.5 %bwd.10 = (bf16[4,4,3,128,512]{4,3,2,1,0:T(8,128)(2,1)}, f32[4096,512]{1,0:T(8,128)}) custom-call(bf16[4096,512]{1,0:T(8,128)(2,1)} %get-tuple-element.98.refs_0_.refs_1_, bf16[4096,512]{1,0:T(8,128)(2,1)} %bitcast.17, bf16[512,4096]{1,0:T(8,128)(2,1)} %get-tuple-element.99.refs_2_.refs_3_, bf16[512,4096]{1,0:T(8,128)(2,1)} %get-tuple-element.100.refs_3_.refs_4_, ...), custom_call_target="tpu_custom_call" | custom-call | flops 68719476736 | bytes 33554432 | tf_op jit(solution)/shard_map/bwd/pallas_call | solution.py:196
  470.8 0.0 reduce-scatter.29.cloned.1.call-update
  470.9 0.0 reduce-scatter.27.cloned.1.call-start
  470.9 0.0 reduce-scatter.25.cloned.1.call-done
  470.9 89.9 %bwd.11 = (bf16[4,4,3,128,512]{4,3,2,1,0:T(8,128)(2,1)}, f32[4096,512]{1,0:T(8,128)}) custom-call(bf16[4,3,128,512]{3,2,1,0:T(8,128)(2,1)} %bitcast.54, bf16[4096,512]{1,0:T(8,128)(2,1)} %get-tuple-element.98.refs_0_.refs_1_, bf16[4096,512]{1,0:T(8,128)(2,1)} %bitcast.18, bf16[512,4096]{1,0:T(8,128)(2,1)} %get-tuple-element.99.refs_2_.refs_3_, ...), custom_call_target="tpu_custom_call" | custom-call | flops 68719476736 | bytes 33554432 | tf_op jit(solution)/shard_map/bwd/pallas_call | solution.py:196
  560.8 0.0 reduce-scatter.27.cloned.1.call-update
  560.8 0.0 reduce-scatter.35.cloned.1.call-start
  560.9 0.0 reduce-scatter.31.cloned.1.call-done
  560.9 0.4 collective-permute-start
  561.3 17.0 %shard_map.179 = (bf16[4096,512]{1,0:T(8,128)(2,1)}, bf16[512,4096]{1,0:T(8,128)(2,1)}, bf16[512,4096]{1,0:T(8,128)(2,1)}) custom-call(bf16[4096,512]{1,0:T(8,128)(2,1)} %get-tuple-element.112.h, bf16[4096,512]{1,0:T(8,128)(2,1)} %bitcast.19, f32[4096,512]{1,0:T(8,128)} %get-tuple-element.113.da, bf16[4096,512]{1,0:T(8,128)(2,1)} %get-tuple-element.111.a.refs_16_.refs_25_), custom_call_target="tpu_custom_call" | custom-call | flops 41943040 | bytes 25165824 | tf_op jit(solution)/shard_map/pallas_call | solution.py:220
  578.2 19.3 %collective-permute-done.refs_4_.refs_5_.refs_6_ = bf16[4,3,128,512]{3,2,1,0:T(8,128)(2,1)} collective-permute-done((bf16[4,3,128,512]{3,2,1,0:T(8,128)(2,1)}, bf16[4,3,128,512]{3,2,1,0:T(8,128)(2,1)}, u32[]{:S(2)}, u32[]{:S(2)}) %collective-permute-start) | collective-permute-done | bytes 1572896 | tf_op jit(solution)/shard_map/ppermute | solution.py:463
  597.6 74.7 %bwd.12 = (bf16[4,4,3,128,512]{4,3,2,1,0:T(8,128)(2,1)}, bf16[2,128,8192]{2,1,0:T(8,128)(2,1)}, bf16[2,128,8192]{2,1,0:T(8,128)(2,1)}, bf16[2,2048,512]{2,1,0:T(...) custom-call(bf16[4,3,128,512]{3,2,1,0:T(8,128)(2,1)} %bitcast.49, ...), custom_call_target="tpu_custom_call" | custom-call | flops 51539607552 | bytes 33554432 | tf_op jit(solution)/shard_map/bwd/pallas_call | solution.py:196
  672.2 0.0 reduce-scatter.35.cloned.1.call-update
  672.3 0.0 reduce-scatter.33.cloned.1.call-start
  672.3 1.3 copy-done.4
  673.6 0.6 collective-permute-start.1
  674.3 34.9 %collective-permute-done.1.refs_13_.refs_14_.refs_15_ = bf16[4,3,128,512]{3,2,1,0:T(8,128)(2,1)} collective-permute-done((bf16[4,3,128,512]{3,2,1,0:T(8,128)(2,1)S(1)}, bf16[4,3,128,512]{3,2,1,0:T(8,128)(2,1)}, u32[]{:S(2)}, u32[]{:S(2)}) %collective-permute-start.1) | collective-permute-done | bytes 1572896 | tf_op jit(solution)/shard_map/ppermute | solution.py:463
  709.2 74.9 %bwd.13 = (bf16[4,4,3,128,512]{4,3,2,1,0:T(8,128)(2,1)}, bf16[2,128,8192]{2,1,0:T(8,128)(2,1)}, bf16[2,128,8192]{2,1,0:T(8,128)(2,1)}, bf16[2,2048,512]{2,1,0:T(...) custom-call(bf16[4,3,128,512]{3,2,1,0:T(8,128)(2,1)} %bitcast.44, ...), custom_call_target="tpu_custom_call", output_to_operand_aliasing={{1}: (1, {}), {2}: (2, {}), {3}: (3, {}), {4}: (4, {}), {5}... | custom-call | flops 51539607552 | bytes 33554432 | tf_op jit(solution)/shard_map/bwd/pallas_call | solution.py:196
  784.1 0.0 reduce-scatter.33.cloned.1.call-update
  784.2 0.0 reduce-scatter.37.cloned.1.call-start
  784.2 1.3 copy-done.3
  785.5 0.8 collective-permute-start.2
  786.4 34.0 %collective-permute-done.2.refs_13_.refs_14_.refs_15_ = bf16[4,3,128,512]{3,2,1,0:T(8,128)(2,1)} collective-permute-done((bf16[4,3,128,512]{3,2,1,0:T(8,128)(2,1)S(1)}, bf16[4,3,128,512]{3,2,1,0:T(8,128)(2,1)}, u32[]{:S(2)}, u32[]{:S(2)}) %collective-permute-start.2) | collective-permute-done | bytes 1572896 | tf_op jit(solution)/shard_map/ppermute | solution.py:463
  820.3 75.0 %bwd.14 = (bf16[4,4,3,128,512]{4,3,2,1,0:T(8,128)(2,1)}, bf16[2,128,8192]{2,1,0:T(8,128)(2,1)}, bf16[2,128,8192]{2,1,0:T(8,128)(2,1)}, bf16[2,2048,512]{2,1,0:T(...) custom-call(bf16[4,3,128,512]{3,2,1,0:T(8,128)(2,1)} %bitcast.20, ...), custom_call_target="tpu_custom_call", output_to_operand_aliasing={{1}: (1, {}), {2}: (2, {}), {3}: (3, {}), {4}: (4, {}), {5}... | custom-call | flops 51539607552 | bytes 33554432 | tf_op jit(solution)/shard_map/bwd/pallas_call | solution.py:196
  895.4 0.0 reduce-scatter.37.cloned.1.call-update
  895.4 0.0 reduce-scatter.39.cloned.1.call-start
  895.5 1.3 copy-done.2
  896.8 1.1 collective-permute-start.3
  897.9 32.9 %collective-permute-done.3.refs_13_.refs_14_.refs_15_ = bf16[4,3,128,512]{3,2,1,0:T(8,128)(2,1)} collective-permute-done((bf16[4,3,128,512]{3,2,1,0:T(8,128)(2,1)S(1)}, bf16[4,3,128,512]{3,2,1,0:T(8,128)(2,1)}, u32[]{:S(2)}, u32[]{:S(2)}) %collective-permute-start.3) | collective-permute-done | bytes 1572896 | tf_op jit(solution)/shard_map/ppermute | solution.py:463
  930.8 75.1 %bwd.15 = (bf16[4,4,3,128,512]{4,3,2,1,0:T(8,128)(2,1)}, bf16[2,128,8192]{2,1,0:T(8,128)(2,1)}, bf16[2,128,8192]{2,1,0:T(8,128)(2,1)}, bf16[2,2048,512]{2,1,0:T(...) custom-call(bf16[4,3,128,512]{3,2,1,0:T(8,128)(2,1)} %bitcast.25, ...), custom_call_target="tpu_custom_call", output_to_operand_aliasing={{1}: (1, {}), {2}: (2, {}), {3}: (3, {}), {4}: (4, {}), {5}... | custom-call | flops 51539607552 | bytes 33554432 | tf_op jit(solution)/shard_map/bwd/pallas_call | solution.py:196
  1005.9 0.0 reduce-scatter.39.cloned.1.call-update
  1005.9 1.4 copy-done
  1007.3 1.2 collective-permute-start.4
  1008.5 0.8 collective-permute-start.5
  1009.3 1.2 collective-permute-start.6
  1010.6 49.6 %reduce-scatter.39.cloned.1.call-done = bf16[1,4,3,128,512]{4,3,2,1,0:T(8,128)(2,1)} async-done(((bf16[4,4,3,128,512]{4,3,2,1,0:T(8,128)(2,1)}), bf16[1,4,3,128,512]{4,3,2,1,0:T(8,128)(2,1)}) %reduce-scatter.39.cloned.1.call-update) | async-done | bytes 1572880
  1060.2 1.5 collective-permute-start.7
  1061.7 0.0 collective-permute-done.4.refs_12_.refs_13_.refs_14_
  1061.7 8.1 adam.4
  1069.8 8.6 collective-permute-done.5.refs_12_.refs_13_.refs_14_
  1078.4 8.1 adam.5
  1086.5 25.6 %collective-permute-done.6.refs_12_.refs_13_.refs_14_ = bf16[4,3,128,512]{3,2,1,0:T(8,128)(2,1)} collective-permute-done((bf16[4,3,128,512]{3,2,1,0:T(8,128)(2,1)}, bf16[4,3,128,512]{3,2,1,0:T(8,128)(2,1)}, u32[]{:S(2)}, u32[]{:S(2)}) %collective-permute-start.6) | collective-permute-done | bytes 1572896 | tf_op jit(solution)/shard_map/ppermute | solution.py:472
  1112.1 8.1 adam.6
  1120.2 21.2 %collective-permute-done.7.refs_12_.refs_13_.refs_14_ = bf16[4,3,128,512]{3,2,1,0:T(8,128)(2,1)} collective-permute-done((bf16[4,3,128,512]{3,2,1,0:T(8,128)(2,1)}, bf16[4,3,128,512]{3,2,1,0:T(8,128)(2,1)}, u32[]{:S(2)}, u32[]{:S(2)}) %collective-permute-start.7) | collective-permute-done | bytes 1572896 | tf_op jit(solution)/shard_map/ppermute | solution.py:475
  1141.4 8.1 adam.7
  (12 shorter events, 0.0 us)
Async XLA Ops:
  7.2 193.4 %all-gather.7.cloned.1.call-start = ((), (), s32[]{:S(2)}) async-start(), calls=%async_computation.8 | async-start | bytes 7864320 | tf_op jit(solution)/shard_map/all_gather | solution.py:447
  13.4 276.3 %all-gather.9.cloned.1.call-start = ((), (), s32[]{:S(2)}) async-start(), calls=%async_computation.9 | async-start | bytes 7864320 | tf_op jit(solution)/shard_map/all_gather | solution.py:449
  14.1 366.2 %all-gather.11.cloned.1.call-start = ((), (), s32[]{:S(2)}) async-start(), calls=%async_computation.10 | async-start | bytes 15728640 | tf_op jit(solution)/shard_map/all_gather | solution.py:449
  14.9 456.0 %reduce-scatter.25.cloned.1.call-start = ((), (), s32[]{:S(2)}) async-start(), calls=%async_computation.11 | async-start | bytes 7864320
  379.6 181.3 %reduce-scatter.31.cloned.1.call-start = ((), (), s32[]{:S(2)}) async-start(), calls=%async_computation.14 | async-start | bytes 7864320
  380.2 217.3 %reduce-scatter.29.cloned.1.call-start = ((), (), s32[]{:S(2)}) async-start(), calls=%async_computation.13 | async-start | bytes 7864320
  470.9 238.4 %reduce-scatter.27.cloned.1.call-start = ((), (), s32[]{:S(2)}) async-start(), calls=%async_computation.12 | async-start | bytes 7864320
  560.8 259.5 %reduce-scatter.35.cloned.1.call-start = ((), (), s32[]{:S(2)}) async-start(), calls=%async_computation.16 | async-start | bytes 7864320
  560.9 36.7 %collective-permute-start = (bf16[4,3,128,512]{3,2,1,0:T(8,128)(2,1)}, bf16[4,3,128,512]{3,2,1,0:T(8,128)(2,1)}, u32[]{:S(2)}, u32[]{:S(2)}) collective-permute-start(bf16[4,3,128,512]{3,2,1,0:T(8,128)(2,1)} %bitcast.59), channel_id=1, source_target_pairs={{0,4},{4,0},{1,5},{5,1},{2,6},{6,2},{3,7},{7,3}} | collective-permute-start | bytes 4718600 | tf_op jit(solution)/shard_map/ppermute | solution.py:463
  672.2 1.4 copy-start.4
  672.3 258.5 %reduce-scatter.33.cloned.1.call-start = ((), (), s32[]{:S(2)}) async-start(), calls=%async_computation.15 | async-start | bytes 7864320
  673.6 35.6 %collective-permute-start.1 = (bf16[4,3,128,512]{3,2,1,0:T(8,128)(2,1)S(1)}, bf16[4,3,128,512]{3,2,1,0:T(8,128)(2,1)}, u32[]{:S(2)}, u32[]{:S(2)}) collective-permute-start(bf16[4,3,128,512]{3,2,1,0:T(8,128)(2,1)S(1)} %bitcast.58), channel_id=1, source_target_pairs={{0,4},{4,0},{1,5},{5,1},{2,6},{6,2},{3,7},{7,3}} | collective-permute-start | bytes 4718600 | tf_op jit(solution)/shard_map/ppermute | solution.py:463
  784.1 1.4 copy-start.3
  784.2 225.2 %reduce-scatter.37.cloned.1.call-start = ((), (), s32[]{:S(2)}) async-start(), calls=%async_computation.17 | async-start | bytes 7864320
  785.5 34.8 %collective-permute-start.2 = (bf16[4,3,128,512]{3,2,1,0:T(8,128)(2,1)S(1)}, bf16[4,3,128,512]{3,2,1,0:T(8,128)(2,1)}, u32[]{:S(2)}, u32[]{:S(2)}) collective-permute-start(bf16[4,3,128,512]{3,2,1,0:T(8,128)(2,1)S(1)} %bitcast.53), channel_id=1, source_target_pairs={{0,4},{4,0},{1,5},{5,1},{2,6},{6,2},{3,7},{7,3}} | collective-permute-start | bytes 4718600 | tf_op jit(solution)/shard_map/ppermute | solution.py:463
  895.4 1.4 copy-start.2
  895.4 164.8 %reduce-scatter.39.cloned.1.call-start = ((), (), s32[]{:S(2)}) async-start(), calls=%async_computation.18 | async-start | bytes 7864320
  896.8 34.0 %collective-permute-start.3 = (bf16[4,3,128,512]{3,2,1,0:T(8,128)(2,1)S(1)}, bf16[4,3,128,512]{3,2,1,0:T(8,128)(2,1)}, u32[]{:S(2)}, u32[]{:S(2)}) collective-permute-start(bf16[4,3,128,512]{3,2,1,0:T(8,128)(2,1)S(1)} %bitcast.48), channel_id=1, source_target_pairs={{0,4},{4,0},{1,5},{5,1},{2,6},{6,2},{3,7},{7,3}} | collective-permute-start | bytes 4718600 | tf_op jit(solution)/shard_map/ppermute | solution.py:463
  1005.9 1.4 copy-start
  1005.9 2.6 copy-start.1
  1007.3 54.4 %collective-permute-start.4 = (bf16[4,3,128,512]{3,2,1,0:T(8,128)(2,1)S(1)}, bf16[4,3,128,512]{3,2,1,0:T(8,128)(2,1)}, u32[]{:S(2)}, u32[]{:S(2)}) collective-permute-start(bf16[4,3,128,512]{3,2,1,0:T(8,128)(2,1)S(1)} %bitcast.24), channel_id=1, source_target_pairs={{0,4},{4,0},{1,5},{5,1},{2,6},{6,2},{3,7},{7,3}} | collective-permute-start | bytes 4718600 | tf_op jit(solution)/shard_map/ppermute | solution.py:463
  1008.5 69.8 %collective-permute-start.5 = (bf16[4,3,128,512]{3,2,1,0:T(8,128)(2,1)S(1)}, bf16[4,3,128,512]{3,2,1,0:T(8,128)(2,1)}, u32[]{:S(2)}, u32[]{:S(2)}) collective-permute-start(bf16[4,3,128,512]{3,2,1,0:T(8,128)(2,1)S(1)} %bitcast.29), channel_id=1, source_target_pairs={{0,4},{4,0},{1,5},{5,1},{2,6},{6,2},{3,7},{7,3}} | collective-permute-start | bytes 4718600 | tf_op jit(solution)/shard_map/ppermute | solution.py:463
  1009.3 102.8 %collective-permute-start.6 = (bf16[4,3,128,512]{3,2,1,0:T(8,128)(2,1)}, bf16[4,3,128,512]{3,2,1,0:T(8,128)(2,1)}, u32[]{:S(2)}, u32[]{:S(2)}) collective-permute-start(bf16[4,3,128,512]{3,2,1,0:T(8,128)(2,1)} %bitcast.30), channel_id=1, source_target_pairs={{0,4},{4,0},{1,5},{5,1},{2,6},{6,2},{3,7},{7,3}} | collective-permute-start | bytes 4718600 | tf_op jit(solution)/shard_map/ppermute | solution.py:472
  1060.2 81.3 %collective-permute-start.7 = (bf16[4,3,128,512]{3,2,1,0:T(8,128)(2,1)}, bf16[4,3,128,512]{3,2,1,0:T(8,128)(2,1)}, u32[]{:S(2)}, u32[]{:S(2)}) collective-permute-start(bf16[4,3,128,512]{3,2,1,0:T(8,128)(2,1)} %bitcast.34), channel_id=1, source_target_pairs={{0,4},{4,0},{1,5},{5,1},{2,6},{6,2},{3,7},{7,3}} | collective-permute-start | bytes 4718600 | tf_op jit(solution)/shard_map/ppermute | solution.py:475
Sparse Core Ops, SparseCore 0:
  13.5 77.6 all-gather.6
  93.3 67.6 all-gather.8
  163.1 79.2 all-gather.10
  379.8 52.7 reduce-scatter.24
  435.5 53.2 reduce-scatter.30
  491.7 53.3 reduce-scatter.28
  560.9 52.8 reduce-scatter.26
  672.4 53.2 reduce-scatter.34
  784.3 53.5 reduce-scatter.32
  895.5 53.7 reduce-scatter.36
  1006.1 54.0 reduce-scatter.38

commit v4 on v3

--- a/solution.py
+++ b/solution.py
@@ -16,6 +16,10 @@
 
 def dot(a, b):
     return jnp.dot(a, b, preferred_element_type=F32)
+
+
+def dot_t(a, b):
+    return lax.dot_general(a, b, (((0,), (0,)), ((), ())), preferred_element_type=F32)
 
 
 def tile(ref, t):
@@ -56,17 +60,18 @@
     gs, gr, w, m, v = (ins[3 * i : 3 * i + 3] for i in range(5))
     for which in range(3):
         g = (gs[which][...].astype(F32) + gr[which][...].astype(F32)).astype(BF16).astype(F32)
-        for k in range(4 if which < 2 else 1):
-            c = slice(128 * k, 128 * (k + 1)) if which < 2 else slice(0, 512)
+        for k in range(g.shape[0]):
+            c = slice(128 * k, 128 * (k + 1)) if which < 2 else slice(0, D)
             new = adamw(w[which][0, :, c].astype(F32), m[which][0, :, c], v[which][0, :, c], g[k, 0])
             for i in range(3):
                 outs[3 * i + which][0, :, c] = new[i]
 
 
-def adam_specs(l, j):
-    cols = [pl.BlockSpec((4, 1, 128, 128), functools.partial(lambda which, i: (0, which, 0, i), which)) for which in range(2)]
-    cols.append(pl.BlockSpec((1, 1, 128, 512), lambda i: (i, 2, 0, 0)))
-    own = [pl.BlockSpec((1, 128, 512), lambda i: (l, 0, 4 * i + j))] * 2 + [pl.BlockSpec((1, 128, 512), lambda i: (l, 4 * j + i, 0))]
+def adam_specs(l, q, n, at):
+    cols = [pl.BlockSpec((n, 1, 128, 128), functools.partial(lambda which, i: (at // n, which, 0, i), which)) for which in range(2)]
+    cols.append(pl.BlockSpec((1, 1, 32 * n, D), lambda i: (at + i * n // 4, 2, i % (4 // n), 0)))
+    own = [pl.BlockSpec((1, 128, 128 * n), lambda i: (l, 0, i * (16 // n) + q // n))] * 2
+    own.append(pl.BlockSpec((1, 32 * n, D), lambda i: (l, q * 4 // n + i, 0)))
     return cols * 2 + own * 3, own * 3
 
 
@@ -75,21 +80,18 @@
     take = lambda count: [refs.pop(0) for _ in range(count)]
     take(skip)
     ad_in = take(15) if state else []
-    a_h, dy_h, aT_h, dyT_h = take(4)
+    a_h, dy_h = take(2)
     da_h = take(1)[0] if need and not first else None
     p = refs.pop(0)
     g = refs.pop(0)
     out_h = refs.pop(0) if need else None
     ad_out = take(9) if state else []
-    a_v, dy_v, aT, dyT, act_v, dgu_v, wT, wdT = take(8)
+    a_v, dy_v, act_v, dgu_v, wT, wdT = take(6)
     gate_s, up_s, dact_s = take(2), take(2), take(2)
     da_v = refs.pop(0) if need else None
-    sa, sd, st = take(3)
+    sa, sd = take(2)
     sp, so = take(2) if need else (None, None)
     k = pl.program_id(0)
-
-    def turned(which):
-        return pltpu.make_async_copy((aT_h, dyT_h)[which], (aT, dyT)[which], st.at[which])
 
     @pl.when(k == 0)
     def _():
@@ -98,8 +100,6 @@
             copies(dy_h, dy_v, sd, t).start()
             if need and not first:
                 copies(da_h, da_v, sp, t).start()
-        for which in range(2):
-            turned(which).start()
 
     def before(t, count):
         @pl.when(k == 0)
@@ -146,14 +146,9 @@
     pipelined(head, tail, before, after)
     after(NT - 2, 2)
 
-    @pl.when(k == 0)
-    def _():
-        for which in range(2):
-            turned(which).wait()
-
     for which in range(2):
-        g[:, 0, which] = dot(aT[...], dgu_v[:, W * which : W * (which + 1)]).astype(BF16).reshape(4, 128, W)
-    g[:, 0, 2] = dot(dyT[...], act_v[...]).astype(BF16).T.reshape(4, 128, D)
+        g[:, 0, which] = dot_t(a_v[...], dgu_v[:, W * which : W * (which + 1)]).astype(BF16).reshape(4, 128, W)
+    g[:, 0, 2] = dot_t(act_v[...], dy_v[...]).astype(BF16).reshape(4, 128, D)
     if state:
         adam_step(ad_in, ad_out)
 
@@ -164,12 +159,10 @@
                 copies(da_v, out_h, so, t).wait()
 
 
-def bwd(a, dy, aT, dyT, p, at, da=None, need=True, deps=(), state=None):
-    n = 4
+def bwd(a, dy, p, at, n, da=None, need=True, state=None):
     first = da is None
     sem = pltpu.SemaphoreType.DMA((NT,))
-    args = list(deps)
-    specs = [ANY] * len(args)
+    args, specs = [], []
     out_shapes = [jax.ShapeDtypeStruct((4, n, 3, 128, 512), BF16)]
     out_specs = [STRIP]
     if need:
@@ -177,19 +170,19 @@
         out_specs.append(ANY)
     aliases = {}
     if state:
-        l, j, gs, gr, weights, m, v, before = state
+        where, gs, gr, weights, m, v, before = state
         before = list(before or [])
         aliases = {len(args) + i: len(out_shapes) + i for i in range(len(before))}
         args += before
         specs += [ANY] * len(before)
     skip = len(args)
     if state:
-        ins, outs = adam_specs(l, j)
+        ins, outs = adam_specs(*where)
         args += [gs] * 3 + [gr] * 3 + [*weights, *m, *v]
         specs += ins
         out_shapes += [jax.ShapeDtypeStruct(w.shape, dt) for dt in (BF16, F32, F32) for w in weights]
         out_specs += outs
-    rest = [a, dy, aT, dyT] + ([da] if need and not first else [])
+    rest = [a, dy] + ([da] if need and not first else [])
     args += rest + [p]
     specs += [ANY] * len(rest) + [pl.BlockSpec((4, 1, 3, 128, 512), lambda k: (0, at + k, 0, 0, 0))]
     big = lambda dt: pltpu.VMEM((TOK, D), dt)
@@ -199,9 +192,9 @@
         out_shape=out_shapes,
         in_specs=specs,
         out_specs=out_specs,
-        scratch_shapes=[big(BF16)] * 2 + [pltpu.VMEM((D, TOK), BF16)] * 2 + [big(BF16), pltpu.VMEM((TOK, 2 * W), BF16), pltpu.VMEM((2 * W, D), BF16), pltpu.VMEM((D, W), BF16)]
+        scratch_shapes=[big(BF16)] * 2 + [big(BF16), pltpu.VMEM((TOK, 2 * W), BF16), pltpu.VMEM((2 * W, D), BF16), pltpu.VMEM((D, W), BF16)]
         + [pltpu.VMEM((T, W), F32)] * 4 + [pltpu.VMEM((T, W), BF16)] * 2
-        + ([big(F32)] if need else []) + [sem] * 2 + [pltpu.SemaphoreType.DMA((2,))] + ([sem] * 2 if need else []),
+        + ([big(F32)] if need else []) + [sem] * 2 + ([sem] * 2 if need else []),
         input_output_aliases=aliases,
         compiler_params=pltpu.CompilerParams(vmem_limit_bytes=63 << 20, dimension_semantics=("arbitrary",)),
         cost_estimate=pl.CostEstimate(flops=2 * (8 if need else 6) * TOK * D * W * n, bytes_accessed=n * 6 * (1 << 19) + (20 << 20), transcendentals=TOK * W * n),
@@ -216,35 +209,31 @@
 
 
 def rowwise(body, ins, outs):
-    spec = lambda one: pl.BlockSpec((T, D), lambda t: (t, 0)) if one.shape[0] == TOK else pl.BlockSpec((D, T), lambda t: (0, t))
+    spec = pl.BlockSpec((T, D), lambda t: (t, 0))
     return pl.pallas_call(
         body,
         grid=(NT,),
         out_shape=outs,
-        in_specs=[spec(one) for one in ins],
-        out_specs=[spec(one) for one in outs],
+        in_specs=[spec] * len(ins),
+        out_specs=[spec] * len(outs),
         cost_estimate=pl.CostEstimate(flops=20 * TOK * D, bytes_accessed=24 << 20, transcendentals=TOK),
     )(*ins)
 
 
-ROW, COL = jax.ShapeDtypeStruct((TOK, D), BF16), jax.ShapeDtypeStruct((D, TOK), BF16)
-
-
-def middle_kernel(x, y, dy, h, a, aT, dyT):
+ROW = jax.ShapeDtypeStruct((TOK, D), BF16)
+
+
+def middle_kernel(x, y, h, a):
     h[...] = (x[...].astype(F32) + y[...].astype(BF16).astype(F32)).astype(BF16)
     a[...] = normed(h[...])
-    aT[...] = a[...].T
-    dyT[...] = dy[...].T
-
-
-def back_kernel(h, dy, da, a, dh, dhT, aT):
+
+
+def back_kernel(h, dy, da, dh):
     wide = h[...].astype(F32)
     scale = lax.rsqrt(jnp.mean(wide**2, -1, keepdims=True) + 1e-6)
     by_a = da[...].astype(BF16).astype(F32)
     by_h = by_a * scale - wide * (scale * scale * scale * jnp.mean(by_a * wide, -1, keepdims=True))
     dh[...] = (dy[...].astype(F32) + by_h.astype(BF16).astype(F32)).astype(BF16)
-    dhT[...] = dh[...].T
-    aT[...] = a[...].T
 
 
 STRIPS = 16
@@ -414,27 +403,28 @@
     )(x, pk)
 
 
-CHUNKS = 4
-
-
 def adam_kernel(skip, *refs):
-    adam_step(refs[skip : skip + 15], refs[skip + 15 : skip + 24])
-
-
-def adam(l, j, gs, gr, weights, m, v, before):
-    ins, outs = adam_specs(l, j)
-    shapes = [jax.ShapeDtypeStruct(w.shape, dt) for dt in (BF16, F32, F32) for w in weights]
-    before = list(before or [])
+    adam_step(refs[skip : skip + 15], refs[skip + 15 :])
+
+
+def adam(where, gs, gr, weights, m, v, before):
+    ins, outs = adam_specs(*where)
+    n = where[2]
     return pl.pallas_call(
         functools.partial(adam_kernel, len(before)),
         grid=(4,),
-        out_shape=shapes,
+        out_shape=[jax.ShapeDtypeStruct(w.shape, dt) for dt in (BF16, F32, F32) for w in weights],
         in_specs=[ANY] * len(before) + ins,
         out_specs=outs,
         input_output_aliases={i: i for i in range(len(before))},
-        cost_estimate=pl.CostEstimate(flops=10 * 3 * 4 * 128 * 512, bytes_accessed=18 << 20, transcendentals=3 * 4 * 128 * 512),
+        cost_estimate=pl.CostEstimate(flops=10 * 3 * n * 128 * 512, bytes_accessed=(18 << 20) * n // 4, transcendentals=3 * n * 128 * 512),
         name="adam",
     )(*before, *[gs] * 3, *[gr] * 3, *weights, *m, *v)
+
+
+CALLS = ((1, 0, 4), (1, 4, 4), (1, 8, 4), (1, 12, 4), (0, 0, 4), (0, 4, 4), (0, 8, 4), (0, 12, 2), (0, 14, 2))
+SWAPS = {i: i - 2 for i in range(2, 8)}
+RIDES = {4: 0, 5: 1, 6: 2}
 
 
 def solution(mesh):
@@ -443,37 +433,40 @@
     def step(x, dy, *arrays):
         weights, m, v = (arrays[i : i + 3] for i in (0, 3, 6))
         x, dy = x[0], dy[0]
+        ours, theirs, out, da = [], {}, [], None
+
+        def swap(i):
+            theirs[i] = lax.ppermute(ours[i], "r", pairs)
+
+        def state(i):
+            return (*CALLS[i], 0), ours[i], theirs[i], weights, m, v, out
+
         early, *rest = pack(1, ((0, 1), (1, 2), (2, 4)), *weights)
         parts = [lax.all_gather(early, "s", axis=0)]
         full0, a0, y = gather_fwd(x, pack(0, ((0, 4),), *weights)[0])
         parts += [lax.all_gather(one, "s", axis=0) for one in rest]
-        full1 = [(parts[0], 0), (parts[1], 0), (parts[2], 0), (parts[2], 4)]
-        h1, a1, a1T, dyT = rowwise(middle_kernel, [x, y, dy], [ROW, ROW, COL, COL])
-        order = [(1, j) for j in range(CHUNKS)] + [(0, j) for j in range(CHUNKS)]
-        ours, theirs, out, da = [], [], None, None
-        for i, (l, j) in enumerate(order):
-            deps, state = [], None
-            if i >= 3:
-                deps = [ours[i - 2]]
-            if i >= 4:
-                state = (*order[i - 4], ours[i - 4], theirs[i - 4], weights, m, v, out)
-            if (l, j) == (0, 0):
-                dh, dhT, a0T = rowwise(back_kernel, [h1, dy, da, a0], [ROW, COL, COL])
-            if i >= 2:
-                theirs.append(lax.ppermute(ours[i - 2], "r", pairs))
+        h1, a1 = rowwise(middle_kernel, [x, y], [ROW, ROW])
+        for i, (l, q, n) in enumerate(CALLS):
+            if (l, q) == (0, 0):
+                dh = rowwise(back_kernel, [h1, dy, da], [ROW])[0]
+            if i in SWAPS:
+                swap(SWAPS[i])
+            ride = state(RIDES[i]) if i in RIDES else None
             if l == 1:
-                term, da, *new = bwd(a1, dy, a1T, dyT, *full1[j], da, deps=deps, state=state)
+                term, da, *new = bwd(a1, dy, parts[min(i, 2)], 4 if i == 3 else 0, n, da, state=ride)
             else:
-                term, *new = bwd(a0, dh, a0T, dhT, full0, 4 * j, need=False, deps=deps, state=state)
-            if state:
+                term, *new = bwd(a0, dh, full0, q, n, need=False, state=ride)
+            if ride:
                 out = new
             ours.append(lax.psum_scatter(term, "s", scatter_dimension=0, tiled=True)[0])
-        last = len(order) - 1
-        theirs.append(lax.ppermute(ours[last - 1], "r", pairs))
-        for i in range(last - 3, last):
-            out = adam(*order[i], ours[i], theirs[i], weights, m, v, out)
-        theirs.append(lax.ppermute(ours[last], "r", pairs))
-        out = adam(*order[last], ours[last], theirs[last], weights, m, v, out)
+        swap(6)
+        out = adam(*state(3))
+        swap(7)
+        out = adam(*state(4))
+        out = adam(*state(5))
+        swap(8)
+        for i in (6, 7, 8):
+            out = adam(*state(i))
         return tuple(out)
 
     states, cut = P(("rep", "r", "s"), None, None), P(None, "s", None)

time: 1160 us -> 1150 us (level)
    pallas_call x4 -> x6, Pallas kernels: 32.5 us -> 43.4 us  [adam(): pl.pallas_call(functools.partial(adam_kernel, len(before)), grid=(4,), ou...]
    unnamed x19 -> x21, waiting for transfers between devices: 51.7 us -> 46.4 us
    ppermute x8 -> x9, waiting for transfers between devices: 177 us -> 173 us  [swap(): theirs[i] = lax.ppermute(ours[i], 'r', pairs)]
    pallas_call x8 -> x9, Pallas kernels: 659 us -> 657 us  [bwd(): pl.pallas_call(functools.partial(bwd_kernel, n, need, first, bool(state),...]
  transfers between devices with their start and end apart: 19 -> 21, of which waited for: 8 -> 10; matrix products, arithmetic and copies ran while one was open for 0% -> 0% of each run, Pallas kernels for 77% -> 78%
where the time goes in v4:
time: 1150 us
  Pallas kernels  902 us (78%)
  waiting for transfers between devices  219 us (19%)
  between operations  14.7 us (1%)
    pallas_call x9, Pallas kernels, bwd(): pl.pallas_call(functools.partial(bwd_kernel, n, need, first, bool(state),...  657 us
    ppermute x9, waiting for transfers between devices, swap(): theirs[i] = lax.ppermute(ours[i], 'r', pairs)  173 us
    pallas_call x1, Pallas kernels, gather_fwd(): pl.pallas_call(gather_kernel, out_shape=[jax.ShapeDtypeStruct((4, STRIPS,...  166 us
    unnamed x21, waiting for transfers between devices  46.4 us
    pallas_call x6, Pallas kernels, adam(): pl.pallas_call(functools.partial(adam_kernel, len(before)), grid=(4,), ou...  43.4 us
    pallas_call x2, Pallas kernels, rowwise(): pl.pallas_call(body, grid=(NT,), out_shape=outs, in_specs=[spec] * len(in...  23.2 us
  transfers between devices with their start and end apart: 21, of which 10 were waited for; matrix products, arithmetic and copies ran while one was open for 0% of the time, Pallas kernels for 78%

profile of v4, /device:TPU:0, one launch (start us, length us, event | category | flops | bytes accessed | tf_op | source)
XLA Modules:
  0.0 1147.3 jit_solution(11294904596615221945)
XLA Ops:
  7.2 0.0 all-gather.7.cloned.1.call-start
  7.2 6.1 pack.3
  13.4 0.0 all-gather.9.cloned.1.call-start
  13.4 0.7 all-gather.9.cloned.1.call-update
  14.1 0.0 all-gather.11.cloned.1.call-start
  14.2 0.7 all-gather.11.cloned.1.call-update
  14.9 0.0 reduce-scatter.28.cloned.1.call-start
  14.9 6.3 pack.2.pk
  21.2 165.8 %gather_fwd.1 = (bf16[4,16,3,128,512]{4,3,2,1,0:T(8,128)(2,1)}, bf16[4096,512]{1,0:T(8,128)(2,1)}, f32[4096,512]{1,0:T(8,128)}) custom-call(bf16[4096,512]{1,0:T(8,128)(2,1)} %bitcast.39, bf16[16,3,128,512]{3,2,1,0:T(8,128)(2,1)} %pack.2.pk), custom_call_target="tpu_custom_call" | custom-call | flops 103079215104 | bytes 83886080 | tf_op jit(solution)/shard_map/gather_fwd/pallas_call | solution.py:393
  187.0 10.3 shard_map.178
  197.4 90.1 %bwd.9 = (bf16[4,4,3,128,512]{4,3,2,1,0:T(8,128)(2,1)}, f32[4096,512]{1,0:T(8,128)}) custom-call(bf16[4096,512]{1,0:T(8,128)(2,1)} %get-tuple-element.101.refs_0_, bf16[4096,512]{1,0:T(8,128)(2,1)} %bitcast.41, bf16[4,4,3,128,512]{4,3,2,1,0:T(8,128)(2,1)} %bitcast.49), custom_call_target="tpu_custom_call" | custom-call | flops 68719476736 | bytes 33554432 | tf_op jit(solution)/shard_map/bwd/pallas_call | solution.py:189
  287.5 0.0 reduce-scatter.28.cloned.1.call-update
  287.5 0.0 reduce-scatter.30.cloned.1.call-start
  287.6 0.0 all-gather.9.cloned.1.call-done
  287.6 90.7 %bwd.10 = (bf16[4,4,3,128,512]{4,3,2,1,0:T(8,128)(2,1)}, f32[4096,512]{1,0:T(8,128)}) custom-call(bf16[4096,512]{1,0:T(8,128)(2,1)} %get-tuple-element.101.refs_0_, bf16[4096,512]{1,0:T(8,128)(2,1)} %bitcast.42, f32[4096,512]{1,0:T(8,128)} %get-tuple-element.106.refs_2_, bf16[4,4,3,128,512]{4,3,2,1,0:T(8,128)(2,1)} %bitcast.48), custom_call_target="tpu_custom_call" | custom-call | flops 68719476736 | bytes 33554432 | tf_op jit(solution)/shard_map/bwd/pallas_call | solution.py:189
  378.3 0.0 reduce-scatter.30.cloned.1.call-update
  378.4 0.0 reduce-scatter.32.cloned.1.call-start
  378.4 0.0 all-gather.11.cloned.1.call-done
  378.4 90.8 %bwd.11 = (bf16[4,4,3,128,512]{4,3,2,1,0:T(8,128)(2,1)}, f32[4096,512]{1,0:T(8,128)}) custom-call(bf16[4096,512]{1,0:T(8,128)(2,1)} %get-tuple-element.101.refs_0_, bf16[4096,512]{1,0:T(8,128)(2,1)} %bitcast.43, f32[4096,512]{1,0:T(8,128)} %get-tuple-element.108.refs_2_, bf16[4,8,3,128,512]{4,3,2,1,0:T(8,128)(2,1)} %bitcast.46), custom_call_target="tpu_custom_call" | custom-call | flops 68719476736 | bytes 33554432 | tf_op jit(solution)/shard_map/bwd/pallas_call | solution.py:189
  469.2 0.0 reduce-scatter.34.cloned.1.call-start
  469.3 91.0 %bwd.12 = (bf16[4,4,3,128,512]{4,3,2,1,0:T(8,128)(2,1)}, f32[4096,512]{1,0:T(8,128)}) custom-call(bf16[4096,512]{1,0:T(8,128)(2,1)} %get-tuple-element.101.refs_0_, bf16[4096,512]{1,0:T(8,128)(2,1)} %bitcast.44, f32[4096,512]{1,0:T(8,128)} %get-tuple-element.110.refs_2_, bf16[4,8,3,128,512]{4,3,2,1,0:T(8,128)(2,1)} %bitcast.47), custom_call_target="tpu_custom_call" | custom-call | flops 68719476736 | bytes 33554432 | tf_op jit(solution)/shard_map/bwd/pallas_call | solution.py:189
  560.3 0.0 reduce-scatter.36.cloned.1.call-start
  560.3 0.0 reduce-scatter.28.cloned.1.call-done
  560.3 0.0 collective-permute-start
  560.4 12.8 %shard_map.179.refs_16_.refs_25_.refs_1_ = bf16[4096,512]{1,0:T(8,128)(2,1)} custom-call(bf16[4096,512]{1,0:T(8,128)(2,1)} %get-tuple-element.105.h, bf16[4096,512]{1,0:T(8,128)(2,1)} %bitcast.45, f32[4096,512]{1,0:T(8,128)} %get-tuple-element.111.da), custom_call_target="tpu_custom_call" | custom-call | flops 41943040 | bytes 25165824 | tf_op jit(solution)/shard_map/pallas_call | solution.py:213
  573.2 24.2 %collective-permute-done.refs_3_.refs_4_.refs_5_ = bf16[4,3,128,512]{3,2,1,0:T(8,128)(2,1)} collective-permute-done((bf16[4,3,128,512]{3,2,1,0:T(8,128)(2,1)}, bf16[4,3,128,512]{3,2,1,0:T(8,128)(2,1)}, u32[]{:S(2)}, u32[]{:S(2)}) %collective-permute-start) | collective-permute-done | bytes 1572896 | tf_op jit(solution)/shard_map/ppermute | solution.py:439
  597.4 73.6 %bwd.13 = (bf16[4,4,3,128,512]{4,3,2,1,0:T(8,128)(2,1)}, bf16[2,128,8192]{2,1,0:T(8,128)(2,1)}, bf16[2,128,8192]{2,1,0:T(8,128)(2,1)}, bf16[2,2048,512]{2,1,0:T(...) custom-call(bf16[4,3,128,512]{3,2,1,0:T(8,128)(2,1)} %bitcast.59, ...), custom_call_target="tpu_custom_call" | custom-call | flops 51539607552 | bytes 33554432 | tf_op jit(solution)/shard_map/bwd/pallas_call | solution.py:189
  671.0 0.0 reduce-scatter.36.cloned.1.call-update
  671.0 0.0 reduce-scatter.38.cloned.1.call-start
  671.1 0.0 reduce-scatter.30.cloned.1.call-done
  671.1 0.2 collective-permute-start.1
  671.3 36.0 %collective-permute-done.1.refs_12_.refs_13_.refs_14_ = bf16[4,3,128,512]{3,2,1,0:T(8,128)(2,1)} collective-permute-done((bf16[4,3,128,512]{3,2,1,0:T(8,128)(2,1)}, bf16[4,3,128,512]{3,2,1,0:T(8,128)(2,1)}, u32[]{:S(2)}, u32[]{:S(2)}) %collective-permute-start.1) | collective-permute-done | bytes 1572896 | tf_op jit(solution)/shard_map/ppermute | solution.py:439
  707.3 73.9 %bwd.14 = (bf16[4,4,3,128,512]{4,3,2,1,0:T(8,128)(2,1)}, bf16[2,128,8192]{2,1,0:T(8,128)(2,1)}, bf16[2,128,8192]{2,1,0:T(8,128)(2,1)}, bf16[2,2048,512]{2,1,0:T(...) custom-call(bf16[2,128,8192]{2,1,0:T(8,128)(2,1)} %get-tuple-element, ...), custom_call_target="tpu_custom_call", output_to_operand_aliasing={{1}: (0, {}), {2}: (1, {}), {3}: (2, {}), {4}: (3, {}), {5}... | custom-call | flops 51539607552 | bytes 33554432 | tf_op jit(solution)/shard_map/bwd/pallas_call | solution.py:189
  781.2 0.0 reduce-scatter.40.cloned.1.call-start
  781.3 0.0 reduce-scatter.32.cloned.1.call-done
  781.3 1.2 collective-permute-start.2
  782.4 34.5 %collective-permute-done.2.refs_12_.refs_13_.refs_14_ = bf16[4,3,128,512]{3,2,1,0:T(8,128)(2,1)} collective-permute-done((bf16[4,3,128,512]{3,2,1,0:T(8,128)(2,1)}, bf16[4,3,128,512]{3,2,1,0:T(8,128)(2,1)}, u32[]{:S(2)}, u32[]{:S(2)}) %collective-permute-start.2) | collective-permute-done | bytes 1572896 | tf_op jit(solution)/shard_map/ppermute | solution.py:439
  817.0 74.2 %bwd.15 = (bf16[4,4,3,128,512]{4,3,2,1,0:T(8,128)(2,1)}, bf16[2,128,8192]{2,1,0:T(8,128)(2,1)}, bf16[2,128,8192]{2,1,0:T(8,128)(2,1)}, bf16[2,2048,512]{2,1,0:T(...) custom-call(bf16[2,128,8192]{2,1,0:T(8,128)(2,1)} %get-tuple-element, ...), custom_call_target="tpu_custom_call", output_to_operand_aliasing={{1}: (0, {}), {2}: (1, {}), {3}: (2, {}), {4}: (3, {}), {5}... | custom-call | flops 51539607552 | bytes 33554432 | tf_op jit(solution)/shard_map/bwd/pallas_call | solution.py:189
  891.2 0.0 reduce-scatter.42.cloned.1.call-start
  891.2 36.5 %bwd.16 = bf16[4,2,3,128,512]{4,3,2,1,0:T(8,128)(2,1)} custom-call(bf16[4096,512]{1,0:T(8,128)(2,1)} %get-tuple-element.104.refs_15_.refs_24_.refs_0_, bf16[4096,512]{1,0:T(8,128)(2,1)} %shard_map.179.refs_16_.refs_25_.refs_1_, bf16[4,16,3,128,512]{4,3,2,1,0:T(8,128)(2,1)} %get-tuple-element.112.refs_17_.refs_26_.refs_2_), custom_call_target="tpu_custom_call" | custom-call | flops 25769803776 | bytes 27262976 | tf_op jit(solution)/shard_map/bwd/pallas_call | solution.py:189
  927.8 0.0 reduce-scatter.44.cloned.1.call-start
  927.9 36.6 %bwd.17 = bf16[4,2,3,128,512]{4,3,2,1,0:T(8,128)(2,1)} custom-call(bf16[4096,512]{1,0:T(8,128)(2,1)} %get-tuple-element.104.refs_15_.refs_24_.refs_0_, bf16[4096,512]{1,0:T(8,128)(2,1)} %shard_map.179.refs_16_.refs_25_.refs_1_, bf16[4,16,3,128,512]{4,3,2,1,0:T(8,128)(2,1)} %get-tuple-element.112.refs_17_.refs_26_.refs_2_), custom_call_target="tpu_custom_call" | custom-call | flops 25769803776 | bytes 27262976 | tf_op jit(solution)/shard_map/bwd/pallas_call | solution.py:189
  964.5 0.0 reduce-scatter.34.cloned.1.call-done
  964.6 1.7 collective-permute-start.3
  966.2 0.4 collective-permute-start.4
  966.6 1.7 collective-permute-start.5
  968.3 0.4 collective-permute-start.6
  968.6 11.5 %reduce-scatter.42.cloned.1.call-done = bf16[1,2,3,128,512]{4,3,2,1,0:T(8,128)(2,1)} async-done(((bf16[4,2,3,128,512]{4,3,2,1,0:T(8,128)(2,1)}), bf16[1,2,3,128,512]{4,3,2,1,0:T(8,128)(2,1)}) %reduce-scatter.42.cloned.1.call-update) | async-done | bytes 786448
  980.2 1.5 collective-permute-start.7
  981.6 33.3 %reduce-scatter.44.cloned.1.call-done = bf16[1,2,3,128,512]{4,3,2,1,0:T(8,128)(2,1)} async-done(((bf16[4,2,3,128,512]{4,3,2,1,0:T(8,128)(2,1)}), bf16[1,2,3,128,512]{4,3,2,1,0:T(8,128)(2,1)}) %reduce-scatter.44.cloned.1.call-update) | async-done | bytes 786448
  1014.9 1.5 collective-permute-start.8
  1016.3 8.1 adam.6
  1024.5 11.4 collective-permute-done.4.refs_12_.refs_13_.refs_14_
  1035.9 8.1 adam.7
  1044.0 25.5 %collective-permute-done.5.refs_12_.refs_13_.refs_14_ = bf16[4,3,128,512]{3,2,1,0:T(8,128)(2,1)S(1)} collective-permute-done((bf16[4,3,128,512]{3,2,1,0:T(8,128)(2,1)}, bf16[4,3,128,512]{3,2,1,0:T(8,128)(2,1)S(1)}, u32[]{:S(2)}, u32[]{:S(2)}) %collective-permute-start.5) | collective-permute-done | bytes 1572896 | tf_op jit(solution)/shard_map/ppermute | solution.py:439
  1069.5 1.2 copy-done.1
  1070.6 8.4 adam.8
  1079.0 24.1 %collective-permute-done.6.refs_12_.refs_13_.refs_14_ = bf16[4,3,128,512]{3,2,1,0:T(8,128)(2,1)S(1)} collective-permute-done((bf16[4,3,128,512]{3,2,1,0:T(8,128)(2,1)}, bf16[4,3,128,512]{3,2,1,0:T(8,128)(2,1)S(1)}, u32[]{:S(2)}, u32[]{:S(2)}) %collective-permute-start.6) | collective-permute-done | bytes 1572896 | tf_op jit(solution)/shard_map/ppermute | solution.py:439
  1103.2 1.2 copy-done
  1104.3 8.1 adam.9
  1112.5 7.6 collective-permute-done.7.refs_12_.refs_13_.refs_14_
  1120.1 5.3 adam.10
  1125.4 9.4 collective-permute-done.8.refs_12_.refs_13_.refs_14_
  1134.9 5.3 adam.11
  (14 shorter events, 0.1 us)
Async XLA Ops:
  7.2 190.2 %all-gather.7.cloned.1.call-start = ((), (), s32[]{:S(2)}) async-start(), calls=%async_computation.9 | async-start | bytes 7864320 | tf_op jit(solution)/shard_map/all_gather | solution.py:445
  13.4 274.2 %all-gather.9.cloned.1.call-start = ((), (), s32[]{:S(2)}) async-start(), calls=%async_computation.10 | async-start | bytes 7864320 | tf_op jit(solution)/shard_map/all_gather | solution.py:447
  14.1 364.3 %all-gather.11.cloned.1.call-start = ((), (), s32[]{:S(2)}) async-start(), calls=%async_computation.11 | async-start | bytes 15728640 | tf_op jit(solution)/shard_map/all_gather | solution.py:447
  14.9 545.5 %reduce-scatter.28.cloned.1.call-start = ((), (), s32[]{:S(2)}) async-start(), calls=%async_computation.12 | async-start | bytes 7864320
  287.5 383.6 %reduce-scatter.30.cloned.1.call-start = ((), (), s32[]{:S(2)}) async-start(), calls=%async_computation.13 | async-start | bytes 7864320
  378.4 402.9 %reduce-scatter.32.cloned.1.call-start = ((), (), s32[]{:S(2)}) async-start(), calls=%async_computation.14 | async-start | bytes 7864320
  469.2 495.3 %reduce-scatter.34.cloned.1.call-start = ((), (), s32[]{:S(2)}) async-start(), calls=%async_computation.15 | async-start | bytes 7864320
  560.3 406.0 %reduce-scatter.36.cloned.1.call-start = ((), (), s32[]{:S(2)}) async-start(), calls=%async_computation.16 | async-start | bytes 7864320
  560.3 37.0 %collective-permute-start = (bf16[4,3,128,512]{3,2,1,0:T(8,128)(2,1)}, bf16[4,3,128,512]{3,2,1,0:T(8,128)(2,1)}, u32[]{:S(2)}, u32[]{:S(2)}) collective-permute-start(bf16[4,3,128,512]{3,2,1,0:T(8,128)(2,1)} %bitcast.58), channel_id=1, source_target_pairs={{0,4},{4,0},{1,5},{5,1},{2,6},{6,2},{3,7},{7,3}} | collective-permute-start | bytes 4718600 | tf_op jit(solution)/shard_map/ppermute | solution.py:439
  671.0 295.6 %reduce-scatter.38.cloned.1.call-start = ((), (), s32[]{:S(2)}) async-start(), calls=%async_computation.17 | async-start | bytes 7864320
  671.1 36.2 %collective-permute-start.1 = (bf16[4,3,128,512]{3,2,1,0:T(8,128)(2,1)}, bf16[4,3,128,512]{3,2,1,0:T(8,128)(2,1)}, u32[]{:S(2)}, u32[]{:S(2)}) collective-permute-start(bf16[4,3,128,512]{3,2,1,0:T(8,128)(2,1)} %bitcast.54), channel_id=1, source_target_pairs={{0,4},{4,0},{1,5},{5,1},{2,6},{6,2},{3,7},{7,3}} | collective-permute-start | bytes 4718600 | tf_op jit(solution)/shard_map/ppermute | solution.py:439
  781.2 187.0 %reduce-scatter.40.cloned.1.call-start = ((), (), s32[]{:S(2)}) async-start(), calls=%async_computation.18 | async-start | bytes 7864320
  781.3 35.7 %collective-permute-start.2 = (bf16[4,3,128,512]{3,2,1,0:T(8,128)(2,1)}, bf16[4,3,128,512]{3,2,1,0:T(8,128)(2,1)}, u32[]{:S(2)}, u32[]{:S(2)}) collective-permute-start(bf16[4,3,128,512]{3,2,1,0:T(8,128)(2,1)} %bitcast.50), channel_id=1, source_target_pairs={{0,4},{4,0},{1,5},{5,1},{2,6},{6,2},{3,7},{7,3}} | collective-permute-start | bytes 4718600 | tf_op jit(solution)/shard_map/ppermute | solution.py:439
  891.2 89.0 %reduce-scatter.42.cloned.1.call-start = ((), (), s32[]{:S(2)}) async-start(), calls=%async_computation.19 | async-start | bytes 3932160
  927.8 87.1 %reduce-scatter.44.cloned.1.call-start = ((), (), s32[]{:S(2)}) async-start(), calls=%async_computation.20 | async-start | bytes 3932160
  964.6 50.3 %collective-permute-start.3 = (bf16[4,3,128,512]{3,2,1,0:T(8,128)(2,1)}, bf16[4,3,128,512]{3,2,1,0:T(8,128)(2,1)}, u32[]{:S(2)}, u32[]{:S(2)}) collective-permute-start(bf16[4,3,128,512]{3,2,1,0:T(8,128)(2,1)} %bitcast.15), channel_id=1, source_target_pairs={{0,4},{4,0},{1,5},{5,1},{2,6},{6,2},{3,7},{7,3}} | collective-permute-start | bytes 4718600 | tf_op jit(solution)/shard_map/ppermute | solution.py:439
  966.2 69.6 %collective-permute-start.4 = (bf16[4,3,128,512]{3,2,1,0:T(8,128)(2,1)}, bf16[4,3,128,512]{3,2,1,0:T(8,128)(2,1)}, u32[]{:S(2)}, u32[]{:S(2)}) collective-permute-start(bf16[4,3,128,512]{3,2,1,0:T(8,128)(2,1)} %bitcast.19), channel_id=1, source_target_pairs={{0,4},{4,0},{1,5},{5,1},{2,6},{6,2},{3,7},{7,3}} | collective-permute-start | bytes 4718600 | tf_op jit(solution)/shard_map/ppermute | solution.py:439
  966.6 102.9 %collective-permute-start.5 = (bf16[4,3,128,512]{3,2,1,0:T(8,128)(2,1)}, bf16[4,3,128,512]{3,2,1,0:T(8,128)(2,1)S(1)}, u32[]{:S(2)}, u32[]{:S(2)}) collective-permute-start(bf16[4,3,128,512]{3,2,1,0:T(8,128)(2,1)} %bitcast.23), channel_id=1, source_target_pairs={{0,4},{4,0},{1,5},{5,1},{2,6},{6,2},{3,7},{7,3}} | collective-permute-start | bytes 4718600 | tf_op jit(solution)/shard_map/ppermute | solution.py:439
  968.3 134.9 %collective-permute-start.6 = (bf16[4,3,128,512]{3,2,1,0:T(8,128)(2,1)}, bf16[4,3,128,512]{3,2,1,0:T(8,128)(2,1)S(1)}, u32[]{:S(2)}, u32[]{:S(2)}) collective-permute-start(bf16[4,3,128,512]{3,2,1,0:T(8,128)(2,1)} %bitcast.27), channel_id=1, source_target_pairs={{0,4},{4,0},{1,5},{5,1},{2,6},{6,2},{3,7},{7,3}} | collective-permute-start | bytes 4718600 | tf_op jit(solution)/shard_map/ppermute | solution.py:439
  980.2 140.0 %collective-permute-start.7 = (bf16[2,3,128,512]{3,2,1,0:T(8,128)(2,1)}, bf16[2,3,128,512]{3,2,1,0:T(8,128)(2,1)}, u32[]{:S(2)}, u32[]{:S(2)}) collective-permute-start(bf16[2,3,128,512]{3,2,1,0:T(8,128)(2,1)} %bitcast.35), channel_id=1, source_target_pairs={{0,4},{4,0},{1,5},{5,1},{2,6},{6,2},{3,7},{7,3}} | collective-permute-start | bytes 2359304 | tf_op jit(solution)/shard_map/ppermute | solution.py:439
  1014.9 120.0 %collective-permute-start.8 = (bf16[2,3,128,512]{3,2,1,0:T(8,128)(2,1)}, bf16[2,3,128,512]{3,2,1,0:T(8,128)(2,1)}, u32[]{:S(2)}, u32[]{:S(2)}) collective-permute-start(bf16[2,3,128,512]{3,2,1,0:T(8,128)(2,1)} %bitcast.31), channel_id=1, source_target_pairs={{0,4},{4,0},{1,5},{5,1},{2,6},{6,2},{3,7},{7,3}} | collective-permute-start | bytes 2359304 | tf_op jit(solution)/shard_map/ppermute | solution.py:439
  1069.5 1.2 copy-start.1
  1103.2 1.2 copy-start
Sparse Core Ops, SparseCore 0:
  13.5 77.6 all-gather.6
  93.3 67.6 all-gather.8
  163.1 79.2 all-gather.10
  287.6 52.7 reduce-scatter.27
  378.5 52.7 reduce-scatter.29
  469.3 53.0 reduce-scatter.31
  560.4 53.3 reduce-scatter.33
  671.2 52.6 reduce-scatter.35
  781.3 53.4 reduce-scatter.37
  891.3 53.9 reduce-scatter.39
  947.8 32.3 reduce-scatter.41
  982.5 32.3 reduce-scatter.43

commit v5 on v4

--- a/solution.py
+++ b/solution.py
@@ -54,6 +54,20 @@
     v = 0.95 * v + 0.05 * g * g
     step = m * lax.rsqrt(v + 1e-8) + 0.1 * w
     return (w - 0.02 * step).astype(BF16), m, v
+
+
+def normed(h):
+    wide = h.astype(F32)
+    scale = lax.rsqrt(jnp.mean(wide**2, -1, keepdims=True) + 1e-6)
+    return (wide * scale).astype(BF16)
+
+
+def by_input(h, dy, da):
+    wide = h.astype(F32)
+    scale = lax.rsqrt(jnp.mean(wide**2, -1, keepdims=True) + 1e-6)
+    by_a = da.astype(BF16).astype(F32)
+    by_h = by_a * scale - wide * (scale * scale * scale * jnp.mean(by_a * wide, -1, keepdims=True))
+    return (dy.astype(F32) + by_h.astype(BF16).astype(F32)).astype(BF16)
 
 
 def adam_step(ins, outs):
@@ -75,13 +89,14 @@
     return cols * 2 + own * 3, own * 3
 
 
-def bwd_kernel(n, need, first, state, skip, *refs):
+def bwd_kernel(n, need, first, end, state, skip, *refs):
     refs = list(refs)
     take = lambda count: [refs.pop(0) for _ in range(count)]
     take(skip)
     ad_in = take(15) if state else []
     a_h, dy_h = take(2)
     da_h = take(1)[0] if need and not first else None
+    h_h = take(1)[0] if end else None
     p = refs.pop(0)
     g = refs.pop(0)
     out_h = refs.pop(0) if need else None
@@ -89,8 +104,10 @@
     a_v, dy_v, act_v, dgu_v, wT, wdT = take(6)
     gate_s, up_s, dact_s = take(2), take(2), take(2)
     da_v = refs.pop(0) if need else None
+    h_v = refs.pop(0) if end else None
     sa, sd = take(2)
     sp, so = take(2) if need else (None, None)
+    sh = refs.pop(0) if end else None
     k = pl.program_id(0)
 
     @pl.when(k == 0)
@@ -100,6 +117,8 @@
             copies(dy_h, dy_v, sd, t).start()
             if need and not first:
                 copies(da_h, da_v, sp, t).start()
+            if end:
+                copies(h_h, h_v, sh, t).start()
 
     def before(t, count):
         @pl.when(k == 0)
@@ -133,7 +152,7 @@
             tile(da_v, t)[...] = old + dot(tile(dgu_v, t)[...], wT[...])
 
     def after(t, count):
-        if need:
+        if need and not end:
             @pl.when(k == n - 1)
             def _():
                 for i in range(count):
@@ -152,21 +171,32 @@
     if state:
         adam_step(ad_in, ad_out)
 
-    if need:
+    if end:
+        @pl.when(k == n - 1)
+        def _():
+            @pl.loop(0, NT)
+            def _(t):
+                copies(h_h, h_v, sh, t).wait()
+                tile(h_v, t)[...] = by_input(tile(h_v, t)[...], tile(dy_v, t)[...], tile(da_v, t)[...])
+                copies(h_v, out_h, so, t).start()
+
+            for t in range(NT):
+                copies(h_v, out_h, so, t).wait()
+    elif need:
         @pl.when(k == n - 1)
         def _():
             for t in range(NT):
                 copies(da_v, out_h, so, t).wait()
 
 
-def bwd(a, dy, p, at, n, da=None, need=True, state=None):
-    first = da is None
+def bwd(a, dy, p, at, n, da=None, need=True, state=None, h=None):
+    first, end = da is None, h is not None
     sem = pltpu.SemaphoreType.DMA((NT,))
     args, specs = [], []
     out_shapes = [jax.ShapeDtypeStruct((4, n, 3, 128, 512), BF16)]
     out_specs = [STRIP]
     if need:
-        out_shapes.append(jax.ShapeDtypeStruct((TOK, D), F32))
+        out_shapes.append(jax.ShapeDtypeStruct((TOK, D), BF16 if end else F32))
         out_specs.append(ANY)
     aliases = {}
     if state:
@@ -182,19 +212,19 @@
         specs += ins
         out_shapes += [jax.ShapeDtypeStruct(w.shape, dt) for dt in (BF16, F32, F32) for w in weights]
         out_specs += outs
-    rest = [a, dy] + ([da] if need and not first else [])
+    rest = [a, dy] + ([da] if need and not first else []) + ([h] if end else [])
     args += rest + [p]
     specs += [ANY] * len(rest) + [pl.BlockSpec((4, 1, 3, 128, 512), lambda k: (0, at + k, 0, 0, 0))]
     big = lambda dt: pltpu.VMEM((TOK, D), dt)
     return pl.pallas_call(
-        functools.partial(bwd_kernel, n, need, first, bool(state), skip),
+        functools.partial(bwd_kernel, n, need, first, end, bool(state), skip),
         grid=(n,),
         out_shape=out_shapes,
         in_specs=specs,
         out_specs=out_specs,
         scratch_shapes=[big(BF16)] * 2 + [big(BF16), pltpu.VMEM((TOK, 2 * W), BF16), pltpu.VMEM((2 * W, D), BF16), pltpu.VMEM((D, W), BF16)]
         + [pltpu.VMEM((T, W), F32)] * 4 + [pltpu.VMEM((T, W), BF16)] * 2
-        + ([big(F32)] if need else []) + [sem] * 2 + ([sem] * 2 if need else []),
+        + ([big(F32)] if need else []) + ([big(BF16)] if end else []) + [sem] * (2 + 2 * need + end),
         input_output_aliases=aliases,
         compiler_params=pltpu.CompilerParams(vmem_limit_bytes=63 << 20, dimension_semantics=("arbitrary",)),
         cost_estimate=pl.CostEstimate(flops=2 * (8 if need else 6) * TOK * D * W * n, bytes_accessed=n * 6 * (1 << 19) + (20 << 20), transcendentals=TOK * W * n),
@@ -202,38 +232,7 @@
     )(*args)
 
 
-def normed(h):
-    wide = h.astype(F32)
-    scale = lax.rsqrt(jnp.mean(wide**2, -1, keepdims=True) + 1e-6)
-    return (wide * scale).astype(BF16)
-
-
-def rowwise(body, ins, outs):
-    spec = pl.BlockSpec((T, D), lambda t: (t, 0))
-    return pl.pallas_call(
-        body,
-        grid=(NT,),
-        out_shape=outs,
-        in_specs=[spec] * len(ins),
-        out_specs=[spec] * len(outs),
-        cost_estimate=pl.CostEstimate(flops=20 * TOK * D, bytes_accessed=24 << 20, transcendentals=TOK),
-    )(*ins)
-
-
 ROW = jax.ShapeDtypeStruct((TOK, D), BF16)
-
-
-def middle_kernel(x, y, h, a):
-    h[...] = (x[...].astype(F32) + y[...].astype(BF16).astype(F32)).astype(BF16)
-    a[...] = normed(h[...])
-
-
-def back_kernel(h, dy, da, dh):
-    wide = h[...].astype(F32)
-    scale = lax.rsqrt(jnp.mean(wide**2, -1, keepdims=True) + 1e-6)
-    by_a = da[...].astype(BF16).astype(F32)
-    by_h = by_a * scale - wide * (scale * scale * scale * jnp.mean(by_a * wide, -1, keepdims=True))
-    dh[...] = (dy[...].astype(F32) + by_h.astype(BF16).astype(F32)).astype(BF16)
 
 
 STRIPS = 16
@@ -265,8 +264,8 @@
     )(*[w_gate] * 4, *[w_up] * 4, w_down)
 
 
-def gather_kernel(x_h, pk, full_h, a_h, y_h, full, a_v, y_v, g0, u0, g1, u1, act_s, *sems):
-    load, own, x_send, x_recv, y_send, y_recv, own_send, own_recv, on_send, on_recv, put, a_out, y_out = sems
+def gather_kernel(x_h, pk, full_h, a_h, h_h, next_h, full, x_v, a_v, y_v, g0, u0, g1, u1, act_s, *sems):
+    load, own, x_send, x_recv, y_send, y_recv, own_send, own_recv, on_send, on_recv, put, a_out, h_out, next_out = sems
     gate_s, up_s = (g0, g1), (u0, u1)
     s, r = lax.axis_index("s"), lax.axis_index("r")
     by_x, by_core = lax.rem(s + 2, 4), s + 1 - 2 * lax.rem(s, 2)
@@ -301,7 +300,7 @@
         return pltpu.make_async_copy(full.at[:, k], full_h.at[:, k], put.at[k])
 
     for t in range(NT):
-        copies(x_h, a_v, load, t).start()
+        copies(x_h, x_v, load, t).start()
     barrier = pltpu.get_barrier_semaphore()
     for where in ({"s": by_x}, {"s": by_core}, {"r": 1 - r}):
         pl.semaphore_signal(barrier, inc=1, device_id=where, device_id_type=pl.DeviceIdType.MESH)
@@ -319,8 +318,8 @@
 
     @pl.loop(0, NT)
     def _(t):
-        copies(x_h, a_v, load, t).wait()
-        tile(a_v, t)[...] = normed(tile(a_v, t)[...])
+        copies(x_h, x_v, load, t).wait()
+        tile(a_v, t)[...] = normed(tile(x_v, t)[...])
         copies(a_v, a_h, a_out, t).start()
 
     def arrive(b):
@@ -369,8 +368,14 @@
 
         pipelined(head, tail, before, lambda t, count: None)
 
-    for t in range(NT):
-        copies(y_v, y_h, y_out, t).start()
+    @pl.loop(0, NT)
+    def _(t):
+        copies(a_v, a_h, a_out, t).wait()
+        h = (tile(x_v, t)[...].astype(F32) + tile(y_v, t)[...].astype(BF16).astype(F32)).astype(BF16)
+        tile(x_v, t)[...] = h
+        tile(a_v, t)[...] = normed(h)
+        copies(x_v, h_h, h_out, t).start()
+        copies(a_v, next_h, next_out, t).start()
 
     @pl.loop(0, STRIPS // 2)
     def _(i):
@@ -384,19 +389,19 @@
         kept(k).wait()
 
     for t in range(NT):
-        copies(a_v, a_h, a_out, t).wait()
-        copies(y_v, y_h, y_out, t).wait()
+        copies(x_v, h_h, h_out, t).wait()
+        copies(a_v, next_h, next_out, t).wait()
 
 
 def gather_fwd(x, pk):
     sem = lambda n: pltpu.SemaphoreType.DMA((n,))
     return pl.pallas_call(
         gather_kernel,
-        out_shape=[jax.ShapeDtypeStruct((4, STRIPS, 3, 128, 512), BF16), ROW, jax.ShapeDtypeStruct((TOK, D), F32)],
+        out_shape=[jax.ShapeDtypeStruct((4, STRIPS, 3, 128, 512), BF16), ROW, ROW, ROW],
         in_specs=[ANY] * 2,
-        out_specs=[ANY] * 3,
-        scratch_shapes=[pltpu.VMEM((4, STRIPS, 3, 128, 512), BF16), pltpu.VMEM((TOK, D), BF16), pltpu.VMEM((TOK, D), F32)]
-        + [pltpu.VMEM((T, W), F32)] * 4 + [pltpu.VMEM((T, W), BF16)] + [sem(NT)] + [sem(STRIPS)] * 10 + [sem(NT)] * 2,
+        out_specs=[ANY] * 4,
+        scratch_shapes=[pltpu.VMEM((4, STRIPS, 3, 128, 512), BF16), pltpu.VMEM((TOK, D), BF16), pltpu.VMEM((TOK, D), BF16), pltpu.VMEM((TOK, D), F32)]
+        + [pltpu.VMEM((T, W), F32)] * 4 + [pltpu.VMEM((T, W), BF16)] + [sem(NT)] + [sem(STRIPS)] * 10 + [sem(NT)] * 3,
         compiler_params=pltpu.CompilerParams(vmem_limit_bytes=60 << 20, collective_id=0, has_side_effects=True),
         cost_estimate=pl.CostEstimate(flops=6 * TOK * D * W * STRIPS, bytes_accessed=80 << 20, transcendentals=TOK * W * STRIPS),
         name="gather_fwd",
@@ -443,19 +448,16 @@
 
         early, *rest = pack(1, ((0, 1), (1, 2), (2, 4)), *weights)
         parts = [lax.all_gather(early, "s", axis=0)]
-        full0, a0, y = gather_fwd(x, pack(0, ((0, 4),), *weights)[0])
+        full0, a0, h1, a1 = gather_fwd(x, pack(0, ((0, 4),), *weights)[0])
         parts += [lax.all_gather(one, "s", axis=0) for one in rest]
-        h1, a1 = rowwise(middle_kernel, [x, y], [ROW, ROW])
         for i, (l, q, n) in enumerate(CALLS):
-            if (l, q) == (0, 0):
-                dh = rowwise(back_kernel, [h1, dy, da], [ROW])[0]
             if i in SWAPS:
                 swap(SWAPS[i])
             ride = state(RIDES[i]) if i in RIDES else None
             if l == 1:
-                term, da, *new = bwd(a1, dy, parts[min(i, 2)], 4 if i == 3 else 0, n, da, state=ride)
+                term, da, *new = bwd(a1, dy, parts[min(i, 2)], 4 if i == 3 else 0, n, da, state=ride, h=h1 if q == 12 else None)
             else:
-                term, *new = bwd(a0, dh, full0, q, n, need=False, state=ride)
+                term, *new = bwd(a0, da, full0, q, n, need=False, state=ride)
             if ride:
                 out = new
             ours.append(lax.psum_scatter(term, "s", scatter_dimension=0, tiled=True)[0])

time: 1150 us -> 1150 us (level)
  Pallas kernels: 902 us -> 885 us
  waiting for transfers between devices: 219 us -> 231 us
    pallas_call x11 -> x9, Pallas kernels: 681 us -> 663 us  [bwd(): pl.pallas_call(functools.partial(bwd_kernel, n, need, first, end, bool(st...]
  transfers between devices with their start and end apart: 21 -> 21, of which waited for: 10 -> 10; matrix products, arithmetic and copies ran while one was open for 0% -> 0% of each run, Pallas kernels for 78% -> 76%
where the time goes in v5:
time: 1150 us; the launch traced here: 1140 us
  Pallas kernels  885 us (77%)
  waiting for transfers between devices  231 us (20%)
  between operations  14.7 us (1%)
    pallas_call x9, Pallas kernels, bwd(): pl.pallas_call(functools.partial(bwd_kernel, n, need, first, end, bool(st...  663 us
    ppermute x9, waiting for transfers between devices, swap(): theirs[i] = lax.ppermute(ours[i], 'r', pairs)  184 us
    pallas_call x1, Pallas kernels, gather_fwd(): pl.pallas_call(gather_kernel, out_shape=[jax.ShapeDtypeStruct((4, STRIPS,...  166 us
    unnamed x21, waiting for transfers between devices  46.7 us
    pallas_call x6, Pallas kernels, adam(): pl.pallas_call(functools.partial(adam_kernel, len(before)), grid=(4,), ou...  43.4 us
  transfers between devices with their start and end apart: 21, of which 10 were waited for; matrix products, arithmetic and copies ran while one was open for 0% of the time, Pallas kernels for 76%

profile of v5, /device:TPU:0, one launch (start us, length us, event | category | flops | bytes accessed | tf_op | source)
XLA Modules:
  0.0 1141.9 jit_solution(9784052208362120680)
XLA Ops:
  7.2 0.0 all-gather.7.cloned.1.call-start
  7.2 6.1 pack.3
  13.4 0.0 all-gather.9.cloned.1.call-start
  13.4 0.7 all-gather.9.cloned.1.call-update
  14.1 0.0 all-gather.11.cloned.1.call-start
  14.2 0.7 all-gather.11.cloned.1.call-update
  14.9 0.0 reduce-scatter.28.cloned.1.call-start
  14.9 6.3 pack.2.pk
  21.2 165.9 %gather_fwd.1 = (bf16[4,16,3,128,512]{4,3,2,1,0:T(8,128)(2,1)}, bf16[4096,512]{1,0:T(8,128)(2,1)}, bf16[4096,512]{1,0:T(8,128)(2,1)}, bf16[4096,512]{1,0:T(8,128)(2,1)}) custom-call(bf16[4096,512]{1,0:T(8,128)(2,1)} %bitcast.43, bf16[16,3,128,512]{3,2,1,0:T(8,128)(2,1)} %pack.2.pk), custom_call_target="tpu_custom_call" | custom-call | flops 103079215104 | bytes 83886080 | tf_op jit(solution)/shard_map/gather_fwd/pallas_call | solution.py:398
  187.2 0.0 all-gather.7.cloned.1.call-done
  187.2 90.1 %bwd.9 = (bf16[4,4,3,128,512]{4,3,2,1,0:T(8,128)(2,1)}, f32[4096,512]{1,0:T(8,128)}) custom-call(bf16[4096,512]{1,0:T(8,128)(2,1)} %get-tuple-element.99.refs_0_, bf16[4096,512]{1,0:T(8,128)(2,1)} %bitcast.44, bf16[4,4,3,128,512]{4,3,2,1,0:T(8,128)(2,1)} %bitcast.42), custom_call_target="tpu_custom_call" | custom-call | flops 68719476736 | bytes 33554432 | tf_op jit(solution)/shard_map/bwd/pallas_call | solution.py:219
  277.3 0.0 reduce-scatter.28.cloned.1.call-update
  277.3 0.0 reduce-scatter.30.cloned.1.call-start
  277.4 0.0 all-gather.9.cloned.1.call-done
  277.4 90.8 %bwd.10 = (bf16[4,4,3,128,512]{4,3,2,1,0:T(8,128)(2,1)}, f32[4096,512]{1,0:T(8,128)}) custom-call(bf16[4096,512]{1,0:T(8,128)(2,1)} %get-tuple-element.99.refs_0_, bf16[4096,512]{1,0:T(8,128)(2,1)} %bitcast.45, f32[4096,512]{1,0:T(8,128)} %get-tuple-element.103.refs_2_, bf16[4,4,3,128,512]{4,3,2,1,0:T(8,128)(2,1)} %bitcast.41), custom_call_target="tpu_custom_call" | custom-call | flops 68719476736 | bytes 33554432 | tf_op jit(solution)/shard_map/bwd/pallas_call | solution.py:219
  368.2 0.0 reduce-scatter.30.cloned.1.call-update
  368.2 0.0 reduce-scatter.32.cloned.1.call-start
  368.2 0.0 all-gather.11.cloned.1.call-done
  368.3 90.9 %bwd.11 = (bf16[4,4,3,128,512]{4,3,2,1,0:T(8,128)(2,1)}, f32[4096,512]{1,0:T(8,128)}) custom-call(bf16[4096,512]{1,0:T(8,128)(2,1)} %get-tuple-element.99.refs_0_, bf16[4096,512]{1,0:T(8,128)(2,1)} %bitcast.46, f32[4096,512]{1,0:T(8,128)} %get-tuple-element.105.refs_2_, bf16[4,8,3,128,512]{4,3,2,1,0:T(8,128)(2,1)} %bitcast.39), custom_call_target="tpu_custom_call" | custom-call | flops 68719476736 | bytes 33554432 | tf_op jit(solution)/shard_map/bwd/pallas_call | solution.py:219
  459.1 0.0 reduce-scatter.32.cloned.1.call-update
  459.2 0.0 reduce-scatter.34.cloned.1.call-start
  459.2 96.4 %bwd.12 = (bf16[4,4,3,128,512]{4,3,2,1,0:T(8,128)(2,1)}, bf16[4096,512]{1,0:T(8,128)(2,1)}) custom-call(bf16[4096,512]{1,0:T(8,128)(2,1)} %get-tuple-element.99.refs_0_, bf16[4096,512]{1,0:T(8,128)(2,1)} %bitcast.47, f32[4096,512]{1,0:T(8,128)} %get-tuple-element.107.refs_2_, bf16[4096,512]{1,0:T(8,128)(2,1)} %get-tuple-element.108.refs_3_, ...), custom_call_target="tpu_custom_call" | custom-call | flops 68719476736 | bytes 33554432 | tf_op jit(solution)/shard_map/bwd/pallas_call | solution.py:219
  555.7 0.0 reduce-scatter.36.cloned.1.call-start
  555.7 0.0 reduce-scatter.28.cloned.1.call-done
  555.8 0.0 collective-permute-start
  555.8 37.0 %collective-permute-done.refs_3_.refs_4_.refs_5_ = bf16[4,3,128,512]{3,2,1,0:T(8,128)(2,1)} collective-permute-done((bf16[4,3,128,512]{3,2,1,0:T(8,128)(2,1)}, bf16[4,3,128,512]{3,2,1,0:T(8,128)(2,1)}, u32[]{:S(2)}, u32[]{:S(2)}) %collective-permute-start) | collective-permute-done | bytes 1572896 | tf_op jit(solution)/shard_map/ppermute | solution.py:444
  592.8 73.8 %bwd.13 = (bf16[4,4,3,128,512]{4,3,2,1,0:T(8,128)(2,1)}, bf16[2,128,8192]{2,1,0:T(8,128)(2,1)}, bf16[2,128,8192]{2,1,0:T(8,128)(2,1)}, bf16[2,2048,512]{2,1,0:T(...) custom-call(bf16[4,3,128,512]{3,2,1,0:T(8,128)(2,1)} %bitcast.57, ...), custom_call_target="tpu_custom_call" | custom-call | flops 51539607552 | bytes 33554432 | tf_op jit(solution)/shard_map/bwd/pallas_call | solution.py:219
  666.6 0.0 reduce-scatter.38.cloned.1.call-start
  666.7 0.0 reduce-scatter.30.cloned.1.call-done
  666.7 0.7 collective-permute-start.1
  667.4 35.5 %collective-permute-done.1.refs_12_.refs_13_.refs_14_ = bf16[4,3,128,512]{3,2,1,0:T(8,128)(2,1)} collective-permute-done((bf16[4,3,128,512]{3,2,1,0:T(8,128)(2,1)}, bf16[4,3,128,512]{3,2,1,0:T(8,128)(2,1)}, u32[]{:S(2)}, u32[]{:S(2)}) %collective-permute-start.1) | collective-permute-done | bytes 1572896 | tf_op jit(solution)/shard_map/ppermute | solution.py:444
  702.9 73.9 %bwd.14 = (bf16[4,4,3,128,512]{4,3,2,1,0:T(8,128)(2,1)}, bf16[2,128,8192]{2,1,0:T(8,128)(2,1)}, bf16[2,128,8192]{2,1,0:T(8,128)(2,1)}, bf16[2,2048,512]{2,1,0:T(...) custom-call(bf16[2,128,8192]{2,1,0:T(8,128)(2,1)} %get-tuple-element, ...), custom_call_target="tpu_custom_call", output_to_operand_aliasing={{1}: (0, {}), {2}: (1, {}), {3}: (2, {}), {4}: (3, {}), {5}... | custom-call | flops 51539607552 | bytes 33554432 | tf_op jit(solution)/shard_map/bwd/pallas_call | solution.py:219
  776.8 0.0 reduce-scatter.38.cloned.1.call-update
  776.8 0.0 reduce-scatter.40.cloned.1.call-start
  776.9 0.0 reduce-scatter.32.cloned.1.call-done
  776.9 1.2 collective-permute-start.2
  778.1 34.2 %collective-permute-done.2.refs_12_.refs_13_.refs_14_ = bf16[4,3,128,512]{3,2,1,0:T(8,128)(2,1)} collective-permute-done((bf16[4,3,128,512]{3,2,1,0:T(8,128)(2,1)}, bf16[4,3,128,512]{3,2,1,0:T(8,128)(2,1)}, u32[]{:S(2)}, u32[]{:S(2)}) %collective-permute-start.2) | collective-permute-done | bytes 1572896 | tf_op jit(solution)/shard_map/ppermute | solution.py:444
  812.2 74.2 %bwd.15 = (bf16[4,4,3,128,512]{4,3,2,1,0:T(8,128)(2,1)}, bf16[2,128,8192]{2,1,0:T(8,128)(2,1)}, bf16[2,128,8192]{2,1,0:T(8,128)(2,1)}, bf16[2,2048,512]{2,1,0:T(...) custom-call(bf16[2,128,8192]{2,1,0:T(8,128)(2,1)} %get-tuple-element, ...), custom_call_target="tpu_custom_call", output_to_operand_aliasing={{1}: (0, {}), {2}: (1, {}), {3}: (2, {}), {4}: (3, {}), {5}... | custom-call | flops 51539607552 | bytes 33554432 | tf_op jit(solution)/shard_map/bwd/pallas_call | solution.py:219
  886.5 0.0 reduce-scatter.42.cloned.1.call-start
  886.5 36.5 %bwd.16 = bf16[4,2,3,128,512]{4,3,2,1,0:T(8,128)(2,1)} custom-call(bf16[4096,512]{1,0:T(8,128)(2,1)} %get-tuple-element.102.refs_15_.refs_24_.refs_0_, bf16[4096,512]{1,0:T(8,128)(2,1)} %get-tuple-element.109.refs_16_.refs_25_.refs_1_, bf16[4,16,3,128,512]{4,3,2,1,0:T(8,128)(2,1)} %get-tuple-element.110.refs_17_.refs_26_.refs_2_), custom_call_target="tpu_custom_call" | custom-call | flops 25769803776 | bytes 27262976 | tf_op jit(solution)/shard_map/bwd/pallas_call | solution.py:219
  923.0 0.0 reduce-scatter.44.cloned.1.call-start
  923.1 36.7 %bwd.17 = bf16[4,2,3,128,512]{4,3,2,1,0:T(8,128)(2,1)} custom-call(bf16[4096,512]{1,0:T(8,128)(2,1)} %get-tuple-element.102.refs_15_.refs_24_.refs_0_, bf16[4096,512]{1,0:T(8,128)(2,1)} %get-tuple-element.109.refs_16_.refs_25_.refs_1_, bf16[4,16,3,128,512]{4,3,2,1,0:T(8,128)(2,1)} %get-tuple-element.110.refs_17_.refs_26_.refs_2_), custom_call_target="tpu_custom_call" | custom-call | flops 25769803776 | bytes 27262976 | tf_op jit(solution)/shard_map/bwd/pallas_call | solution.py:219
  959.8 0.0 reduce-scatter.34.cloned.1.call-done
  959.8 1.6 collective-permute-start.3
  961.5 0.4 collective-permute-start.4
  961.9 1.6 collective-permute-start.5
  963.5 0.4 collective-permute-start.6
  963.9 11.9 %reduce-scatter.42.cloned.1.call-done = bf16[1,2,3,128,512]{4,3,2,1,0:T(8,128)(2,1)} async-done(((bf16[4,2,3,128,512]{4,3,2,1,0:T(8,128)(2,1)}), bf16[1,2,3,128,512]{4,3,2,1,0:T(8,128)(2,1)}) %reduce-scatter.42.cloned.1.call-update) | async-done | bytes 786448
  975.8 1.5 collective-permute-start.7
  977.2 33.2 %reduce-scatter.44.cloned.1.call-done = bf16[1,2,3,128,512]{4,3,2,1,0:T(8,128)(2,1)} async-done(((bf16[4,2,3,128,512]{4,3,2,1,0:T(8,128)(2,1)}), bf16[1,2,3,128,512]{4,3,2,1,0:T(8,128)(2,1)}) %reduce-scatter.44.cloned.1.call-update) | async-done | bytes 786448
  1010.5 1.5 collective-permute-start.8
  1011.9 8.1 adam.6
  1020.1 11.0 collective-permute-done.4.refs_12_.refs_13_.refs_14_
  1031.1 8.1 adam.7
  1039.3 25.5 %collective-permute-done.5.refs_12_.refs_13_.refs_14_ = bf16[4,3,128,512]{3,2,1,0:T(8,128)(2,1)S(1)} collective-permute-done((bf16[4,3,128,512]{3,2,1,0:T(8,128)(2,1)}, bf16[4,3,128,512]{3,2,1,0:T(8,128)(2,1)S(1)}, u32[]{:S(2)}, u32[]{:S(2)}) %collective-permute-start.5) | collective-permute-done | bytes 1572896 | tf_op jit(solution)/shard_map/ppermute | solution.py:444
  1064.7 1.2 copy-done.1
  1065.9 8.4 adam.8
  1074.3 24.1 %collective-permute-done.6.refs_12_.refs_13_.refs_14_ = bf16[4,3,128,512]{3,2,1,0:T(8,128)(2,1)S(1)} collective-permute-done((bf16[4,3,128,512]{3,2,1,0:T(8,128)(2,1)}, bf16[4,3,128,512]{3,2,1,0:T(8,128)(2,1)S(1)}, u32[]{:S(2)}, u32[]{:S(2)}) %collective-permute-start.6) | collective-permute-done | bytes 1572896 | tf_op jit(solution)/shard_map/ppermute | solution.py:444
  1098.4 1.2 copy-done
  1099.6 8.1 adam.9
  1107.8 7.6 collective-permute-done.7.refs_12_.refs_13_.refs_14_
  1115.4 5.3 adam.10
  1120.7 8.8 collective-permute-done.8.refs_12_.refs_13_.refs_14_
  1129.5 5.3 adam.11
  (12 shorter events, 0.1 us)
Async XLA Ops:
  7.2 180.0 %all-gather.7.cloned.1.call-start = ((), (), s32[]{:S(2)}) async-start(), calls=%async_computation.9 | async-start | bytes 7864320 | tf_op jit(solution)/shard_map/all_gather | solution.py:450
  13.4 264.0 %all-gather.9.cloned.1.call-start = ((), (), s32[]{:S(2)}) async-start(), calls=%async_computation.10 | async-start | bytes 7864320 | tf_op jit(solution)/shard_map/all_gather | solution.py:452
  14.1 354.1 %all-gather.11.cloned.1.call-start = ((), (), s32[]{:S(2)}) async-start(), calls=%async_computation.11 | async-start | bytes 15728640 | tf_op jit(solution)/shard_map/all_gather | solution.py:452
  14.9 540.9 %reduce-scatter.28.cloned.1.call-start = ((), (), s32[]{:S(2)}) async-start(), calls=%async_computation.12 | async-start | bytes 7864320
  277.3 389.4 %reduce-scatter.30.cloned.1.call-start = ((), (), s32[]{:S(2)}) async-start(), calls=%async_computation.13 | async-start | bytes 7864320
  368.2 408.7 %reduce-scatter.32.cloned.1.call-start = ((), (), s32[]{:S(2)}) async-start(), calls=%async_computation.14 | async-start | bytes 7864320
  459.2 500.6 %reduce-scatter.34.cloned.1.call-start = ((), (), s32[]{:S(2)}) async-start(), calls=%async_computation.15 | async-start | bytes 7864320
  555.7 405.8 %reduce-scatter.36.cloned.1.call-start = ((), (), s32[]{:S(2)}) async-start(), calls=%async_computation.16 | async-start | bytes 7864320
  555.8 37.0 %collective-permute-start = (bf16[4,3,128,512]{3,2,1,0:T(8,128)(2,1)}, bf16[4,3,128,512]{3,2,1,0:T(8,128)(2,1)}, u32[]{:S(2)}, u32[]{:S(2)}) collective-permute-start(bf16[4,3,128,512]{3,2,1,0:T(8,128)(2,1)} %bitcast.56), channel_id=1, source_target_pairs={{0,4},{4,0},{1,5},{5,1},{2,6},{6,2},{3,7},{7,3}} | collective-permute-start | bytes 4718600 | tf_op jit(solution)/shard_map/ppermute | solution.py:444
  666.6 295.2 %reduce-scatter.38.cloned.1.call-start = ((), (), s32[]{:S(2)}) async-start(), calls=%async_computation.17 | async-start | bytes 7864320
  666.7 36.2 %collective-permute-start.1 = (bf16[4,3,128,512]{3,2,1,0:T(8,128)(2,1)}, bf16[4,3,128,512]{3,2,1,0:T(8,128)(2,1)}, u32[]{:S(2)}, u32[]{:S(2)}) collective-permute-start(bf16[4,3,128,512]{3,2,1,0:T(8,128)(2,1)} %bitcast.52), channel_id=1, source_target_pairs={{0,4},{4,0},{1,5},{5,1},{2,6},{6,2},{3,7},{7,3}} | collective-permute-start | bytes 4718600 | tf_op jit(solution)/shard_map/ppermute | solution.py:444
  776.8 186.7 %reduce-scatter.40.cloned.1.call-start = ((), (), s32[]{:S(2)}) async-start(), calls=%async_computation.18 | async-start | bytes 7864320
  776.9 35.3 %collective-permute-start.2 = (bf16[4,3,128,512]{3,2,1,0:T(8,128)(2,1)}, bf16[4,3,128,512]{3,2,1,0:T(8,128)(2,1)}, u32[]{:S(2)}, u32[]{:S(2)}) collective-permute-start(bf16[4,3,128,512]{3,2,1,0:T(8,128)(2,1)} %bitcast.48), channel_id=1, source_target_pairs={{0,4},{4,0},{1,5},{5,1},{2,6},{6,2},{3,7},{7,3}} | collective-permute-start | bytes 4718600 | tf_op jit(solution)/shard_map/ppermute | solution.py:444
  886.5 89.3 %reduce-scatter.42.cloned.1.call-start = ((), (), s32[]{:S(2)}) async-start(), calls=%async_computation.19 | async-start | bytes 3932160
  923.0 87.4 %reduce-scatter.44.cloned.1.call-start = ((), (), s32[]{:S(2)}) async-start(), calls=%async_computation.20 | async-start | bytes 3932160
  959.8 50.6 %collective-permute-start.3 = (bf16[4,3,128,512]{3,2,1,0:T(8,128)(2,1)}, bf16[4,3,128,512]{3,2,1,0:T(8,128)(2,1)}, u32[]{:S(2)}, u32[]{:S(2)}) collective-permute-start(bf16[4,3,128,512]{3,2,1,0:T(8,128)(2,1)} %bitcast.15), channel_id=1, source_target_pairs={{0,4},{4,0},{1,5},{5,1},{2,6},{6,2},{3,7},{7,3}} | collective-permute-start | bytes 4718600 | tf_op jit(solution)/shard_map/ppermute | solution.py:444
  961.5 69.7 %collective-permute-start.4 = (bf16[4,3,128,512]{3,2,1,0:T(8,128)(2,1)}, bf16[4,3,128,512]{3,2,1,0:T(8,128)(2,1)}, u32[]{:S(2)}, u32[]{:S(2)}) collective-permute-start(bf16[4,3,128,512]{3,2,1,0:T(8,128)(2,1)} %bitcast.19), channel_id=1, source_target_pairs={{0,4},{4,0},{1,5},{5,1},{2,6},{6,2},{3,7},{7,3}} | collective-permute-start | bytes 4718600 | tf_op jit(solution)/shard_map/ppermute | solution.py:444
  961.9 102.9 %collective-permute-start.5 = (bf16[4,3,128,512]{3,2,1,0:T(8,128)(2,1)}, bf16[4,3,128,512]{3,2,1,0:T(8,128)(2,1)S(1)}, u32[]{:S(2)}, u32[]{:S(2)}) collective-permute-start(bf16[4,3,128,512]{3,2,1,0:T(8,128)(2,1)} %bitcast.23), channel_id=1, source_target_pairs={{0,4},{4,0},{1,5},{5,1},{2,6},{6,2},{3,7},{7,3}} | collective-permute-start | bytes 4718600 | tf_op jit(solution)/shard_map/ppermute | solution.py:444
  963.5 135.0 %collective-permute-start.6 = (bf16[4,3,128,512]{3,2,1,0:T(8,128)(2,1)}, bf16[4,3,128,512]{3,2,1,0:T(8,128)(2,1)S(1)}, u32[]{:S(2)}, u32[]{:S(2)}) collective-permute-start(bf16[4,3,128,512]{3,2,1,0:T(8,128)(2,1)} %bitcast.27), channel_id=1, source_target_pairs={{0,4},{4,0},{1,5},{5,1},{2,6},{6,2},{3,7},{7,3}} | collective-permute-start | bytes 4718600 | tf_op jit(solution)/shard_map/ppermute | solution.py:444
  975.8 139.6 %collective-permute-start.7 = (bf16[2,3,128,512]{3,2,1,0:T(8,128)(2,1)}, bf16[2,3,128,512]{3,2,1,0:T(8,128)(2,1)}, u32[]{:S(2)}, u32[]{:S(2)}) collective-permute-start(bf16[2,3,128,512]{3,2,1,0:T(8,128)(2,1)} %bitcast.35), channel_id=1, source_target_pairs={{0,4},{4,0},{1,5},{5,1},{2,6},{6,2},{3,7},{7,3}} | collective-permute-start | bytes 2359304 | tf_op jit(solution)/shard_map/ppermute | solution.py:444
  1010.5 119.0 %collective-permute-start.8 = (bf16[2,3,128,512]{3,2,1,0:T(8,128)(2,1)}, bf16[2,3,128,512]{3,2,1,0:T(8,128)(2,1)}, u32[]{:S(2)}, u32[]{:S(2)}) collective-permute-start(bf16[2,3,128,512]{3,2,1,0:T(8,128)(2,1)} %bitcast.31), channel_id=1, source_target_pairs={{0,4},{4,0},{1,5},{5,1},{2,6},{6,2},{3,7},{7,3}} | collective-permute-start | bytes 2359304 | tf_op jit(solution)/shard_map/ppermute | solution.py:444
  1064.7 1.2 copy-start.1
  1098.4 1.2 copy-start
Sparse Core Ops, SparseCore 0:
  13.5 77.6 all-gather.6
  93.3 67.6 all-gather.8
  163.1 79.2 all-gather.10
  277.4 52.8 reduce-scatter.27
  368.3 52.9 reduce-scatter.29
  459.3 53.0 reduce-scatter.31
  555.8 53.4 reduce-scatter.33
  666.7 52.4 reduce-scatter.35
  776.9 53.2 reduce-scatter.37
  886.6 54.2 reduce-scatter.39
  943.4 32.3 reduce-scatter.41
  978.1 32.3 reduce-scatter.43
